TPU v7x, 256 devices: a whole 4x4x8 slice. The times are simulated.
256 devices in a mesh: seq: 32 (over y, z_hi, core), head: 8 (over x, z_lo).
Axes of the slice: x: 4, y: 4, z: 8 (z_hi: 4, z_lo: 2; z = z_hi * 2 + z_lo), core: 2. Of those that a mesh axis runs over, the one named last changes fastest.
Arguments:
- queries: bfloat16 [16384, 4096], P('seq', 'head'), may hold values from -20 to 20
- key_rows: bfloat16 [16384, 2048], P('seq', 'head'), may hold values from -20 to 20
- values: bfloat16 [16384, 2048], P('seq', 'head'), may hold values from -24 to 24
- out_weight: bfloat16 [4096, 5376], P('head'), may hold values from -0.09375 to 0.09375
Outputs:
- projected: bfloat16 [16384, 5376], P(('seq', 'head'))
All inputs are finite; a program needn't handle non-finite values.
Results may differ from a plain program's by a relative error of at most 0.019.
Values may be sent and summed in bfloat16 or wider, within the bound.
No kernel may reach another device: no remote copies, remote signals or barrier semaphores. Data moves between devices by JAX's collectives and lax.ppermute only.
A program may use at most 128 MiB of HBM per device.

v0:
```python
import jax
import jax.numpy as jnp
from jax import lax
from jax.experimental import pallas as pl
from jax.experimental.pallas import tpu as pltpu
from jax.sharding import Mesh
from jax.sharding import PartitionSpec as P

HD = 128
PAIR = 2 * HD
LOG2E = 1.4426950408889634
query_scale = 168.0 ** (-0.5) * LOG2E
neg_fill = -1e30
TILE = 256
PLACES = (
    [(4 * dy, 0) for dy in (0, 1, 3)]
    + [(8, 0), (8, 1)]
    + [(4 * dy + dz, 0) for dz in (1, 3) for dy in (0, 1, 3, 2)]
    + [(4 * dy + 2, 0) for dy in (0, 1, 3)]
    + [(10, 0), (10, 1)]
)


def moved(value, axes, mapping):
    names = axes if isinstance(axes, tuple) else (axes,)
    sizes = [lax.axis_size(name) for name in names]
    pairs = []
    total = 1
    for size in sizes:
        total *= size
    for source in range(total):
        coords, rest = [], source
        for size in reversed(sizes):
            coords.append(rest % size)
            rest //= size
        target = 0
        for size, at in zip(sizes, mapping(tuple(reversed(coords)))):
            target = target * size + at % size
        pairs.append((source, target))
    return lax.ppermute(value, axes, pairs)


def attend_kernel(lo, hi, diag, slots, q_ref, *refs):
    pieces, (out_ref, lse_ref, kv_ref, m_ref, l_ref, acc_ref, sems) = refs[:-7], refs[-7:]
    tasks, _, rows = q_ref.shape
    half = rows // 2
    span = kv_ref.shape[1] // 2

    copies = [
        pltpu.make_async_copy(
            piece, kv_ref.at[slot, pl.ds(part * span, piece.shape[0]), :], sems.at[i]
        )
        for i, (piece, (slot, part)) in enumerate(zip(pieces, PLACES))
    ]
    for copy in copies:
        copy.start()
    for copy in copies:
        copy.wait()

    def step(task, at_span, masked):
        slot = slots[at_span]
        keys = kv_ref[slot, pl.ds(0, span), :]
        keys_twice = jnp.concatenate([keys, keys], axis=1)
        values_t = jnp.concatenate(
            [kv_ref[slot, pl.ds(span + i * HD, HD), :] for i in range(span // HD)], axis=1
        )
        tiles = [pl.ds(r * TILE, TILE) for r in range(rows // TILE)]
        all_scores = [
            jnp.dot(keys_twice, q_ref[task, :, cols], preferred_element_type=jnp.float32)
            for cols in tiles
        ]
        for r, (cols, scores) in enumerate(zip(tiles, all_scores)):
            if masked:
                key_pos = lax.broadcasted_iota(jnp.int32, (span, TILE), 0)
                row_pos = lax.broadcasted_iota(jnp.int32, (span, TILE), 1) + (r * TILE) % half
                scores = jnp.where(key_pos <= row_pos + task * half, scores, neg_fill)
            old_max = m_ref[:, cols]
            new_max = jnp.maximum(old_max, jnp.max(scores, axis=0, keepdims=True))
            weights = jnp.exp2(scores - new_max)
            factor = jnp.exp2(old_max - new_max)
            l_ref[:, cols] = l_ref[:, cols] * factor + jnp.sum(weights, axis=0, keepdims=True)
            m_ref[:, cols] = new_max
            acc_ref[:, cols] = acc_ref[:, cols] * factor + jnp.dot(
                values_t, weights.astype(jnp.bfloat16), preferred_element_type=jnp.float32
            )

    def one_task(t, _):
        m_ref[...] = jnp.full_like(m_ref, neg_fill)
        l_ref[...] = jnp.zeros_like(l_ref)
        acc_ref[...] = jnp.zeros_like(acc_ref)

        def body(at_span, _):
            step(t, at_span, False)
            return 0

        lax.fori_loop(lo[t], hi[t], body, 0)

        @pl.when(diag[t] > 0)
        def _():
            step(t, hi[t], True)

        total = l_ref[...]
        some = total > 0.0
        safe = jnp.where(some, total, 1.0)
        lse_ref[t] = jnp.where(some, m_ref[...] + jnp.log2(safe), neg_fill)
        out = acc_ref[...] / safe
        for h in range(2):
            out_ref[t, :, h * HD : (h + 1) * HD] = out[:, h * half : (h + 1) * half].T.astype(
                out_ref.dtype
            )
        return 0

    lax.fori_loop(0, tasks, one_task, 0)


def attend(lo, hi, diag, slots, q, pieces):
    tasks, _, rows = q.shape
    smem = pl.BlockSpec(memory_space=pltpu.SMEM)
    vmem = pl.BlockSpec(memory_space=pltpu.VMEM)
    hbm = pl.BlockSpec(memory_space=pltpu.MemorySpace.HBM)
    return pl.pallas_call(
        attend_kernel,
        out_shape=(
            jax.ShapeDtypeStruct((tasks, rows // 2, PAIR), jnp.bfloat16),
            jax.ShapeDtypeStruct((tasks, 1, rows), jnp.float32),
        ),
        in_specs=[smem] * 4 + [vmem] + [hbm] * len(pieces),
        out_specs=(vmem, vmem),
        scratch_shapes=[
            pltpu.VMEM((16,) + pieces[0].shape, jnp.bfloat16),
            pltpu.VMEM((1, rows), jnp.float32),
            pltpu.VMEM((1, rows), jnp.float32),
            pltpu.VMEM((HD, rows), jnp.float32),
            pltpu.SemaphoreType.DMA((len(pieces),)),
        ],
        compiler_params=pltpu.CompilerParams(vmem_limit_bytes=48 * 2**20),
        cost_estimate=pl.CostEstimate(
            flops=16384 * 1024 * HD * 4, bytes_accessed=9_000_000, transcendentals=0
        ),
    )(lo, hi, diag, slots, q, *pieces)


def packed_queries(q):
    tokens = q.shape[0]
    scaled = q.astype(jnp.float32) * query_scale
    scaled = scaled.reshape(tokens, 2, HD).transpose(2, 1, 0).reshape(HD, 2 * tokens)
    high = lax.reduce_precision(scaled, 8, 7)
    low = scaled - high
    return jnp.concatenate([high, low], axis=0).astype(jnp.bfloat16)


def values_in_blocks(v):
    tokens = v.shape[0]
    return v.reshape(tokens // HD, HD, HD).transpose(0, 2, 1).reshape(tokens, HD)


def layer(queries, key_rows, values, out_weight):
    core = lax.axis_index("c")
    x = lax.axis_index("x")
    zl = lax.axis_index("zl")
    spans_y, spans_z = lax.axis_size("y"), lax.axis_size("zh")
    spans = spans_y * spans_z
    span = lax.axis_index("y") * spans_z + lax.axis_index("zh")
    rows = queries.shape[0]
    width = out_weight.shape[1]
    half_width = width // 2

    mine = jnp.concatenate(
        [
            lax.dynamic_slice_in_dim(queries, core * PAIR, PAIR, 1),
            lax.dynamic_slice_in_dim(key_rows, core * HD, HD, 1),
            lax.dynamic_slice_in_dim(values, core * HD, HD, 1),
        ],
        axis=1,
    )
    theirs = jnp.concatenate(
        [
            lax.dynamic_slice_in_dim(queries, (1 - core) * PAIR, PAIR, 1),
            lax.dynamic_slice_in_dim(key_rows, (1 - core) * HD, HD, 1),
            lax.dynamic_slice_in_dim(values, (1 - core) * HD, HD, 1),
        ],
        axis=1,
    )
    got = moved(theirs, "c", lambda at: (1 - at[0],))
    first = jnp.where(core == 0, mine, got)
    second = jnp.where(core == 0, got, mine)

    kv_own = jnp.concatenate(
        [
            first[:, PAIR : PAIR + HD],
            second[:, PAIR : PAIR + HD],
            values_in_blocks(first[:, PAIR + HD :]),
            values_in_blocks(second[:, PAIR + HD :]),
        ],
        axis=0,
    )
    y_up = lambda a: moved(a, "y", lambda at: (at[0] + 1,))
    y_down = lambda a: moved(a, "y", lambda at: (at[0] - 1,))
    z_up = lambda a: moved(a, "zh", lambda at: (at[0] + 1,))
    z_down = lambda a: moved(a, "zh", lambda at: (at[0] - 1,))
    own_kv = kv_own
    z1, z3 = z_up(own_kv), z_down(own_kv)
    y1, y3 = y_up(own_kv), y_down(own_kv)
    mirror = lambda at: (spans_y - 1 - at[0], spans_z - 1 - at[1])
    lent = moved(second[:, :PAIR], ("y", "zh"), mirror)
    own_w = lax.dynamic_slice_in_dim(out_weight, core * half_width, half_width, 1)
    part = own_w.shape[0] // 2
    w_left = moved(own_w, "x", lambda at: (at[0] + 1,))
    w_right = moved(own_w, "x", lambda at: (at[0] - 1,))

    size = own_kv.shape[0] // 2
    pieces = [own_kv, y1, y3, y_up(y1[:size]), y_down(y3[size:])]
    z2 = jnp.concatenate([z_up(z1[:size]), z_down(z3[size:])], axis=0)
    z1_up, z1_down = y_up(z1), y_down(z1)
    z3_up, z3_down = y_up(z3), y_down(z3)
    pieces += [z1, z1_up, z1_down, y_up(z1_up)]
    pieces += [z3, z3_up, z3_down, y_down(z3_down)]
    z2_up, z2_down = y_up(z2), y_down(z2)
    pieces += [z2, z2_up, z2_down, y_up(z2_up[:size]), y_down(z2_down[size:])]
    w_left, w_right, *_ = lax.optimization_barrier((w_left, w_right, z1_up, z1_down, z3_up, z3_down))
    w_far_top = moved(w_left[:part], "x", lambda at: (at[0] + 1,))
    w_far_low = moved(w_right[part:], "x", lambda at: (at[0] - 1,))

    lent_len = jnp.maximum(2 * span - (spans - 1), 0)
    taken_len = jnp.maximum(spans - 1 - 2 * span, 0)
    ints = lambda *v: jnp.stack([jnp.asarray(e, jnp.int32) for e in v])
    order = jnp.arange(spans, dtype=jnp.int32)
    slots = (lax.axis_index("y") - order // spans_z) % spans_y * 4
    slots = (slots + (lax.axis_index("zh") - order % spans_z) % spans_z).astype(jnp.int32)
    q_all = jnp.stack([packed_queries(a) for a in (first[:, :PAIR], second[:, :PAIR], lent)])
    out, lse = attend(
        ints(0, lent_len, 0), ints(span, span, taken_len), ints(1, 1, 0), slots, q_all, pieces
    )
    back_out = moved(out[2], ("y", "zh"), mirror)
    back_lse = moved(lse[2], ("y", "zh"), mirror)
    back_lse = jnp.where(lent_len > 0, back_lse[0], neg_fill)
    joint = jnp.maximum(lse[1, 0], back_lse)
    own_part = jnp.exp2(lse[1, 0] - joint)
    back_part = jnp.exp2(back_lse - joint)
    total = own_part + back_part

    def by_row(a):
        return jnp.repeat(a.reshape(2, rows).T, HD, axis=1)

    merged = out[1].astype(jnp.float32) * by_row(own_part / total) + back_out.astype(
        jnp.float32
    ) * by_row(back_part / total)
    attended = jnp.stack([out[0], merged.astype(jnp.bfloat16)])

    groups = lax.axis_size("x")
    piece = rows // groups
    by_x = attended.reshape(2, groups, piece, PAIR).transpose(1, 0, 2, 3)
    by_x = by_x.reshape(groups, 2 * piece, PAIR)

    def towards(k):
        block = lax.dynamic_index_in_dim(by_x, (x + k) % groups, 0, keepdims=False)
        return block if k == 0 else moved(block, "x", lambda at: (at[0] + k,))

    heads_mine = jnp.concatenate([towards(k) for k in range(groups)], axis=1)
    heads_other = moved(heads_mine, "c", lambda at: (1 - at[0],))
    of_core = [jnp.where(core == 0, heads_mine, heads_other), jnp.where(core == 0, heads_other, heads_mine)]
    w_terms = [own_w, w_left, jnp.concatenate([w_far_top, w_far_low], axis=0), w_right]
    partial = 0.0
    for k in range(groups):
        lhs = jnp.concatenate([half[:, k * PAIR : (k + 1) * PAIR] for half in of_core], axis=1)
        partial = partial + jnp.dot(lhs, w_terms[k], preferred_element_type=jnp.float32)

    partial = partial.reshape(2, 2, piece // 2, half_width)

    def block_of(c_at, z_at):
        return lax.dynamic_slice(partial, (c_at, z_at, 0, 0), (1, 1, piece // 2, half_width))[0, 0]

    send_z = block_of(core, 1 - zl).astype(jnp.bfloat16)
    send_c = block_of(1 - core, zl).astype(jnp.bfloat16)
    send_cz = block_of(1 - core, 1 - zl).astype(jnp.bfloat16)
    got_z = moved(send_z, "zl", lambda at: (1 - at[0],))
    got_cz = moved(send_cz, ("c", "zl"), lambda at: (1 - at[0], 1 - at[1]))
    got_c = moved(send_c, "c", lambda at: (1 - at[0],))
    mine_cols = (block_of(core, zl) + got_z.astype(jnp.float32)).astype(jnp.bfloat16)
    other_cols = (got_c.astype(jnp.float32) + got_cz.astype(jnp.float32)).astype(jnp.bfloat16)
    return jnp.where(
        core == 0,
        jnp.concatenate([mine_cols, other_cols], axis=1),
        jnp.concatenate([other_cols, mine_cols], axis=1),
    )


def solution(mesh):
    names = ("y", "zh", "c", "x", "zl")
    torus = Mesh(mesh.devices.reshape(4, 4, 2, 4, 2), names)
    seq, head = ("y", "zh", "c"), ("x", "zl")
    in_specs = (P(seq, head), P(seq, head), P(seq, head), P(head, None))
    out_specs = P(seq + head, None)
    return jax.shard_map(layer, mesh=torus, in_specs=in_specs, out_specs=out_specs, check_vma=False)
```

profile of v0, /device:TPU:1, one launch (start us, length us, event | category | flops | bytes accessed | tf_op | source)
XLA Modules:
  0.0 244.3 jit_solution(10582458039982453561)
XLA Ops:
  0.0 1.1 constant_dynamic-slice_fusion.6
  1.1 1.1 constant_dynamic-slice_fusion.4
  2.3 3.3 %collective-permute-start = (bf16[512,512]{1,0:T(8,128)(2,1)S(1)}, bf16[512,512]{1,0:T(8,128)(2,1)S(1)}, u32[]{:S(2)}, u32[]{:S(2)}) collective-permute-start(bf16[512,512]{1,0:T(8,128)(2,1)S(1)} %pad_maximum_fusion.1), channel_id=1, source_target_pairs={{0,8},{8,0},{1,9},{9,1},{2,10},{10,2},{3,11},{11,3},{4,12},{12,4},... | collective-permute-start | bytes 1572872 | tf_op jit(solution)/shard_map/ppermute | solution.py:40
  5.6 1.5 collective-permute-done
  8.3 2.6 %collective-permute-start.6 = (bf16[2048,128]{1,0:T(8,128)(2,1)S(1)}, bf16[2048,128]{1,0:T(8,128)(2,1)S(1)}, u32[]{:S(2)}, u32[]{:S(2)}) collective-permute-start(bf16[2048,128]{1,0:T(8,128)(2,1)S(1)} %pad_maximum_fusion.2.refs_0_), channel_id=1, source_target_pairs={{0,16},{16,32},{32,48},{48,0},{1,17},{17,33},{33,49},{49,1},{2,18}... | collective-permute-start | bytes 1572872 | tf_op jit(solution)/shard_map/ppermute | solution.py:40
  10.8 3.0 %collective-permute-start.10 = (bf16[2048,128]{1,0:T(8,128)(2,1)S(1)}, bf16[2048,128]{1,0:T(8,128)(2,1)S(1)}, u32[]{:S(2)}, u32[]{:S(2)}) collective-permute-start(bf16[2048,128]{1,0:T(8,128)(2,1)S(1)} %pad_maximum_fusion.2.refs_0_), channel_id=1, source_target_pairs={{0,48},{16,0},{32,16},{48,32},{1,49},{17,1},{33,17},{49,33},{2,50}... | collective-permute-start | bytes 1572872 | tf_op jit(solution)/shard_map/ppermute | solution.py:40
  13.9 3.5 %constant_dynamic-slice_fusion = bf16[512,2688]{1,0:T(8,128)(2,1)} fusion(bf16[512,5376]{1,0:T(8,128)(2,1)} %param.7, s32[]{:T(128)S(6)} %select_n.155), kind=kLoop, calls=%fused_computation.82 | loop fusion | bytes 5505028 | tf_op jit(solution)/shard_map/dynamic_slice | solution.py:206
  17.4 1.6 collective-permute-start.3
  19.1 10.6 %collective-permute-done.6.refs_5_ = bf16[2048,128]{1,0:T(8,128)(2,1)S(1)} collective-permute-done((bf16[2048,128]{1,0:T(8,128)(2,1)S(1)}, bf16[2048,128]{1,0:T(8,128)(2,1)S(1)}, u32[]{:S(2)}, u32[]{:S(2)}) %collective-permute-start.6) | collective-permute-done | bytes 524320 | tf_op jit(solution)/shard_map/ppermute | solution.py:40
  29.7 7.8 %collective-permute-start.14 = (bf16[1024,128]{1,0:T(8,128)(2,1)S(1)}, bf16[1024,128]{1,0:T(8,128)(2,1)}, u32[]{:S(2)}, u32[]{:S(2)}) collective-permute-start(bf16[1024,128]{1,0:T(8,128)(2,1)S(1)} %slice.118), channel_id=1, source_target_pairs={{0,16},{16,32},{32,48},{48,0},{1,17},{17,33},{33,49},{49,1},{2,18}... | collective-permute-start | bytes 786440 | tf_op jit(solution)/shard_map/ppermute | solution.py:40
  39.0 4.9 %collective-permute-start.15 = (bf16[1024,128]{1,0:T(8,128)(2,1)}, bf16[1024,128]{1,0:T(8,128)(2,1)}, u32[]{:S(2)}, u32[]{:S(2)}) collective-permute-start(bf16[1024,128]{1,0:T(8,128)(2,1)} %slice.119), channel_id=1, source_target_pairs={{0,48},{16,0},{32,16},{48,32},{1,49},{17,1},{33,17},{49,33},{2,50}... | collective-permute-start | bytes 786440 | tf_op jit(solution)/shard_map/ppermute | solution.py:40
  44.8 1.3 reshape.155
  46.1 1.0 copy.13
  47.1 1.1 copy.22
  49.5 1.7 constant_dynamic-update-slice_fusion.1
  51.2 5.4 %collective-permute-done.15 = bf16[1024,128]{1,0:T(8,128)(2,1)} collective-permute-done((bf16[1024,128]{1,0:T(8,128)(2,1)}, bf16[1024,128]{1,0:T(8,128)(2,1)}, u32[]{:S(2)}, u32[]{:S(2)}) %collective-permute-start.15) | collective-permute-done | bytes 262176 | tf_op jit(solution)/shard_map/ppermute | solution.py:40
  56.6 1.1 collective-permute-start.12
  57.7 1.7 constant_dynamic-update-slice_fusion.refs_13_
  59.8 2.3 collective-permute-start.17
  62.0 0.9 fusion.16
  62.9 1.8 convert_multiply_fusion.2
  64.7 2.1 reshape.153
  66.8 1.9 copy.12
  68.7 1.1 copy.21
  70.6 2.3 collective-permute-done.7.refs_6_
  73.0 0.9 fusion.15
  73.8 1.5 collective-permute-start.11
  75.3 9.0 %collective-permute-done.16.refs_14_ = bf16[2048,128]{1,0:T(8,128)(2,1)} collective-permute-done((bf16[2048,128]{1,0:T(8,128)(2,1)}, bf16[2048,128]{1,0:T(8,128)(2,1)}, u32[]{:S(2)}, u32[]{:S(2)}) %collective-permute-start.16) | collective-permute-done | bytes 524320 | tf_op jit(solution)/shard_map/ppermute | solution.py:40
  84.3 2.7 %collective-permute-start.13 = (bf16[2048,128]{1,0:T(8,128)(2,1)}, bf16[2048,128]{1,0:T(8,128)(2,1)}, u32[]{:S(2)}, u32[]{:S(2)}) collective-permute-start(bf16[2048,128]{1,0:T(8,128)(2,1)} %collective-permute-done.12.refs_11_), channel_id=1, source_target_pairs={{0,192},{64,0},{128,64},{192,128},{1,193},{65,1},{129,65},{193,129... | collective-permute-start | bytes 1572872 | tf_op jit(solution)/shard_map/ppermute | solution.py:40
  87.0 1.8 convert_multiply_fusion
  88.8 2.1 reshape.157
  90.9 1.9 copy.14
  92.8 1.2 copy.23
  94.0 1.0 slice.120
  95.0 1.0 slice.121
  96.1 2.7 %collective-permute-start.19 = (bf16[1024,128]{1,0:T(8,128)(2,1)S(1)}, bf16[1024,128]{1,0:T(8,128)(2,1)S(1)}, u32[]{:S(2)}, u32[]{:S(2)}) collective-permute-start(bf16[1024,128]{1,0:T(8,128)(2,1)S(1)} %slice.121), channel_id=1, source_target_pairs={{0,192},{64,0},{128,64},{192,128},{1,193},{65,1},{129,65},{193,129... | collective-permute-start | bytes 786440 | tf_op jit(solution)/shard_map/ppermute | solution.py:40
  98.9 1.3 maximum_maximum_fusion.q_ref
  100.2 1.2 collective-permute-start.26
  101.4 5.4 %collective-permute-done.9.refs_8_ = bf16[2048,128]{1,0:T(8,128)(2,1)} collective-permute-done((bf16[2048,128]{1,0:T(8,128)(2,1)S(1)}, bf16[2048,128]{1,0:T(8,128)(2,1)}, u32[]{:S(2)}, u32[]{:S(2)}) %collective-permute-start.9) | collective-permute-done | bytes 524320 | tf_op jit(solution)/shard_map/ppermute | solution.py:40
  106.8 2.5 %collective-permute-start.27 = (bf16[512,2688]{1,0:T(8,128)(2,1)}, bf16[512,2688]{1,0:T(8,128)(2,1)}, u32[]{:S(2)}, u32[]{:S(2)}) collective-permute-start(bf16[512,2688]{1,0:T(8,128)(2,1)} %constant_dynamic-slice_fusion), channel_id=1, source_target_pairs={{0,6},{2,0},{4,2},{6,4},{1,7},{3,1},{5,3},{7,5},{8,14},{10,8},{12,... | collective-permute-start | bytes 8257544 | tf_op jit(solution)/shard_map/ppermute | solution.py:40
  109.8 32.2 %shard_map.46 = (bf16[3,512,256]{2,1,0:T(8,128)(2,1)}, f32[3,1,1024]{2,1,0:T(1,128)S(1)}) custom-call(s32[3]{0:T(128)S(1)} %get-tuple-element.54.lo, s32[3]{0:T(128)S(1)} %get-tuple-element.55.hi, s32[3]{0:T(128)S(1)} %copy-done, s32[16]{0:T(128)S(1)} %fusion.39.slots, bf16[3,256,1024]{2,1,0:T(8,128)(2,1)} %maximum_maximum_fusion.q_ref, ...), custom_call_target="tpu_custom_call" | custom-call | flops 8589934592 | bytes 9000000 | tf_op jit(solution)/shard_map/pallas_call | solution.py:121
  142.0 4.4 %collective-permute-start.20 = (f32[1,1024]{1,0:T(1,128)S(1)}, f32[1,1024]{1,0:T(1,128)S(1)}, u32[]{:S(2)}, u32[]{:S(2)}) collective-permute-start(f32[1,1024]{1,0:T(1,128)S(1)} %get-tuple-element.51), channel_id=1, source_target_pairs={{0,240},{16,224},{32,208},{48,192},{64,176},{80,160},{96,144},{112... | collective-permute-start | bytes 12296 | tf_op jit(solution)/shard_map/ppermute | solution.py:40
  146.4 1.1 fusion.48
  147.5 1.7 collective-permute-start.21
  149.6 7.8 %collective-permute-done.21 = bf16[512,256]{1,0:T(8,128)(2,1)S(1)} collective-permute-done((bf16[512,256]{1,0:T(8,128)(2,1)S(1)}, bf16[512,256]{1,0:T(8,128)(2,1)S(1)}, u32[]{:S(2)}, u32[]{:S(2)}) %collective-permute-start.21) | collective-permute-done | bytes 262176 | tf_op jit(solution)/shard_map/ppermute | solution.py:40
  158.6 1.1 fusion.8
  159.7 2.6 %collective-permute-start.24 = (bf16[256,256]{1,0:T(8,128)(2,1)S(1)}, bf16[256,256]{1,0:T(8,128)(2,1)S(1)}, u32[]{:S(2)}, u32[]{:S(2)}) collective-permute-start(bf16[256,256]{1,0:T(8,128)(2,1)S(1)} %get-tuple-element.31), channel_id=1, source_target_pairs={{0,6},{2,0},{4,2},{6,4},{1,7},{3,1},{5,3},{7,5},{8,14},{10,8},{12,... | collective-permute-start | bytes 393224 | tf_op jit(solution)/shard_map/ppermute | solution.py:40
  163.4 3.9 %collective-permute-done.24 = bf16[256,256]{1,0:T(8,128)(2,1)S(1)} collective-permute-done((bf16[256,256]{1,0:T(8,128)(2,1)S(1)}, bf16[256,256]{1,0:T(8,128)(2,1)S(1)}, u32[]{:S(2)}, u32[]{:S(2)}) %collective-permute-start.24) | collective-permute-done | bytes 131104 | tf_op jit(solution)/shard_map/ppermute | solution.py:40
  167.7 1.3 collective-permute-done.22
  169.1 11.1 %collective-permute-start.25 = (bf16[256,1024]{1,0:T(8,128)(2,1)S(1)}, bf16[256,1024]{1,0:T(8,128)(2,1)S(1)}, u32[]{:S(2)}, u32[]{:S(2)}) collective-permute-start(bf16[256,1024]{1,0:T(8,128)(2,1)S(1)} %pad_maximum_fusion.4), channel_id=1, source_target_pairs={{0,8},{8,0},{1,9},{9,1},{2,10},{10,2},{3,11},{11,3},{4,12},{12,4},... | collective-permute-start | bytes 1572872 | tf_op jit(solution)/shard_map/ppermute | solution.py:40
  180.2 1.4 slice.107
  182.0 1.4 slice.106
  183.4 1.3 collective-permute-start.28
  185.0 2.7 %fusion.18 = f32[256,2688]{1,0:T(8,128)S(1)} fusion(bf16[512,2688]{1,0:T(8,128)(2,1)} %constant_dynamic-slice_fusion, bf16[256,256]{1,0:T(8,128)(2,1)S(1)} %get-tuple-element.29, bf16[256,256]{1,0:T(8,128)(2,1)S(1)} %get-tuple-element.25), kind=kOutput, calls=%fused_computation.48 | convolution fusion | flops 705167360 | bytes 5767168 | tf_op jit(solution)/shard_map/dot_general | solution.py:266
  187.7 2.7 %convolution_add_fusion.2 = f32[256,2688]{1,0:T(8,128)S(1)} fusion(f32[256,2688]{1,0:T(8,128)S(1)} %fusion.18, bf16[512,2688]{1,0:T(8,128)(2,1)} %collective-permute-done.26, bf16[256,256]{1,0:T(8,128)(2,1)S(1)} %get-tuple-element.28, bf16[256,256]{1,0:T(8,128)(2,1)S(1)} %get-tuple-element.24), kind=kOutput, calls=%fused_computation.2 | convolution fusion | flops 705855488 | bytes 8519680 | tf_op jit(solution)/shard_map/dot_general | solution.py:266
  190.4 23.0 %collective-permute-done.29 = bf16[256,2688]{1,0:T(8,128)(2,1)S(1)} collective-permute-done((bf16[256,2688]{1,0:T(8,128)(2,1)S(1)}, bf16[256,2688]{1,0:T(8,128)(2,1)S(1)}, u32[]{:S(2)}, u32[]{:S(2)}) %collective-permute-start.29) | collective-permute-done | bytes 1376288 | tf_op jit(solution)/shard_map/ppermute | solution.py:40
  213.4 2.7 %collective-permute-done.28 = bf16[256,2688]{1,0:T(8,128)(2,1)S(1)} collective-permute-done((bf16[256,2688]{1,0:T(8,128)(2,1)S(1)}, bf16[256,2688]{1,0:T(8,128)(2,1)S(1)}, u32[]{:S(2)}, u32[]{:S(2)}) %collective-permute-start.28) | collective-permute-done | bytes 1376288 | tf_op jit(solution)/shard_map/ppermute | solution.py:40
  216.1 0.9 convolution_add_fusion.1
  217.0 2.7 %convolution_add_fusion = f32[256,2688]{1,0:T(8,128)S(1)} fusion(f32[256,2688]{1,0:T(8,128)S(1)} %convolution_add_fusion.1, bf16[512,2688]{1,0:T(8,128)(2,1)} %collective-permute-done.27, bf16[256,256]{1,0:T(8,128)(2,1)S(1)} %get-tuple-element.26, bf16[256,256]{1,0:T(8,128)(2,1)S(1)} %get-tuple-element.22), kind=kOutput, calls=%fused_computation | convolution fusion | flops 705855488 | bytes 8519680 | tf_op jit(solution)/shard_map/dot_general | solution.py:266
  219.9 7.6 %collective-permute-start.30 = (bf16[64,2688]{1,0:T(8,128)(2,1)S(1)}, bf16[64,2688]{1,0:T(8,128)(2,1)S(1)}, u32[]{:S(2)}, u32[]{:S(2)}) collective-permute-start(bf16[64,2688]{1,0:T(8,128)(2,1)S(1)} %get-tuple-element.13), channel_id=1, source_target_pairs={{0,1},{1,0},{2,3},{3,2},{4,5},{5,4},{6,7},{7,6},{8,9},{9,8},{10,11... | collective-permute-start | bytes 1032200 | tf_op jit(solution)/shard_map/ppermute | solution.py:40
  227.5 1.2 collective-permute-start.32
  228.9 5.8 %collective-permute-done.30 = bf16[64,2688]{1,0:T(8,128)(2,1)S(1)} collective-permute-done((bf16[64,2688]{1,0:T(8,128)(2,1)S(1)}, bf16[64,2688]{1,0:T(8,128)(2,1)S(1)}, u32[]{:S(2)}, u32[]{:S(2)}) %collective-permute-start.30) | collective-permute-done | bytes 344096 | tf_op jit(solution)/shard_map/ppermute | solution.py:40
  234.8 8.4 %collective-permute-done.32 = bf16[64,2688]{1,0:T(8,128)(2,1)S(1)} collective-permute-done((bf16[64,2688]{1,0:T(8,128)(2,1)S(1)}, bf16[64,2688]{1,0:T(8,128)(2,1)S(1)}, u32[]{:S(2)}, u32[]{:S(2)}) %collective-permute-start.32) | collective-permute-done | bytes 344096 | tf_op jit(solution)/shard_map/ppermute | solution.py:40
  243.2 1.0 maximum_select_fusion
  (79 shorter events, 11.2 us)
Async XLA Ops:
  2.3 4.8 %collective-permute-start = (bf16[512,512]{1,0:T(8,128)(2,1)S(1)}, bf16[512,512]{1,0:T(8,128)(2,1)S(1)}, u32[]{:S(2)}, u32[]{:S(2)}) collective-permute-start(bf16[512,512]{1,0:T(8,128)(2,1)S(1)} %pad_maximum_fusion.1), channel_id=1, source_target_pairs={{0,8},{8,0},{1,9},{9,1},{2,10},{10,2},{3,11},{11,3},{4,12},{12,4},... | collective-permute-start | bytes 1572872 | tf_op jit(solution)/shard_map/ppermute | solution.py:40
  7.4 0.8 copy-start.1
  8.2 40.1 %collective-permute-start.2 = (bf16[2048,128]{1,0:T(8,128)(2,1)S(1)}, bf16[2048,128]{1,0:T(8,128)(2,1)S(1)}, u32[]{:S(2)}, u32[]{:S(2)}) collective-permute-start(bf16[2048,128]{1,0:T(8,128)(2,1)S(1)} %pad_maximum_fusion.2.refs_0_), channel_id=1, source_target_pairs={{0,64},{64,128},{128,192},{192,0},{1,65},{65,129},{129,193},{193,1... | collective-permute-start | bytes 1572872 | tf_op jit(solution)/shard_map/ppermute | solution.py:40
  8.3 21.4 %collective-permute-start.6 = (bf16[2048,128]{1,0:T(8,128)(2,1)S(1)}, bf16[2048,128]{1,0:T(8,128)(2,1)S(1)}, u32[]{:S(2)}, u32[]{:S(2)}) collective-permute-start(bf16[2048,128]{1,0:T(8,128)(2,1)S(1)} %pad_maximum_fusion.2.refs_0_), channel_id=1, source_target_pairs={{0,16},{16,32},{32,48},{48,0},{1,17},{17,33},{33,49},{49,1},{2,18}... | collective-permute-start | bytes 1572872 | tf_op jit(solution)/shard_map/ppermute | solution.py:40
  10.8 27.4 %collective-permute-start.10 = (bf16[2048,128]{1,0:T(8,128)(2,1)S(1)}, bf16[2048,128]{1,0:T(8,128)(2,1)S(1)}, u32[]{:S(2)}, u32[]{:S(2)}) collective-permute-start(bf16[2048,128]{1,0:T(8,128)(2,1)S(1)} %pad_maximum_fusion.2.refs_0_), channel_id=1, source_target_pairs={{0,48},{16,0},{32,16},{48,32},{1,49},{17,1},{33,17},{49,33},{2,50}... | collective-permute-start | bytes 1572872 | tf_op jit(solution)/shard_map/ppermute | solution.py:40
  17.4 42.3 %collective-permute-start.3 = (bf16[2048,128]{1,0:T(8,128)(2,1)S(1)}, bf16[2048,128]{1,0:T(8,128)(2,1)S(1)}, u32[]{:S(2)}, u32[]{:S(2)}) collective-permute-start(bf16[2048,128]{1,0:T(8,128)(2,1)S(1)} %pad_maximum_fusion.2.refs_0_), channel_id=1, source_target_pairs={{0,192},{64,0},{128,64},{192,128},{1,193},{65,1},{129,65},{193,129... | collective-permute-start | bytes 1572872 | tf_op jit(solution)/shard_map/ppermute | solution.py:40
  29.7 19.4 %collective-permute-start.14 = (bf16[1024,128]{1,0:T(8,128)(2,1)S(1)}, bf16[1024,128]{1,0:T(8,128)(2,1)}, u32[]{:S(2)}, u32[]{:S(2)}) collective-permute-start(bf16[1024,128]{1,0:T(8,128)(2,1)S(1)} %slice.118), channel_id=1, source_target_pairs={{0,16},{16,32},{32,48},{48,0},{1,17},{17,33},{33,49},{49,1},{2,18}... | collective-permute-start | bytes 786440 | tf_op jit(solution)/shard_map/ppermute | solution.py:40
  38.3 21.1 %collective-permute-start.1 = (bf16[512,256]{1,0:T(8,128)(2,1)}, bf16[512,256]{1,0:T(8,128)(2,1)}, u32[]{:S(2)}, u32[]{:S(2)}) collective-permute-start(bf16[512,256]{1,0:T(8,128)(2,1)} %slice.111), channel_id=1, source_target_pairs={{0,240},{16,224},{32,208},{48,192},{64,176},{80,160},{96,144},{112... | collective-permute-start | bytes 786440 | tf_op jit(solution)/shard_map/ppermute | solution.py:40
  39.0 17.6 %collective-permute-start.15 = (bf16[1024,128]{1,0:T(8,128)(2,1)}, bf16[1024,128]{1,0:T(8,128)(2,1)}, u32[]{:S(2)}, u32[]{:S(2)}) collective-permute-start(bf16[1024,128]{1,0:T(8,128)(2,1)} %slice.119), channel_id=1, source_target_pairs={{0,48},{16,0},{32,16},{48,32},{1,49},{17,1},{33,17},{49,33},{2,50}... | collective-permute-start | bytes 786440 | tf_op jit(solution)/shard_map/ppermute | solution.py:40
  48.3 14.6 %collective-permute-start.4 = (bf16[1024,128]{1,0:T(8,128)(2,1)S(1)}, bf16[1024,128]{1,0:T(8,128)(2,1)S(1)}, u32[]{:S(2)}, u32[]{:S(2)}) collective-permute-start(bf16[1024,128]{1,0:T(8,128)(2,1)S(1)} %slice.116), channel_id=1, source_target_pairs={{0,64},{64,128},{128,192},{192,0},{1,65},{65,129},{129,193},{193,1... | collective-permute-start | bytes 786440 | tf_op jit(solution)/shard_map/ppermute | solution.py:40
  49.0 23.9 %collective-permute-start.7 = (bf16[2048,128]{1,0:T(8,128)(2,1)S(1)}, bf16[2048,128]{1,0:T(8,128)(2,1)S(1)}, u32[]{:S(2)}, u32[]{:S(2)}) collective-permute-start(bf16[2048,128]{1,0:T(8,128)(2,1)S(1)} %collective-permute-done.6.refs_5_), channel_id=1, source_target_pairs={{0,64},{64,128},{128,192},{192,0},{1,65},{65,129},{129,193},{193,1... | collective-permute-start | bytes 1572872 | tf_op jit(solution)/shard_map/ppermute | solution.py:40
  56.6 17.2 %collective-permute-start.12 = (bf16[2048,128]{1,0:T(8,128)(2,1)S(1)}, bf16[2048,128]{1,0:T(8,128)(2,1)}, u32[]{:S(2)}, u32[]{:S(2)}) collective-permute-start(bf16[2048,128]{1,0:T(8,128)(2,1)S(1)} %collective-permute-done.10.refs_9_), channel_id=1, source_target_pairs={{0,192},{64,0},{128,64},{192,128},{1,193},{65,1},{129,65},{193,129... | collective-permute-start | bytes 1572872 | tf_op jit(solution)/shard_map/ppermute | solution.py:40
  59.4 24.9 %collective-permute-start.16 = (bf16[2048,128]{1,0:T(8,128)(2,1)}, bf16[2048,128]{1,0:T(8,128)(2,1)}, u32[]{:S(2)}, u32[]{:S(2)}) collective-permute-start(bf16[2048,128]{1,0:T(8,128)(2,1)} %constant_dynamic-update-slice_fusion.refs_13_), channel_id=1, source_target_pairs={{0,64},{64,128},{128,192},{192,0},{1,65},{65,129},{129,193},{193,1... | collective-permute-start | bytes 1572872 | tf_op jit(solution)/shard_map/ppermute | solution.py:40
  59.8 24.5 %collective-permute-start.17 = (bf16[2048,128]{1,0:T(8,128)(2,1)}, bf16[2048,128]{1,0:T(8,128)(2,1)}, u32[]{:S(2)}, u32[]{:S(2)}) collective-permute-start(bf16[2048,128]{1,0:T(8,128)(2,1)} %constant_dynamic-update-slice_fusion.refs_13_), channel_id=1, source_target_pairs={{0,192},{64,0},{128,64},{192,128},{1,193},{65,1},{129,65},{193,129... | collective-permute-start | bytes 1572872 | tf_op jit(solution)/shard_map/ppermute | solution.py:40
  62.9 33.2 %collective-permute-start.8 = (bf16[2048,128]{1,0:T(8,128)(2,1)S(1)}, bf16[2048,128]{1,0:T(8,128)(2,1)}, u32[]{:S(2)}, u32[]{:S(2)}) collective-permute-start(bf16[2048,128]{1,0:T(8,128)(2,1)S(1)} %collective-permute-done.6.refs_5_), channel_id=1, source_target_pairs={{0,192},{64,0},{128,64},{192,128},{1,193},{65,1},{129,65},{193,129... | collective-permute-start | bytes 1572872 | tf_op jit(solution)/shard_map/ppermute | solution.py:40
  73.0 23.0 %collective-permute-start.5 = (bf16[1024,128]{1,0:T(8,128)(2,1)}, bf16[1024,128]{1,0:T(8,128)(2,1)}, u32[]{:S(2)}, u32[]{:S(2)}) collective-permute-start(bf16[1024,128]{1,0:T(8,128)(2,1)} %slice.117), channel_id=1, source_target_pairs={{0,192},{64,0},{128,64},{192,128},{1,193},{65,1},{129,65},{193,129... | collective-permute-start | bytes 786440 | tf_op jit(solution)/shard_map/ppermute | solution.py:40
  73.8 26.3 %collective-permute-start.11 = (bf16[2048,128]{1,0:T(8,128)(2,1)S(1)}, bf16[2048,128]{1,0:T(8,128)(2,1)}, u32[]{:S(2)}, u32[]{:S(2)}) collective-permute-start(bf16[2048,128]{1,0:T(8,128)(2,1)S(1)} %collective-permute-done.10.refs_9_), channel_id=1, source_target_pairs={{0,64},{64,128},{128,192},{192,0},{1,65},{65,129},{129,193},{193,1... | collective-permute-start | bytes 1572872 | tf_op jit(solution)/shard_map/ppermute | solution.py:40
  84.3 22.5 %collective-permute-start.9 = (bf16[2048,128]{1,0:T(8,128)(2,1)S(1)}, bf16[2048,128]{1,0:T(8,128)(2,1)}, u32[]{:S(2)}, u32[]{:S(2)}) collective-permute-start(bf16[2048,128]{1,0:T(8,128)(2,1)S(1)} %collective-permute-done.7.refs_6_), channel_id=1, source_target_pairs={{0,64},{64,128},{128,192},{192,0},{1,65},{65,129},{129,193},{193,1... | collective-permute-start | bytes 1572872 | tf_op jit(solution)/shard_map/ppermute | solution.py:40
  84.3 24.9 %collective-permute-start.13 = (bf16[2048,128]{1,0:T(8,128)(2,1)}, bf16[2048,128]{1,0:T(8,128)(2,1)}, u32[]{:S(2)}, u32[]{:S(2)}) collective-permute-start(bf16[2048,128]{1,0:T(8,128)(2,1)} %collective-permute-done.12.refs_11_), channel_id=1, source_target_pairs={{0,192},{64,0},{128,64},{192,128},{1,193},{65,1},{129,65},{193,129... | collective-permute-start | bytes 1572872 | tf_op jit(solution)/shard_map/ppermute | solution.py:40
  92.8 6.1 %copy-start.2 = (bf16[1,128,1024]{2,1,0:T(8,128)(2,1)S(1)}, bf16[1,128,1024]{2,1,0:T(8,128)(2,1)}, u32[]{:S(2)}) copy-start(bf16[1,128,1024]{2,1,0:T(8,128)(2,1)} %get-tuple-element.40) | copy-start | bytes 786436
  92.8 6.1 %copy-start.3 = (bf16[1,128,1024]{2,1,0:T(8,128)(2,1)S(1)}, bf16[1,128,1024]{2,1,0:T(8,128)(2,1)}, u32[]{:S(2)}) copy-start(bf16[1,128,1024]{2,1,0:T(8,128)(2,1)} %get-tuple-element.41) | copy-start | bytes 786436
  92.8 6.1 %copy-start.4 = (bf16[1,128,1024]{2,1,0:T(8,128)(2,1)S(1)}, bf16[1,128,1024]{2,1,0:T(8,128)(2,1)}, u32[]{:S(2)}) copy-start(bf16[1,128,1024]{2,1,0:T(8,128)(2,1)} %get-tuple-element.38) | copy-start | bytes 786436
  92.8 6.1 %copy-start.5 = (bf16[1,128,1024]{2,1,0:T(8,128)(2,1)S(1)}, bf16[1,128,1024]{2,1,0:T(8,128)(2,1)}, u32[]{:S(2)}) copy-start(bf16[1,128,1024]{2,1,0:T(8,128)(2,1)} %get-tuple-element.39) | copy-start | bytes 786436
  94.0 15.8 %copy-start = (s32[3]{0:T(128)S(1)}, s32[3]{0:T(128)}, u32[]{:S(2)}) copy-start(s32[3]{0:T(128)} %constant.107.clone.1.diag) | copy-start | bytes 40
  96.0 13.8 %collective-permute-start.18 = (bf16[1024,128]{1,0:T(8,128)(2,1)S(1)}, bf16[1024,128]{1,0:T(8,128)(2,1)S(1)}, u32[]{:S(2)}, u32[]{:S(2)}) collective-permute-start(bf16[1024,128]{1,0:T(8,128)(2,1)S(1)} %slice.120), channel_id=1, source_target_pairs={{0,64},{64,128},{128,192},{192,0},{1,65},{65,129},{129,193},{193,1... | collective-permute-start | bytes 786440 | tf_op jit(solution)/shard_map/ppermute | solution.py:40
  96.1 13.7 %collective-permute-start.19 = (bf16[1024,128]{1,0:T(8,128)(2,1)S(1)}, bf16[1024,128]{1,0:T(8,128)(2,1)S(1)}, u32[]{:S(2)}, u32[]{:S(2)}) collective-permute-start(bf16[1024,128]{1,0:T(8,128)(2,1)S(1)} %slice.121), channel_id=1, source_target_pairs={{0,192},{64,0},{128,64},{192,128},{1,193},{65,1},{129,65},{193,129... | collective-permute-start | bytes 786440 | tf_op jit(solution)/shard_map/ppermute | solution.py:40
  100.2 80.0 %collective-permute-start.26 = (bf16[512,2688]{1,0:T(8,128)(2,1)}, bf16[512,2688]{1,0:T(8,128)(2,1)}, u32[]{:S(2)}, u32[]{:S(2)}) collective-permute-start(bf16[512,2688]{1,0:T(8,128)(2,1)} %constant_dynamic-slice_fusion), channel_id=1, source_target_pairs={{0,2},{2,4},{4,6},{6,0},{1,3},{3,5},{5,7},{7,1},{8,10},{10,12},{12... | collective-permute-start | bytes 8257544 | tf_op jit(solution)/shard_map/ppermute | solution.py:40
  106.8 73.4 %collective-permute-start.27 = (bf16[512,2688]{1,0:T(8,128)(2,1)}, bf16[512,2688]{1,0:T(8,128)(2,1)}, u32[]{:S(2)}, u32[]{:S(2)}) collective-permute-start(bf16[512,2688]{1,0:T(8,128)(2,1)} %constant_dynamic-slice_fusion), channel_id=1, source_target_pairs={{0,6},{2,0},{4,2},{6,4},{1,7},{3,1},{5,3},{7,5},{8,14},{10,8},{12,... | collective-permute-start | bytes 8257544 | tf_op jit(solution)/shard_map/ppermute | solution.py:40
  142.0 7.2 %collective-permute-start.20 = (f32[1,1024]{1,0:T(1,128)S(1)}, f32[1,1024]{1,0:T(1,128)S(1)}, u32[]{:S(2)}, u32[]{:S(2)}) collective-permute-start(f32[1,1024]{1,0:T(1,128)S(1)} %get-tuple-element.51), channel_id=1, source_target_pairs={{0,240},{16,224},{32,208},{48,192},{64,176},{80,160},{96,144},{112... | collective-permute-start | bytes 12296 | tf_op jit(solution)/shard_map/ppermute | solution.py:40
  147.5 9.8 %collective-permute-start.21 = (bf16[512,256]{1,0:T(8,128)(2,1)S(1)}, bf16[512,256]{1,0:T(8,128)(2,1)S(1)}, u32[]{:S(2)}, u32[]{:S(2)}) collective-permute-start(bf16[512,256]{1,0:T(8,128)(2,1)S(1)} %get-tuple-element.21), channel_id=1, source_target_pairs={{0,240},{16,224},{32,208},{48,192},{64,176},{80,160},{96,144},{112... | collective-permute-start | bytes 786440 | tf_op jit(solution)/shard_map/ppermute | solution.py:40
  159.7 7.6 %collective-permute-start.24 = (bf16[256,256]{1,0:T(8,128)(2,1)S(1)}, bf16[256,256]{1,0:T(8,128)(2,1)S(1)}, u32[]{:S(2)}, u32[]{:S(2)}) collective-permute-start(bf16[256,256]{1,0:T(8,128)(2,1)S(1)} %get-tuple-element.31), channel_id=1, source_target_pairs={{0,6},{2,0},{4,2},{6,4},{1,7},{3,1},{5,3},{7,5},{8,14},{10,8},{12,... | collective-permute-start | bytes 393224 | tf_op jit(solution)/shard_map/ppermute | solution.py:40
  162.3 5.4 %collective-permute-start.23 = (bf16[256,256]{1,0:T(8,128)(2,1)S(1)}, bf16[256,256]{1,0:T(8,128)(2,1)S(1)}, u32[]{:S(2)}, u32[]{:S(2)}) collective-permute-start(bf16[256,256]{1,0:T(8,128)(2,1)S(1)} %get-tuple-element.32), channel_id=1, source_target_pairs={{0,4},{2,6},{4,0},{6,2},{1,5},{3,7},{5,1},{7,3},{8,12},{10,14},{12... | collective-permute-start | bytes 393224 | tf_op jit(solution)/shard_map/ppermute | solution.py:40
  162.8 6.2 %collective-permute-start.22 = (bf16[256,256]{1,0:T(8,128)(2,1)S(1)}, bf16[256,256]{1,0:T(8,128)(2,1)S(1)}, u32[]{:S(2)}, u32[]{:S(2)}) collective-permute-start(bf16[256,256]{1,0:T(8,128)(2,1)S(1)} %get-tuple-element.33), channel_id=1, source_target_pairs={{0,2},{2,4},{4,6},{6,0},{1,3},{3,5},{5,7},{7,1},{8,10},{10,12},{12... | collective-permute-start | bytes 393224 | tf_op jit(solution)/shard_map/ppermute | solution.py:40
  169.1 15.6 %collective-permute-start.25 = (bf16[256,1024]{1,0:T(8,128)(2,1)S(1)}, bf16[256,1024]{1,0:T(8,128)(2,1)S(1)}, u32[]{:S(2)}, u32[]{:S(2)}) collective-permute-start(bf16[256,1024]{1,0:T(8,128)(2,1)S(1)} %pad_maximum_fusion.4), channel_id=1, source_target_pairs={{0,8},{8,0},{1,9},{9,1},{2,10},{10,2},{3,11},{11,3},{4,12},{12,4},... | collective-permute-start | bytes 1572872 | tf_op jit(solution)/shard_map/ppermute | solution.py:40
  181.6 31.8 %collective-permute-start.29 = (bf16[256,2688]{1,0:T(8,128)(2,1)S(1)}, bf16[256,2688]{1,0:T(8,128)(2,1)S(1)}, u32[]{:S(2)}, u32[]{:S(2)}) collective-permute-start(bf16[256,2688]{1,0:T(8,128)(2,1)S(1)} %slice.107), channel_id=1, source_target_pairs={{0,6},{2,0},{4,2},{6,4},{1,7},{3,1},{5,3},{7,5},{8,14},{10,8},{12,... | collective-permute-start | bytes 4128776 | tf_op jit(solution)/shard_map/ppermute | solution.py:40
  183.4 32.7 %collective-permute-start.28 = (bf16[256,2688]{1,0:T(8,128)(2,1)S(1)}, bf16[256,2688]{1,0:T(8,128)(2,1)S(1)}, u32[]{:S(2)}, u32[]{:S(2)}) collective-permute-start(bf16[256,2688]{1,0:T(8,128)(2,1)S(1)} %slice.106), channel_id=1, source_target_pairs={{0,2},{2,4},{4,6},{6,0},{1,3},{3,5},{5,7},{7,1},{8,10},{10,12},{12... | collective-permute-start | bytes 4128776 | tf_op jit(solution)/shard_map/ppermute | solution.py:40
  219.9 14.8 %collective-permute-start.30 = (bf16[64,2688]{1,0:T(8,128)(2,1)S(1)}, bf16[64,2688]{1,0:T(8,128)(2,1)S(1)}, u32[]{:S(2)}, u32[]{:S(2)}) collective-permute-start(bf16[64,2688]{1,0:T(8,128)(2,1)S(1)} %get-tuple-element.13), channel_id=1, source_target_pairs={{0,1},{1,0},{2,3},{3,2},{4,5},{5,4},{6,7},{7,6},{8,9},{9,8},{10,11... | collective-permute-start | bytes 1032200 | tf_op jit(solution)/shard_map/ppermute | solution.py:40
  227.5 15.7 %collective-permute-start.32 = (bf16[64,2688]{1,0:T(8,128)(2,1)S(1)}, bf16[64,2688]{1,0:T(8,128)(2,1)S(1)}, u32[]{:S(2)}, u32[]{:S(2)}) collective-permute-start(bf16[64,2688]{1,0:T(8,128)(2,1)S(1)} %get-tuple-element.14), channel_id=1, source_target_pairs={{0,9},{1,8},{8,1},{9,0},{2,11},{3,10},{10,3},{11,2},{4,13},{5,12},... | collective-permute-start | bytes 1032200 | tf_op jit(solution)/shard_map/ppermute | solution.py:40
  228.6 14.5 %collective-permute-start.31 = (bf16[64,2688]{1,0:T(8,128)(2,1)S(1)}, bf16[64,2688]{1,0:T(8,128)(2,1)S(1)}, u32[]{:S(2)}, u32[]{:S(2)}) collective-permute-start(bf16[64,2688]{1,0:T(8,128)(2,1)S(1)} %get-tuple-element.15), channel_id=1, source_target_pairs={{0,8},{8,0},{1,9},{9,1},{2,10},{10,2},{3,11},{11,3},{4,12},{12,4},... | collective-permute-start | bytes 1032200 | tf_op jit(solution)/shard_map/ppermute | solution.py:40
where the time goes:
time: 248 us; the launch traced here: 244 us
  waiting for transfers between devices  88.1 us (36%)
  starting transfers between devices  70.3 us (28%)
  local copies, waits for them, and re-layouts  33.6 us (14%)
  Pallas kernels  32.2 us (13%)
  other arithmetic  10.5 us (4%)
  matrix products  9.08 us (4%)
    ppermute x33, waiting for transfers between devices, moved(): return lax.ppermute(value, axes, pairs)  88.1 us
    ppermute x33, starting transfers between devices, moved(): return lax.ppermute(value, axes, pairs)  70.3 us
    pallas_call x1, Pallas kernels, attend(): pl.pallas_call(attend_kernel, out_shape=(jax.ShapeDtypeStruct((tasks, row...  32.2 us
    dot_general x4, matrix products, layer(): jnp.dot(lhs, w_terms[k], preferred_element_type=jnp.float32)  9.08 us
    unnamed x16, local copies, waits for them, and re-layouts  5.65 us
    reshape x3, local copies, waits for them, and re-layouts, packed_queries(): scaled.reshape(tokens, 2, HD).transpose(2, 1, 0).reshape(HD, 2 * tokens)  5.5 us
  transfers between devices with their start and end apart: 33, of which 15 were waited for; matrix products, arithmetic and copies ran while one was open for 18% of the time, Pallas kernels for 13%

commit v1 on v0

--- a/solution.py
+++ b/solution.py
@@ -13,8 +13,7 @@
 neg_fill = -1e30
 TILE = 256
 PLACES = (
-    [(4 * dy, 0) for dy in (0, 1, 3)]
-    + [(8, 0), (8, 1)]
+    [(4 * dy, 0) for dy in (0, 1, 3, 2)]
     + [(4 * dy + dz, 0) for dz in (1, 3) for dy in (0, 1, 3, 2)]
     + [(4 * dy + 2, 0) for dy in (0, 1, 3)]
     + [(10, 0), (10, 1)]
@@ -41,7 +40,7 @@
 
 
 def attend_kernel(lo, hi, diag, slots, q_ref, *refs):
-    pieces, (out_ref, lse_ref, kv_ref, m_ref, l_ref, acc_ref, sems) = refs[:-7], refs[-7:]
+    pieces, (out_ref, lse_ref, kv_ref, s_ref, m_ref, l_ref, acc_ref, sems) = refs[:-8], refs[-8:]
     tasks, _, rows = q_ref.shape
     half = rows // 2
     span = kv_ref.shape[1] // 2
@@ -57,20 +56,25 @@
     for copy in copies:
         copy.wait()
 
-    def step(task, at_span, masked):
+    tiles = [pl.ds(r * TILE, TILE) for r in range(rows // TILE)]
+
+    def keys_twice(at_span):
+        keys = kv_ref[slots[at_span], pl.ds(0, span), :]
+        return jnp.concatenate([keys, keys], axis=1)
+
+    def scores_of(keys, task, cols):
+        return jnp.dot(keys, q_ref[task, :, cols], preferred_element_type=jnp.float32)
+
+    def step(task, at_span, last):
         slot = slots[at_span]
-        keys = kv_ref[slot, pl.ds(0, span), :]
-        keys_twice = jnp.concatenate([keys, keys], axis=1)
         values_t = jnp.concatenate(
             [kv_ref[slot, pl.ds(span + i * HD, HD), :] for i in range(span // HD)], axis=1
         )
-        tiles = [pl.ds(r * TILE, TILE) for r in range(rows // TILE)]
-        all_scores = [
-            jnp.dot(keys_twice, q_ref[task, :, cols], preferred_element_type=jnp.float32)
-            for cols in tiles
-        ]
-        for r, (cols, scores) in enumerate(zip(tiles, all_scores)):
-            if masked:
+        keys = None if last else keys_twice(at_span + 1)
+        for r, cols in enumerate(tiles):
+            scores = s_ref[:, cols]
+            following = None if last else scores_of(keys, task, cols)
+            if last:
                 key_pos = lax.broadcasted_iota(jnp.int32, (span, TILE), 0)
                 row_pos = lax.broadcasted_iota(jnp.int32, (span, TILE), 1) + (r * TILE) % half
                 scores = jnp.where(key_pos <= row_pos + task * half, scores, neg_fill)
@@ -83,11 +87,19 @@
             acc_ref[:, cols] = acc_ref[:, cols] * factor + jnp.dot(
                 values_t, weights.astype(jnp.bfloat16), preferred_element_type=jnp.float32
             )
+            if not last:
+                s_ref[:, cols] = following
 
     def one_task(t, _):
         m_ref[...] = jnp.full_like(m_ref, neg_fill)
         l_ref[...] = jnp.zeros_like(l_ref)
         acc_ref[...] = jnp.zeros_like(acc_ref)
+
+        @pl.when((diag[t] > 0) | (lo[t] < hi[t]))
+        def _():
+            keys = keys_twice(lo[t])
+            for cols in tiles:
+                s_ref[:, cols] = scores_of(keys, t, cols)
 
         def body(at_span, _):
             step(t, at_span, False)
@@ -128,6 +140,7 @@
         out_specs=(vmem, vmem),
         scratch_shapes=[
             pltpu.VMEM((16,) + pieces[0].shape, jnp.bfloat16),
+            pltpu.VMEM((pieces[0].shape[0] // 2, rows), jnp.float32),
             pltpu.VMEM((1, rows), jnp.float32),
             pltpu.VMEM((1, rows), jnp.float32),
             pltpu.VMEM((HD, rows), jnp.float32),
@@ -140,6 +153,41 @@
     )(lo, hi, diag, slots, q, *pieces)
 
 
+def project_kernel(at, low_ref, high_ref, *refs):
+    weights, (keep, out_z, out_c, out_cz, acc) = refs[:8], refs[8:]
+    acc[...] = jnp.dot(
+        jnp.concatenate([low_ref[...], high_ref[...]], axis=1),
+        jnp.concatenate([w[...] for w in weights[::2] + weights[1::2]], axis=0),
+        preferred_element_type=jnp.float32,
+    )
+    count = acc.shape[0] // 4
+    block = lambda i: acc[pl.ds(pl.multiple_of(at[i] * count, count), count), :]
+    keep[...] = block(0)
+    out_z[...] = block(1).astype(jnp.bfloat16)
+    out_c[...] = block(2).astype(jnp.bfloat16)
+    out_cz[...] = block(3).astype(jnp.bfloat16)
+
+
+def project(at, low, high, *weights):
+    rows, width = low.shape[0], weights[0].shape[1]
+    tile = 384
+    whole = pl.BlockSpec(low.shape, lambda n: (0, 0))
+    weight = pl.BlockSpec((PAIR, tile), lambda n: (0, n))
+    out = pl.BlockSpec((rows // 4, tile), lambda n: (0, n))
+    sent = jax.ShapeDtypeStruct((rows // 4, width), jnp.bfloat16)
+    return pl.pallas_call(
+        project_kernel,
+        grid=(width // tile,),
+        out_shape=(jax.ShapeDtypeStruct((rows // 4, width), jnp.float32), sent, sent, sent),
+        in_specs=[pl.BlockSpec(memory_space=pltpu.SMEM), whole, whole] + [weight] * 8,
+        out_specs=(out,) * 4,
+        scratch_shapes=[pltpu.VMEM((rows, tile), jnp.float32)],
+        cost_estimate=pl.CostEstimate(
+            flops=rows * 2048 * width * 2, bytes_accessed=12_000_000, transcendentals=0
+        ),
+    )(at, low, high, *weights)
+
+
 def packed_queries(q):
     tokens = q.shape[0]
     scaled = q.astype(jnp.float32) * query_scale
@@ -198,28 +246,40 @@
     y_down = lambda a: moved(a, "y", lambda at: (at[0] - 1,))
     z_up = lambda a: moved(a, "zh", lambda at: (at[0] + 1,))
     z_down = lambda a: moved(a, "zh", lambda at: (at[0] - 1,))
-    own_kv = kv_own
+    own_kv, out_weight = lax.optimization_barrier((kv_own, out_weight))
+    size = own_kv.shape[0] // 2
     z1, z3 = z_up(own_kv), z_down(own_kv)
     y1, y3 = y_up(own_kv), y_down(own_kv)
-    mirror = lambda at: (spans_y - 1 - at[0], spans_z - 1 - at[1])
-    lent = moved(second[:, :PAIR], ("y", "zh"), mirror)
+    x_up = lambda a: moved(a, "x", lambda at: (at[0] + 1,))
+    x_down = lambda a: moved(a, "x", lambda at: (at[0] - 1,))
     own_w = lax.dynamic_slice_in_dim(out_weight, core * half_width, half_width, 1)
-    part = own_w.shape[0] // 2
-    w_left = moved(own_w, "x", lambda at: (at[0] + 1,))
-    w_right = moved(own_w, "x", lambda at: (at[0] - 1,))
-
-    size = own_kv.shape[0] // 2
-    pieces = [own_kv, y1, y3, y_up(y1[:size]), y_down(y3[size:])]
-    z2 = jnp.concatenate([z_up(z1[:size]), z_down(z3[size:])], axis=0)
+    w0 = (own_w[:PAIR], own_w[PAIR:])
+    w1_top, w3_low = x_up(w0[0]), x_down(w0[1])
+    w1_low, w3_top = x_up(w0[1]), x_down(w0[0])
+
+    y2 = [y_up(y1[:size]), y_down(y3[size:])]
+    y2 = jnp.concatenate(y2, axis=0)
+    z1, z3, y1, y3, y2, lending = lax.optimization_barrier(
+        (z1, z3, y1, y3, y2, second[:, :PAIR])
+    )
     z1_up, z1_down = y_up(z1), y_down(z1)
     z3_up, z3_down = y_up(z3), y_down(z3)
-    pieces += [z1, z1_up, z1_down, y_up(z1_up)]
-    pieces += [z3, z3_up, z3_down, y_down(z3_down)]
+    z2 = [z_up(z1[:size]), z_down(z3[size:])]
+    z2 = jnp.concatenate(z2, axis=0)
+    mirror = lambda at: (spans_y - 1 - at[0], spans_z - 1 - at[1])
+    lent = moved(lending, ("y", "zh"), mirror)
+    z2, y2 = lax.optimization_barrier((z2, y2))
     z2_up, z2_down = y_up(z2), y_down(z2)
+    z1_far, z3_far = z_up(y2), z_down(y2)
+    pieces = [own_kv, y1, y3, y2]
+    pieces += [z1, z1_up, z1_down, z1_far]
+    pieces += [z3, z3_up, z3_down, z3_far]
     pieces += [z2, z2_up, z2_down, y_up(z2_up[:size]), y_down(z2_down[size:])]
-    w_left, w_right, *_ = lax.optimization_barrier((w_left, w_right, z1_up, z1_down, z3_up, z3_down))
-    w_far_top = moved(w_left[:part], "x", lambda at: (at[0] + 1,))
-    w_far_low = moved(w_right[part:], "x", lambda at: (at[0] - 1,))
+    w1_top, w3_low, *_ = lax.optimization_barrier(
+        (w1_top, w3_low, z1_up, z1_down, z3_up, z3_down)
+    )
+    w2_top = x_up(w1_top)
+    w2_low = x_down(w3_low)
 
     lent_len = jnp.maximum(2 * span - (spans - 1), 0)
     taken_len = jnp.maximum(spans - 1 - 2 * span, 0)
@@ -258,25 +318,16 @@
 
     heads_mine = jnp.concatenate([towards(k) for k in range(groups)], axis=1)
     heads_other = moved(heads_mine, "c", lambda at: (1 - at[0],))
-    of_core = [jnp.where(core == 0, heads_mine, heads_other), jnp.where(core == 0, heads_other, heads_mine)]
-    w_terms = [own_w, w_left, jnp.concatenate([w_far_top, w_far_low], axis=0), w_right]
-    partial = 0.0
-    for k in range(groups):
-        lhs = jnp.concatenate([half[:, k * PAIR : (k + 1) * PAIR] for half in of_core], axis=1)
-        partial = partial + jnp.dot(lhs, w_terms[k], preferred_element_type=jnp.float32)
-
-    partial = partial.reshape(2, 2, piece // 2, half_width)
-
-    def block_of(c_at, z_at):
-        return lax.dynamic_slice(partial, (c_at, z_at, 0, 0), (1, 1, piece // 2, half_width))[0, 0]
-
-    send_z = block_of(core, 1 - zl).astype(jnp.bfloat16)
-    send_c = block_of(1 - core, zl).astype(jnp.bfloat16)
-    send_cz = block_of(1 - core, 1 - zl).astype(jnp.bfloat16)
+    low = jnp.where(core == 0, heads_mine, heads_other)
+    high = jnp.where(core == 0, heads_other, heads_mine)
+    blocks = ints(core * 2 + zl, core * 2 + 1 - zl, 2 - core * 2 + zl, 2 - core * 2 + 1 - zl)
+    keep, send_z, send_c, send_cz = project(
+        blocks, low, high, *w0, w1_top, w1_low, w2_top, w2_low, w3_top, w3_low
+    )
     got_z = moved(send_z, "zl", lambda at: (1 - at[0],))
     got_cz = moved(send_cz, ("c", "zl"), lambda at: (1 - at[0], 1 - at[1]))
     got_c = moved(send_c, "c", lambda at: (1 - at[0],))
-    mine_cols = (block_of(core, zl) + got_z.astype(jnp.float32)).astype(jnp.bfloat16)
+    mine_cols = (keep + got_z.astype(jnp.float32)).astype(jnp.bfloat16)
     other_cols = (got_c.astype(jnp.float32) + got_cz.astype(jnp.float32)).astype(jnp.bfloat16)
     return jnp.where(
         core == 0,

time: 248 us -> 222 us (0.90); the launches traced: 244 us -> 221 us
  waiting for transfers between devices: 88.1 us -> 70 us
  matrix products: 9.08 us -> 0 us
  Pallas kernels: 32.2 us -> 39 us
  local copies, waits for them, and re-layouts: 33.6 us -> 29.3 us
  other arithmetic: 10.5 us -> 14.3 us
    ppermute x33 -> x35, waiting for transfers between devices: 88.1 us -> 70 us  [moved(): return lax.ppermute(value, axes, pairs)]
    pallas_call x0 -> x1, Pallas kernels: none -> 10.2 us  [project(): pl.pallas_call(project_kernel, grid=(width // tile,), out_shape=(jax.Shap...]
    dot_general x4 -> x0, matrix products: 9.08 us -> none  [layer(): jnp.dot(lhs, w_terms[k], preferred_element_type=jnp.float32)]
    dynamic_slice x1 -> x0, local copies, waits for them, and re-layouts: 3.48 us -> none  [layer(): lax.dynamic_slice_in_dim(out_weight, core * half_width, half_width, 1)]
    pallas_call x1, Pallas kernels: 32.2 us -> 28.8 us  [attend(): pl.pallas_call(attend_kernel, out_shape=(jax.ShapeDtypeStruct((tasks, row...]
    concatenate x0 -> x2, other arithmetic: none -> 2.95 us  [the longest x1 1.88 us: layer(): z2 = jnp.concatenate(z2, axis=0)]
    ppermute x33 -> x35, starting transfers between devices: 70.3 us -> 68.4 us  [moved(): return lax.ppermute(value, axes, pairs)]
    unnamed x16 -> x27, local copies, waits for them, and re-layouts: 5.65 us -> 5.1 us
  transfers between devices with their start and end apart: 33 -> 35, of which waited for: 15 -> 17; matrix products, arithmetic and copies ran while one was open for 18% -> 17% of each run, Pallas kernels for 13% -> 13%
where the time goes in v1:
time: 222 us; the launch traced here: 221 us
  waiting for transfers between devices  70 us (32%)
  starting transfers between devices  68.4 us (31%)
  Pallas kernels  39 us (18%)
  local copies, waits for them, and re-layouts  29.3 us (13%)
  other arithmetic  14.3 us (6%)
    ppermute x35, waiting for transfers between devices, moved(): return lax.ppermute(value, axes, pairs)  70 us
    ppermute x35, starting transfers between devices, moved(): return lax.ppermute(value, axes, pairs)  68.4 us
    pallas_call x1, Pallas kernels, attend(): pl.pallas_call(attend_kernel, out_shape=(jax.ShapeDtypeStruct((tasks, row...  28.8 us
    pallas_call x1, Pallas kernels, project(): pl.pallas_call(project_kernel, grid=(width // tile,), out_shape=(jax.Shap...  10.2 us
    reshape x3, local copies, waits for them, and re-layouts, packed_queries(): scaled.reshape(tokens, 2, HD).transpose(2, 1, 0).reshape(HD, 2 * tokens)  6.31 us
    transpose x3, local copies, waits for them, and re-layouts, packed_queries(): scaled.reshape(tokens, 2, HD).transpose(2, 1, 0).reshape(HD, 2 * tokens)  5.8 us
    unnamed x27, local copies, waits for them, and re-layouts  5.1 us
  transfers between devices with their start and end apart: 35, of which 17 were waited for; matrix products, arithmetic and copies ran while one was open for 17% of the time, Pallas kernels for 13%

profile of v1, /device:TPU:1, one launch (start us, length us, event | category | flops | bytes accessed | tf_op | source)
XLA Modules:
  0.0 221.3 jit_solution(9496792726796923586)
XLA Ops:
  0.0 1.1 constant_dynamic-slice_fusion.6
  1.1 1.1 constant_dynamic-slice_fusion.4
  2.3 3.3 %collective-permute-start = (bf16[512,512]{1,0:T(8,128)(2,1)S(1)}, bf16[512,512]{1,0:T(8,128)(2,1)S(1)}, u32[]{:S(2)}, u32[]{:S(2)}) collective-permute-start(bf16[512,512]{1,0:T(8,128)(2,1)S(1)} %pad_maximum_fusion.1), channel_id=1, source_target_pairs={{0,8},{8,0},{1,9},{9,1},{2,10},{10,2},{3,11},{11,3},{4,12},{12,4},... | collective-permute-start | bytes 1572872 | tf_op jit(solution)/shard_map/ppermute | solution.py:39
  5.6 1.5 collective-permute-done
  8.5 1.1 collective-permute-start.4
  10.1 5.6 %collective-permute-start.2 = (bf16[2048,128]{1,0:T(8,128)(2,1)S(1)}, bf16[2048,128]{1,0:T(8,128)(2,1)S(1)}, u32[]{:S(2)}, u32[]{:S(2)}) collective-permute-start(bf16[2048,128]{1,0:T(8,128)(2,1)S(1)} %pad_maximum_fusion.2.refs_0_), channel_id=1, source_target_pairs={{0,48},{16,0},{32,16},{48,32},{1,49},{17,1},{33,17},{49,33},{2,50}... | collective-permute-start | bytes 1572872 | tf_op jit(solution)/shard_map/ppermute | solution.py:39
  15.7 6.1 %collective-permute-done.4.refs_2_ = bf16[2048,128]{1,0:T(8,128)(2,1)S(1)} collective-permute-done((bf16[2048,128]{1,0:T(8,128)(2,1)S(1)}, bf16[2048,128]{1,0:T(8,128)(2,1)S(1)}, u32[]{:S(2)}, u32[]{:S(2)}) %collective-permute-start.4) | collective-permute-done | bytes 524320 | tf_op jit(solution)/shard_map/ppermute | solution.py:39
  21.7 2.3 %collective-permute-start.6 = (bf16[1024,128]{1,0:T(8,128)(2,1)S(1)}, bf16[1024,128]{1,0:T(8,128)(2,1)}, u32[]{:S(2)}, u32[]{:S(2)}) collective-permute-start(bf16[1024,128]{1,0:T(8,128)(2,1)S(1)} %slice.85), channel_id=1, source_target_pairs={{0,192},{64,0},{128,64},{192,128},{1,193},{65,1},{129,65},{193,129... | collective-permute-start | bytes 786440 | tf_op jit(solution)/shard_map/ppermute | solution.py:39
  25.6 2.9 %collective-permute-done.6 = bf16[1024,128]{1,0:T(8,128)(2,1)} collective-permute-done((bf16[1024,128]{1,0:T(8,128)(2,1)S(1)}, bf16[1024,128]{1,0:T(8,128)(2,1)}, u32[]{:S(2)}, u32[]{:S(2)}) %collective-permute-start.6) | collective-permute-done | bytes 262176 | tf_op jit(solution)/shard_map/ppermute | solution.py:39
  28.6 4.1 %collective-permute-done.5 = bf16[1024,128]{1,0:T(8,128)(2,1)} collective-permute-done((bf16[1024,128]{1,0:T(8,128)(2,1)}, bf16[1024,128]{1,0:T(8,128)(2,1)}, u32[]{:S(2)}, u32[]{:S(2)}) %collective-permute-start.5) | collective-permute-done | bytes 262176 | tf_op jit(solution)/shard_map/ppermute | solution.py:39
  32.7 1.1 pad_maximum_fusion.3.refs_3_
  33.7 1.9 collective-permute-done.2.refs_8_
  35.7 2.6 %collective-permute-start.11 = (bf16[2048,128]{1,0:T(8,128)(2,1)S(1)}, bf16[2048,128]{1,0:T(8,128)(2,1)}, u32[]{:S(2)}, u32[]{:S(2)}) collective-permute-start(bf16[2048,128]{1,0:T(8,128)(2,1)S(1)} %collective-permute-done.1.refs_4_), channel_id=1, source_target_pairs={{0,192},{64,0},{128,64},{192,128},{1,193},{65,1},{129,65},{193,129... | collective-permute-start | bytes 1572872 | tf_op jit(solution)/shard_map/ppermute | solution.py:39
  38.2 5.7 %collective-permute-start.9 = (bf16[1024,128]{1,0:T(8,128)(2,1)S(1)}, bf16[1024,128]{1,0:T(8,128)(2,1)S(1)}, u32[]{:S(2)}, u32[]{:S(2)}) collective-permute-start(bf16[1024,128]{1,0:T(8,128)(2,1)S(1)} %slice.68), channel_id=1, source_target_pairs={{0,48},{16,0},{32,16},{48,32},{1,49},{17,1},{33,17},{49,33},{2,50}... | collective-permute-start | bytes 786440 | tf_op jit(solution)/shard_map/ppermute | solution.py:39
  43.9 3.5 %fusion.24 = (bf16[256,2688]{1,0:T(8,128)(2,1)}, bf16[256,2688]{1,0:T(8,128)(2,1)}) fusion(bf16[512,5376]{1,0:T(8,128)(2,1)} %param.7, s32[]{:T(128)S(6)} %add.141, s32[]{:T(128)S(6)} %select_n.139), kind=kLoop, calls=%fused_computation.83 | loop fusion | bytes 5505032 | tf_op jit(solution)/shard_map/slice | solution.py:256
  47.4 2.5 %collective-permute-start.27 = (bf16[256,2688]{1,0:T(8,128)(2,1)}, bf16[256,2688]{1,0:T(8,128)(2,1)}, u32[]{:S(2)}, u32[]{:S(2)}) collective-permute-start(bf16[256,2688]{1,0:T(8,128)(2,1)} %get-tuple-element.41.refs_1_), channel_id=1, source_target_pairs={{0,6},{2,0},{4,2},{6,4},{1,7},{3,1},{5,3},{7,5},{8,14},{10,8},{12,... | collective-permute-start | bytes 4128776 | tf_op jit(solution)/shard_map/ppermute | solution.py:39
  49.9 1.5 collective-permute-done.9
  52.1 3.2 %collective-permute-start.7 = (bf16[512,256]{1,0:T(8,128)(2,1)}, bf16[512,256]{1,0:T(8,128)(2,1)S(1)}, u32[]{:S(2)}, u32[]{:S(2)}) collective-permute-start(bf16[512,256]{1,0:T(8,128)(2,1)} %slice.79), channel_id=1, source_target_pairs={{0,240},{16,224},{32,208},{48,192},{64,176},{80,160},{96,144},{112... | collective-permute-start | bytes 786440 | tf_op jit(solution)/shard_map/ppermute | solution.py:39
  56.2 2.1 reshape.147
  58.3 1.9 copy.5
  60.2 1.2 copy.13
  61.4 1.9 pad_maximum_fusion.4.refs_12_
  63.3 2.3 %collective-permute-done.7 = bf16[512,256]{1,0:T(8,128)(2,1)S(1)} collective-permute-done((bf16[512,256]{1,0:T(8,128)(2,1)}, bf16[512,256]{1,0:T(8,128)(2,1)S(1)}, u32[]{:S(2)}, u32[]{:S(2)}) %collective-permute-start.7) | collective-permute-done | bytes 262176 | tf_op jit(solution)/shard_map/ppermute | solution.py:39
  65.5 1.2 collective-permute-start.26
  66.8 6.3 %collective-permute-start.17 = (bf16[2048,128]{1,0:T(8,128)(2,1)}, bf16[2048,128]{1,0:T(8,128)(2,1)}, u32[]{:S(2)}, u32[]{:S(2)}) collective-permute-start(bf16[2048,128]{1,0:T(8,128)(2,1)} %pad_maximum_fusion.4.refs_12_), channel_id=1, source_target_pairs={{0,192},{64,0},{128,64},{192,128},{1,193},{65,1},{129,65},{193,129... | collective-permute-start | bytes 1572872 | tf_op jit(solution)/shard_map/ppermute | solution.py:39
  74.2 1.4 collective-permute-start.13
  76.4 2.1 reshape.149
  78.5 1.9 copy.6
  80.4 1.2 copy.14
  82.9 5.7 %collective-permute-start.15 = (bf16[2048,128]{1,0:T(8,128)(2,1)S(1)}, bf16[2048,128]{1,0:T(8,128)(2,1)}, u32[]{:S(2)}, u32[]{:S(2)}) collective-permute-start(bf16[2048,128]{1,0:T(8,128)(2,1)S(1)} %pad_maximum_fusion.3.refs_3_), channel_id=1, source_target_pairs={{0,48},{16,0},{32,16},{48,32},{1,49},{17,1},{33,17},{49,33},{2,50}... | collective-permute-start | bytes 1572872 | tf_op jit(solution)/shard_map/ppermute | solution.py:39
  89.4 2.1 reshape.155
  91.5 1.9 copy.9
  93.4 1.2 copy.15
  94.6 1.0 slice.87
  95.6 1.0 slice.86
  96.6 1.3 collective-permute-start.19
  97.9 1.2 collective-permute-start.18
  99.2 1.3 maximum_maximum_fusion.q_ref
  100.5 1.2 collective-permute-start.28
  101.8 7.4 %collective-permute-done.15.refs_11_ = bf16[2048,128]{1,0:T(8,128)(2,1)} collective-permute-done((bf16[2048,128]{1,0:T(8,128)(2,1)S(1)}, bf16[2048,128]{1,0:T(8,128)(2,1)}, u32[]{:S(2)}, u32[]{:S(2)}) %collective-permute-start.15) | collective-permute-done | bytes 524320 | tf_op jit(solution)/shard_map/ppermute | solution.py:39
  109.2 1.5 collective-permute-start.29
  110.6 2.7 %collective-permute-start.30 = (bf16[256,2688]{1,0:T(8,128)(2,1)}, bf16[256,2688]{1,0:T(8,128)(2,1)}, u32[]{:S(2)}, u32[]{:S(2)}) collective-permute-start(bf16[256,2688]{1,0:T(8,128)(2,1)} %collective-permute-done.27.refs_7_), channel_id=1, source_target_pairs={{0,6},{2,0},{4,2},{6,4},{1,7},{3,1},{5,3},{7,5},{8,14},{10,8},{12,... | collective-permute-start | bytes 4128776 | tf_op jit(solution)/shard_map/ppermute | solution.py:39
  113.4 28.8 %shard_map.46 = (bf16[3,512,256]{2,1,0:T(8,128)(2,1)}, f32[3,1,1024]{2,1,0:T(1,128)S(1)}) custom-call(s32[3]{0:T(128)S(1)} %get-tuple-element.73.lo, s32[3]{0:T(128)S(1)} %get-tuple-element.74.hi, s32[3]{0:T(128)S(1)} %copy-done, s32[16]{0:T(128)S(1)} %fusion.19.slots, bf16[3,256,1024]{2,1,0:T(8,128)(2,1)} %maximum_maximum_fusion.q_ref, ...), custom_call_target="tpu_custom_call" | custom-call | flops 8589934592 | bytes 9000000 | tf_op jit(solution)/shard_map/pallas_call | solution.py:133
  142.2 2.6 %collective-permute-start.20 = (f32[1,1024]{1,0:T(1,128)S(1)}, f32[1,1024]{1,0:T(1,128)S(1)}, u32[]{:S(2)}, u32[]{:S(2)}) collective-permute-start(f32[1,1024]{1,0:T(1,128)S(1)} %get-tuple-element.70), channel_id=1, source_target_pairs={{0,240},{16,224},{32,208},{48,192},{64,176},{80,160},{96,144},{112... | collective-permute-start | bytes 12296 | tf_op jit(solution)/shard_map/ppermute | solution.py:39
  144.8 1.1 fusion.25
  145.9 3.1 %collective-permute-done.20 = f32[1,1024]{1,0:T(1,128)S(1)} collective-permute-done((f32[1,1024]{1,0:T(1,128)S(1)}, f32[1,1024]{1,0:T(1,128)S(1)}, u32[]{:S(2)}, u32[]{:S(2)}) %collective-permute-start.20) | collective-permute-done | bytes 4128 | tf_op jit(solution)/shard_map/ppermute | solution.py:39
  148.9 2.5 %collective-permute-start.21 = (bf16[512,256]{1,0:T(8,128)(2,1)S(1)}, bf16[512,256]{1,0:T(8,128)(2,1)S(1)}, u32[]{:S(2)}, u32[]{:S(2)}) collective-permute-start(bf16[512,256]{1,0:T(8,128)(2,1)S(1)} %get-tuple-element.48), channel_id=1, source_target_pairs={{0,240},{16,224},{32,208},{48,192},{64,176},{80,160},{96,144},{112... | collective-permute-start | bytes 786440 | tf_op jit(solution)/shard_map/ppermute | solution.py:39
  151.8 6.7 %collective-permute-done.21 = bf16[512,256]{1,0:T(8,128)(2,1)S(1)} collective-permute-done((bf16[512,256]{1,0:T(8,128)(2,1)S(1)}, bf16[512,256]{1,0:T(8,128)(2,1)S(1)}, u32[]{:S(2)}, u32[]{:S(2)}) %collective-permute-start.21) | collective-permute-done | bytes 262176 | tf_op jit(solution)/shard_map/ppermute | solution.py:39
  159.7 1.1 fusion.4
  160.9 1.5 collective-permute-start.24
  162.4 8.3 %collective-permute-done.24 = bf16[256,256]{1,0:T(8,128)(2,1)S(1)} collective-permute-done((bf16[256,256]{1,0:T(8,128)(2,1)S(1)}, bf16[256,256]{1,0:T(8,128)(2,1)S(1)}, u32[]{:S(2)}, u32[]{:S(2)}) %collective-permute-start.24) | collective-permute-done | bytes 131104 | tf_op jit(solution)/shard_map/ppermute | solution.py:39
  170.8 1.8 collective-permute-start.23
  172.6 3.5 %collective-permute-done.23 = bf16[256,256]{1,0:T(8,128)(2,1)S(1)} collective-permute-done((bf16[256,256]{1,0:T(8,128)(2,1)S(1)}, bf16[256,256]{1,0:T(8,128)(2,1)S(1)}, u32[]{:S(2)}, u32[]{:S(2)}) %collective-permute-start.23) | collective-permute-done | bytes 131104 | tf_op jit(solution)/shard_map/ppermute | solution.py:39
  176.1 1.2 collective-permute-start.22
  177.3 5.2 %collective-permute-done.22 = bf16[256,256]{1,0:T(8,128)(2,1)S(1)} collective-permute-done((bf16[256,256]{1,0:T(8,128)(2,1)S(1)}, bf16[256,256]{1,0:T(8,128)(2,1)S(1)}, u32[]{:S(2)}, u32[]{:S(2)}) %collective-permute-start.22) | collective-permute-done | bytes 131104 | tf_op jit(solution)/shard_map/ppermute | solution.py:39
  182.5 7.2 %collective-permute-start.25 = (bf16[256,1024]{1,0:T(8,128)(2,1)S(1)}, bf16[256,1024]{1,0:T(8,128)(2,1)S(1)}, u32[]{:S(2)}, u32[]{:S(2)}) collective-permute-start(bf16[256,1024]{1,0:T(8,128)(2,1)S(1)} %pad_maximum_fusion.5), channel_id=1, source_target_pairs={{0,8},{8,0},{1,9},{9,1},{2,10},{10,2},{3,11},{11,3},{4,12},{12,4},... | collective-permute-start | bytes 1572872 | tf_op jit(solution)/shard_map/ppermute | solution.py:39
  190.3 1.0 collective-permute-done.25
  191.2 1.3 broadcast_select_fusion.2
  192.5 10.2 %shard_map.47 = (f32[64,2688]{1,0:T(8,128)}, bf16[64,2688]{1,0:T(8,128)(2,1)}, bf16[64,2688]{1,0:T(8,128)(2,1)}, bf16[64,2688]{1,0:T(8,128)(2,1)}) custom-call(s32[4]{0:T(128)} %pad_add_fusion.at, bf16[256,1024]{1,0:T(8,128)(2,1)} %get-tuple-element.44.low_ref, bf16[256,1024]{1,0:T(8,128)(2,1)} %get-tuple-element.43.high_ref, ...), custom_call_target="tpu_custom_call" | custom-call | flops 2818572288 | bytes 12000000 | tf_op jit(solution)/shard_map/pallas_call | solution.py:178
  203.3 1.5 collective-permute-start.34
  204.8 7.5 %collective-permute-done.32 = bf16[64,2688]{1,0:T(8,128)(2,1)S(1)} collective-permute-done((bf16[64,2688]{1,0:T(8,128)(2,1)}, bf16[64,2688]{1,0:T(8,128)(2,1)S(1)}, u32[]{:S(2)}, u32[]{:S(2)}) %collective-permute-start.32) | collective-permute-done | bytes 344096 | tf_op jit(solution)/shard_map/ppermute | solution.py:39
  212.3 1.2 add_convert_fusion.1
  213.5 6.7 %collective-permute-done.34 = bf16[64,2688]{1,0:T(8,128)(2,1)S(1)} collective-permute-done((bf16[64,2688]{1,0:T(8,128)(2,1)}, bf16[64,2688]{1,0:T(8,128)(2,1)S(1)}, u32[]{:S(2)}, u32[]{:S(2)}) %collective-permute-start.34) | collective-permute-done | bytes 344096 | tf_op jit(solution)/shard_map/ppermute | solution.py:39
  220.3 1.0 maximum_select_fusion
  (89 shorter events, 12.2 us)
Async XLA Ops:
  2.3 4.8 %collective-permute-start = (bf16[512,512]{1,0:T(8,128)(2,1)S(1)}, bf16[512,512]{1,0:T(8,128)(2,1)S(1)}, u32[]{:S(2)}, u32[]{:S(2)}) collective-permute-start(bf16[512,512]{1,0:T(8,128)(2,1)S(1)} %pad_maximum_fusion.1), channel_id=1, source_target_pairs={{0,8},{8,0},{1,9},{9,1},{2,10},{10,2},{3,11},{11,3},{4,12},{12,4},... | collective-permute-start | bytes 1572872 | tf_op jit(solution)/shard_map/ppermute | solution.py:39
  7.4 0.8 copy-start.3
  7.4 17.5 %copy-start.1 = (bf16[512,512]{1,0:T(8,128)(2,1)}, bf16[512,512]{1,0:T(8,128)(2,1)S(1)}, u32[]{:S(2)}) copy-start(bf16[512,512]{1,0:T(8,128)(2,1)S(1)} %get-tuple-element.46) | copy-start | bytes 1572868
  8.5 13.2 %collective-permute-start.4 = (bf16[2048,128]{1,0:T(8,128)(2,1)S(1)}, bf16[2048,128]{1,0:T(8,128)(2,1)S(1)}, u32[]{:S(2)}, u32[]{:S(2)}) collective-permute-start(bf16[2048,128]{1,0:T(8,128)(2,1)S(1)} %pad_maximum_fusion.2.refs_0_), channel_id=1, source_target_pairs={{0,192},{64,0},{128,64},{192,128},{1,193},{65,1},{129,65},{193,129... | collective-permute-start | bytes 1572872 | tf_op jit(solution)/shard_map/ppermute | solution.py:39
  9.6 14.4 %collective-permute-start.3 = (bf16[2048,128]{1,0:T(8,128)(2,1)S(1)}, bf16[2048,128]{1,0:T(8,128)(2,1)S(1)}, u32[]{:S(2)}, u32[]{:S(2)}) collective-permute-start(bf16[2048,128]{1,0:T(8,128)(2,1)S(1)} %pad_maximum_fusion.2.refs_0_), channel_id=1, source_target_pairs={{0,64},{64,128},{128,192},{192,0},{1,65},{65,129},{129,193},{193,1... | collective-permute-start | bytes 1572872 | tf_op jit(solution)/shard_map/ppermute | solution.py:39
  10.1 25.6 %collective-permute-start.2 = (bf16[2048,128]{1,0:T(8,128)(2,1)S(1)}, bf16[2048,128]{1,0:T(8,128)(2,1)S(1)}, u32[]{:S(2)}, u32[]{:S(2)}) collective-permute-start(bf16[2048,128]{1,0:T(8,128)(2,1)S(1)} %pad_maximum_fusion.2.refs_0_), channel_id=1, source_target_pairs={{0,48},{16,0},{32,16},{48,32},{1,49},{17,1},{33,17},{49,33},{2,50}... | collective-permute-start | bytes 1572872 | tf_op jit(solution)/shard_map/ppermute | solution.py:39
  15.7 20.0 %collective-permute-start.1 = (bf16[2048,128]{1,0:T(8,128)(2,1)S(1)}, bf16[2048,128]{1,0:T(8,128)(2,1)S(1)}, u32[]{:S(2)}, u32[]{:S(2)}) collective-permute-start(bf16[2048,128]{1,0:T(8,128)(2,1)S(1)} %pad_maximum_fusion.2.refs_0_), channel_id=1, source_target_pairs={{0,16},{16,32},{32,48},{48,0},{1,17},{17,33},{33,49},{49,1},{2,18}... | collective-permute-start | bytes 1572872 | tf_op jit(solution)/shard_map/ppermute | solution.py:39
  21.7 6.8 %collective-permute-start.6 = (bf16[1024,128]{1,0:T(8,128)(2,1)S(1)}, bf16[1024,128]{1,0:T(8,128)(2,1)}, u32[]{:S(2)}, u32[]{:S(2)}) collective-permute-start(bf16[1024,128]{1,0:T(8,128)(2,1)S(1)} %slice.85), channel_id=1, source_target_pairs={{0,192},{64,0},{128,64},{192,128},{1,193},{65,1},{129,65},{193,129... | collective-permute-start | bytes 786440 | tf_op jit(solution)/shard_map/ppermute | solution.py:39
  24.8 7.9 %collective-permute-start.5 = (bf16[1024,128]{1,0:T(8,128)(2,1)}, bf16[1024,128]{1,0:T(8,128)(2,1)}, u32[]{:S(2)}, u32[]{:S(2)}) collective-permute-start(bf16[1024,128]{1,0:T(8,128)(2,1)} %slice.84), channel_id=1, source_target_pairs={{0,64},{64,128},{128,192},{192,0},{1,65},{65,129},{129,193},{193,1... | collective-permute-start | bytes 786440 | tf_op jit(solution)/shard_map/ppermute | solution.py:39
  35.7 31.1 %collective-permute-start.11 = (bf16[2048,128]{1,0:T(8,128)(2,1)S(1)}, bf16[2048,128]{1,0:T(8,128)(2,1)}, u32[]{:S(2)}, u32[]{:S(2)}) collective-permute-start(bf16[2048,128]{1,0:T(8,128)(2,1)S(1)} %collective-permute-done.1.refs_4_), channel_id=1, source_target_pairs={{0,192},{64,0},{128,64},{192,128},{1,193},{65,1},{129,65},{193,129... | collective-permute-start | bytes 1572872 | tf_op jit(solution)/shard_map/ppermute | solution.py:39
  38.2 34.8 %collective-permute-start.10 = (bf16[2048,128]{1,0:T(8,128)(2,1)S(1)}, bf16[2048,128]{1,0:T(8,128)(2,1)}, u32[]{:S(2)}, u32[]{:S(2)}) collective-permute-start(bf16[2048,128]{1,0:T(8,128)(2,1)S(1)} %collective-permute-done.1.refs_4_), channel_id=1, source_target_pairs={{0,64},{64,128},{128,192},{192,0},{1,65},{65,129},{129,193},{193,1... | collective-permute-start | bytes 1572872 | tf_op jit(solution)/shard_map/ppermute | solution.py:39
  38.2 17.1 %copy-start.4 = (bf16[512,512]{1,0:T(8,128)(2,1)S(1)}, bf16[512,512]{1,0:T(8,128)(2,1)}, u32[]{:S(2)}) copy-start(bf16[512,512]{1,0:T(8,128)(2,1)} %copy-done.3) | copy-start | bytes 1572868
  38.2 13.1 %collective-permute-start.9 = (bf16[1024,128]{1,0:T(8,128)(2,1)S(1)}, bf16[1024,128]{1,0:T(8,128)(2,1)S(1)}, u32[]{:S(2)}, u32[]{:S(2)}) collective-permute-start(bf16[1024,128]{1,0:T(8,128)(2,1)S(1)} %slice.68), channel_id=1, source_target_pairs={{0,48},{16,0},{32,16},{48,32},{1,49},{17,1},{33,17},{49,33},{2,50}... | collective-permute-start | bytes 786440 | tf_op jit(solution)/shard_map/ppermute | solution.py:39
  43.9 7.5 %collective-permute-start.8 = (bf16[1024,128]{1,0:T(8,128)(2,1)S(1)}, bf16[1024,128]{1,0:T(8,128)(2,1)S(1)}, u32[]{:S(2)}, u32[]{:S(2)}) collective-permute-start(bf16[1024,128]{1,0:T(8,128)(2,1)S(1)} %slice.67), channel_id=1, source_target_pairs={{0,16},{16,32},{32,48},{48,0},{1,17},{17,33},{33,49},{49,1},{2,18}... | collective-permute-start | bytes 786440 | tf_op jit(solution)/shard_map/ppermute | solution.py:39
  47.4 50.4 %collective-permute-start.27 = (bf16[256,2688]{1,0:T(8,128)(2,1)}, bf16[256,2688]{1,0:T(8,128)(2,1)}, u32[]{:S(2)}, u32[]{:S(2)}) collective-permute-start(bf16[256,2688]{1,0:T(8,128)(2,1)} %get-tuple-element.41.refs_1_), channel_id=1, source_target_pairs={{0,6},{2,0},{4,2},{6,4},{1,7},{3,1},{5,3},{7,5},{8,14},{10,8},{12,... | collective-permute-start | bytes 4128776 | tf_op jit(solution)/shard_map/ppermute | solution.py:39
  51.4 0.7 copy-start.10
  51.4 22.8 %collective-permute-start.14 = (bf16[2048,128]{1,0:T(8,128)(2,1)S(1)}, bf16[2048,128]{1,0:T(8,128)(2,1)}, u32[]{:S(2)}, u32[]{:S(2)}) collective-permute-start(bf16[2048,128]{1,0:T(8,128)(2,1)S(1)} %collective-permute-done.2.refs_8_), channel_id=1, source_target_pairs={{0,192},{64,0},{128,64},{192,128},{1,193},{65,1},{129,65},{193,129... | collective-permute-start | bytes 1572872 | tf_op jit(solution)/shard_map/ppermute | solution.py:39
  52.1 3.2 %copy-start.11 = (bf16[1024,128]{1,0:T(8,128)(2,1)}, bf16[1024,128]{1,0:T(8,128)(2,1)S(1)}, u32[]{:S(2)}) copy-start(bf16[1024,128]{1,0:T(8,128)(2,1)S(1)} %collective-permute-done.8) | copy-start | bytes 786436
  52.1 13.5 %collective-permute-start.7 = (bf16[512,256]{1,0:T(8,128)(2,1)}, bf16[512,256]{1,0:T(8,128)(2,1)S(1)}, u32[]{:S(2)}, u32[]{:S(2)}) collective-permute-start(bf16[512,256]{1,0:T(8,128)(2,1)} %slice.79), channel_id=1, source_target_pairs={{0,240},{16,224},{32,208},{48,192},{64,176},{80,160},{96,144},{112... | collective-permute-start | bytes 786440 | tf_op jit(solution)/shard_map/ppermute | solution.py:39
  60.2 15.3 %copy-start.2 = (bf16[512,512]{1,0:T(8,128)(2,1)S(1)}, bf16[512,512]{1,0:T(8,128)(2,1)}, u32[]{:S(2)}) copy-start(bf16[512,512]{1,0:T(8,128)(2,1)} %copy-done.1) | copy-start | bytes 1572868
  65.5 7.8 %copy-start.8 = (bf16[512,256]{1,0:T(8,128)(2,1)}, bf16[512,256]{1,0:T(8,128)(2,1)S(1)}, u32[]{:S(2)}) copy-start(bf16[512,256]{1,0:T(8,128)(2,1)S(1)} %collective-permute-done.7) | copy-start | bytes 786436
  65.5 35.0 %collective-permute-start.26 = (bf16[256,2688]{1,0:T(8,128)(2,1)}, bf16[256,2688]{1,0:T(8,128)(2,1)}, u32[]{:S(2)}, u32[]{:S(2)}) collective-permute-start(bf16[256,2688]{1,0:T(8,128)(2,1)} %get-tuple-element.42.refs_0_), channel_id=1, source_target_pairs={{0,2},{2,4},{4,6},{6,0},{1,3},{3,5},{5,7},{7,1},{8,10},{10,12},{12... | collective-permute-start | bytes 4128776 | tf_op jit(solution)/shard_map/ppermute | solution.py:39
  66.8 16.1 %collective-permute-start.17 = (bf16[2048,128]{1,0:T(8,128)(2,1)}, bf16[2048,128]{1,0:T(8,128)(2,1)}, u32[]{:S(2)}, u32[]{:S(2)}) collective-permute-start(bf16[2048,128]{1,0:T(8,128)(2,1)} %pad_maximum_fusion.4.refs_12_), channel_id=1, source_target_pairs={{0,192},{64,0},{128,64},{192,128},{1,193},{65,1},{129,65},{193,129... | collective-permute-start | bytes 1572872 | tf_op jit(solution)/shard_map/ppermute | solution.py:39
  73.0 15.5 %collective-permute-start.16 = (bf16[2048,128]{1,0:T(8,128)(2,1)}, bf16[2048,128]{1,0:T(8,128)(2,1)}, u32[]{:S(2)}, u32[]{:S(2)}) collective-permute-start(bf16[2048,128]{1,0:T(8,128)(2,1)} %pad_maximum_fusion.4.refs_12_), channel_id=1, source_target_pairs={{0,64},{64,128},{128,192},{192,0},{1,65},{65,129},{129,193},{193,1... | collective-permute-start | bytes 1572872 | tf_op jit(solution)/shard_map/ppermute | solution.py:39
  74.2 22.4 %collective-permute-start.13 = (bf16[2048,128]{1,0:T(8,128)(2,1)S(1)}, bf16[2048,128]{1,0:T(8,128)(2,1)}, u32[]{:S(2)}, u32[]{:S(2)}) collective-permute-start(bf16[2048,128]{1,0:T(8,128)(2,1)S(1)} %collective-permute-done.2.refs_8_), channel_id=1, source_target_pairs={{0,64},{64,128},{128,192},{192,0},{1,65},{65,129},{129,193},{193,1... | collective-permute-start | bytes 1572872 | tf_op jit(solution)/shard_map/ppermute | solution.py:39
  80.4 8.1 %copy-start.9 = (bf16[512,256]{1,0:T(8,128)(2,1)S(1)}, bf16[512,256]{1,0:T(8,128)(2,1)}, u32[]{:S(2)}) copy-start(bf16[512,256]{1,0:T(8,128)(2,1)} %copy-done.8) | copy-start | bytes 786436
  82.9 26.3 %collective-permute-start.15 = (bf16[2048,128]{1,0:T(8,128)(2,1)S(1)}, bf16[2048,128]{1,0:T(8,128)(2,1)}, u32[]{:S(2)}, u32[]{:S(2)}) collective-permute-start(bf16[2048,128]{1,0:T(8,128)(2,1)S(1)} %pad_maximum_fusion.3.refs_3_), channel_id=1, source_target_pairs={{0,48},{16,0},{32,16},{48,32},{1,49},{17,1},{33,17},{49,33},{2,50}... | collective-permute-start | bytes 1572872 | tf_op jit(solution)/shard_map/ppermute | solution.py:39
  88.5 20.6 %collective-permute-start.12 = (bf16[2048,128]{1,0:T(8,128)(2,1)S(1)}, bf16[2048,128]{1,0:T(8,128)(2,1)}, u32[]{:S(2)}, u32[]{:S(2)}) collective-permute-start(bf16[2048,128]{1,0:T(8,128)(2,1)S(1)} %pad_maximum_fusion.3.refs_3_), channel_id=1, source_target_pairs={{0,16},{16,32},{32,48},{48,0},{1,17},{17,33},{33,49},{49,1},{2,18}... | collective-permute-start | bytes 1572872 | tf_op jit(solution)/shard_map/ppermute | solution.py:39
  93.4 5.8 %copy-start.5 = (bf16[1,128,1024]{2,1,0:T(8,128)(2,1)S(1)}, bf16[1,128,1024]{2,1,0:T(8,128)(2,1)}, u32[]{:S(2)}) copy-start(bf16[1,128,1024]{2,1,0:T(8,128)(2,1)} %get-tuple-element.54) | copy-start | bytes 786436
  93.4 5.8 %copy-start.6 = (bf16[1,128,1024]{2,1,0:T(8,128)(2,1)S(1)}, bf16[1,128,1024]{2,1,0:T(8,128)(2,1)}, u32[]{:S(2)}) copy-start(bf16[1,128,1024]{2,1,0:T(8,128)(2,1)} %get-tuple-element.55) | copy-start | bytes 786436
  93.4 5.8 %copy-start.7 = (bf16[1,128,1024]{2,1,0:T(8,128)(2,1)S(1)}, bf16[1,128,1024]{2,1,0:T(8,128)(2,1)}, u32[]{:S(2)}) copy-start(bf16[1,128,1024]{2,1,0:T(8,128)(2,1)} %get-tuple-element.56) | copy-start | bytes 786436
  96.6 14.0 %collective-permute-start.19 = (bf16[1024,128]{1,0:T(8,128)(2,1)S(1)}, bf16[1024,128]{1,0:T(8,128)(2,1)S(1)}, u32[]{:S(2)}, u32[]{:S(2)}) collective-permute-start(bf16[1024,128]{1,0:T(8,128)(2,1)S(1)} %slice.87), channel_id=1, source_target_pairs={{0,192},{64,0},{128,64},{192,128},{1,193},{65,1},{129,65},{193,129... | collective-permute-start | bytes 786440 | tf_op jit(solution)/shard_map/ppermute | solution.py:39
  97.9 15.5 %collective-permute-start.18 = (bf16[1024,128]{1,0:T(8,128)(2,1)S(1)}, bf16[1024,128]{1,0:T(8,128)(2,1)S(1)}, u32[]{:S(2)}, u32[]{:S(2)}) collective-permute-start(bf16[1024,128]{1,0:T(8,128)(2,1)S(1)} %slice.86), channel_id=1, source_target_pairs={{0,64},{64,128},{128,192},{192,0},{1,65},{65,129},{129,193},{193,1... | collective-permute-start | bytes 786440 | tf_op jit(solution)/shard_map/ppermute | solution.py:39
  99.2 14.1 %copy-start = (s32[3]{0:T(128)S(1)}, s32[3]{0:T(128)}, u32[]{:S(2)}) copy-start(s32[3]{0:T(128)} %constant.108.clone.1.diag) | copy-start | bytes 40
  100.5 92.0 %collective-permute-start.28 = (bf16[256,2688]{1,0:T(8,128)(2,1)}, bf16[256,2688]{1,0:T(8,128)(2,1)}, u32[]{:S(2)}, u32[]{:S(2)}) collective-permute-start(bf16[256,2688]{1,0:T(8,128)(2,1)} %get-tuple-element.41.refs_1_), channel_id=1, source_target_pairs={{0,2},{2,4},{4,6},{6,0},{1,3},{3,5},{5,7},{7,1},{8,10},{10,12},{12... | collective-permute-start | bytes 4128776 | tf_op jit(solution)/shard_map/ppermute | solution.py:39
  109.2 83.4 %collective-permute-start.31 = (bf16[256,2688]{1,0:T(8,128)(2,1)}, bf16[256,2688]{1,0:T(8,128)(2,1)}, u32[]{:S(2)}, u32[]{:S(2)}) collective-permute-start(bf16[256,2688]{1,0:T(8,128)(2,1)} %get-tuple-element.42.refs_0_), channel_id=1, source_target_pairs={{0,6},{2,0},{4,2},{6,4},{1,7},{3,1},{5,3},{7,5},{8,14},{10,8},{12,... | collective-permute-start | bytes 4128776 | tf_op jit(solution)/shard_map/ppermute | solution.py:39
  109.2 83.3 %collective-permute-start.29 = (bf16[256,2688]{1,0:T(8,128)(2,1)}, bf16[256,2688]{1,0:T(8,128)(2,1)}, u32[]{:S(2)}, u32[]{:S(2)}) collective-permute-start(bf16[256,2688]{1,0:T(8,128)(2,1)} %collective-permute-done.26.refs_2_), channel_id=1, source_target_pairs={{0,2},{2,4},{4,6},{6,0},{1,3},{3,5},{5,7},{7,1},{8,10},{10,12},{12... | collective-permute-start | bytes 4128776 | tf_op jit(solution)/shard_map/ppermute | solution.py:39
  110.6 81.9 %collective-permute-start.30 = (bf16[256,2688]{1,0:T(8,128)(2,1)}, bf16[256,2688]{1,0:T(8,128)(2,1)}, u32[]{:S(2)}, u32[]{:S(2)}) collective-permute-start(bf16[256,2688]{1,0:T(8,128)(2,1)} %collective-permute-done.27.refs_7_), channel_id=1, source_target_pairs={{0,6},{2,0},{4,2},{6,4},{1,7},{3,1},{5,3},{7,5},{8,14},{10,8},{12,... | collective-permute-start | bytes 4128776 | tf_op jit(solution)/shard_map/ppermute | solution.py:39
  142.2 6.8 %collective-permute-start.20 = (f32[1,1024]{1,0:T(1,128)S(1)}, f32[1,1024]{1,0:T(1,128)S(1)}, u32[]{:S(2)}, u32[]{:S(2)}) collective-permute-start(f32[1,1024]{1,0:T(1,128)S(1)} %get-tuple-element.70), channel_id=1, source_target_pairs={{0,240},{16,224},{32,208},{48,192},{64,176},{80,160},{96,144},{112... | collective-permute-start | bytes 12296 | tf_op jit(solution)/shard_map/ppermute | solution.py:39
  148.9 9.6 %collective-permute-start.21 = (bf16[512,256]{1,0:T(8,128)(2,1)S(1)}, bf16[512,256]{1,0:T(8,128)(2,1)S(1)}, u32[]{:S(2)}, u32[]{:S(2)}) collective-permute-start(bf16[512,256]{1,0:T(8,128)(2,1)S(1)} %get-tuple-element.48), channel_id=1, source_target_pairs={{0,240},{16,224},{32,208},{48,192},{64,176},{80,160},{96,144},{112... | collective-permute-start | bytes 786440 | tf_op jit(solution)/shard_map/ppermute | solution.py:39
  160.9 9.8 %collective-permute-start.24 = (bf16[256,256]{1,0:T(8,128)(2,1)S(1)}, bf16[256,256]{1,0:T(8,128)(2,1)S(1)}, u32[]{:S(2)}, u32[]{:S(2)}) collective-permute-start(bf16[256,256]{1,0:T(8,128)(2,1)S(1)} %get-tuple-element.50), channel_id=1, source_target_pairs={{0,6},{2,0},{4,2},{6,4},{1,7},{3,1},{5,3},{7,5},{8,14},{10,8},{12,... | collective-permute-start | bytes 393224 | tf_op jit(solution)/shard_map/ppermute | solution.py:39
  170.8 5.3 %collective-permute-start.23 = (bf16[256,256]{1,0:T(8,128)(2,1)S(1)}, bf16[256,256]{1,0:T(8,128)(2,1)S(1)}, u32[]{:S(2)}, u32[]{:S(2)}) collective-permute-start(bf16[256,256]{1,0:T(8,128)(2,1)S(1)} %get-tuple-element.51), channel_id=1, source_target_pairs={{0,4},{2,6},{4,0},{6,2},{1,5},{3,7},{5,1},{7,3},{8,12},{10,14},{12... | collective-permute-start | bytes 393224 | tf_op jit(solution)/shard_map/ppermute | solution.py:39
  176.1 6.4 %collective-permute-start.22 = (bf16[256,256]{1,0:T(8,128)(2,1)S(1)}, bf16[256,256]{1,0:T(8,128)(2,1)S(1)}, u32[]{:S(2)}, u32[]{:S(2)}) collective-permute-start(bf16[256,256]{1,0:T(8,128)(2,1)S(1)} %get-tuple-element.52), channel_id=1, source_target_pairs={{0,2},{2,4},{4,6},{6,0},{1,3},{3,5},{5,7},{7,1},{8,10},{10,12},{12... | collective-permute-start | bytes 393224 | tf_op jit(solution)/shard_map/ppermute | solution.py:39
  182.5 8.7 %collective-permute-start.25 = (bf16[256,1024]{1,0:T(8,128)(2,1)S(1)}, bf16[256,1024]{1,0:T(8,128)(2,1)S(1)}, u32[]{:S(2)}, u32[]{:S(2)}) collective-permute-start(bf16[256,1024]{1,0:T(8,128)(2,1)S(1)} %pad_maximum_fusion.5), channel_id=1, source_target_pairs={{0,8},{8,0},{1,9},{9,1},{2,10},{10,2},{3,11},{11,3},{4,12},{12,4},... | collective-permute-start | bytes 1572872 | tf_op jit(solution)/shard_map/ppermute | solution.py:39
  202.7 9.5 %collective-permute-start.32 = (bf16[64,2688]{1,0:T(8,128)(2,1)}, bf16[64,2688]{1,0:T(8,128)(2,1)S(1)}, u32[]{:S(2)}, u32[]{:S(2)}) collective-permute-start(bf16[64,2688]{1,0:T(8,128)(2,1)} %get-tuple-element.38), channel_id=1, source_target_pairs={{0,1},{1,0},{2,3},{3,2},{4,5},{5,4},{6,7},{7,6},{8,9},{9,8},{10,11... | collective-permute-start | bytes 1032200 | tf_op jit(solution)/shard_map/ppermute | solution.py:39
  202.8 10.6 %collective-permute-start.33 = (bf16[64,2688]{1,0:T(8,128)(2,1)}, bf16[64,2688]{1,0:T(8,128)(2,1)S(1)}, u32[]{:S(2)}, u32[]{:S(2)}) collective-permute-start(bf16[64,2688]{1,0:T(8,128)(2,1)} %get-tuple-element.39), channel_id=1, source_target_pairs={{0,8},{8,0},{1,9},{9,1},{2,10},{10,2},{3,11},{11,3},{4,12},{12,4},... | collective-permute-start | bytes 1032200 | tf_op jit(solution)/shard_map/ppermute | solution.py:39
  203.3 16.9 %collective-permute-start.34 = (bf16[64,2688]{1,0:T(8,128)(2,1)}, bf16[64,2688]{1,0:T(8,128)(2,1)S(1)}, u32[]{:S(2)}, u32[]{:S(2)}) collective-permute-start(bf16[64,2688]{1,0:T(8,128)(2,1)} %get-tuple-element.40), channel_id=1, source_target_pairs={{0,9},{1,8},{8,1},{9,0},{2,11},{3,10},{10,3},{11,2},{4,13},{5,12},... | collective-permute-start | bytes 1032200 | tf_op jit(solution)/shard_map/ppermute | solution.py:39

commit v2 on v1

--- a/solution.py
+++ b/solution.py
@@ -1,3 +1,5 @@
+import functools
+
 import jax
 import jax.numpy as jnp
 from jax import lax
@@ -39,10 +41,10 @@
     return lax.ppermute(value, axes, pairs)
 
 
-def attend_kernel(lo, hi, diag, slots, q_ref, *refs):
-    pieces, (out_ref, lse_ref, kv_ref, s_ref, m_ref, l_ref, acc_ref, sems) = refs[:-8], refs[-8:]
-    tasks, _, rows = q_ref.shape
-    half = rows // 2
+def attend_kernel(lo, hi, slots, q_ref, *refs, masked):
+    pieces, (out_ref, lse_ref, kv_ref, qt_ref, s_ref, m_ref, l_ref, acc_ref, sems) = refs[:-9], refs[-9:]
+    tasks, half, _ = q_ref.shape
+    rows = 2 * half
     span = kv_ref.shape[1] // 2
 
     copies = [
@@ -53,6 +55,18 @@
     ]
     for copy in copies:
         copy.start()
+
+    def pack(t, _):
+        for h in range(2):
+            cols = pl.ds(h * half, half)
+            scaled = q_ref[t, :, h * HD : (h + 1) * HD].astype(jnp.float32) * query_scale
+            scaled = scaled.T
+            high = scaled.astype(jnp.bfloat16)
+            qt_ref[t, :HD, cols] = high
+            qt_ref[t, HD:, cols] = (scaled - high.astype(jnp.float32)).astype(jnp.bfloat16)
+        return 0
+
+    lax.fori_loop(0, tasks, pack, 0)
     for copy in copies:
         copy.wait()
 
@@ -63,21 +77,15 @@
         return jnp.concatenate([keys, keys], axis=1)
 
     def scores_of(keys, task, cols):
-        return jnp.dot(keys, q_ref[task, :, cols], preferred_element_type=jnp.float32)
+        return jnp.dot(keys, qt_ref[task, :, cols], preferred_element_type=jnp.float32)
 
     def step(task, at_span, last):
         slot = slots[at_span]
         values_t = jnp.concatenate(
             [kv_ref[slot, pl.ds(span + i * HD, HD), :] for i in range(span // HD)], axis=1
         )
-        keys = None if last else keys_twice(at_span + 1)
-        for r, cols in enumerate(tiles):
-            scores = s_ref[:, cols]
-            following = None if last else scores_of(keys, task, cols)
-            if last:
-                key_pos = lax.broadcasted_iota(jnp.int32, (span, TILE), 0)
-                row_pos = lax.broadcasted_iota(jnp.int32, (span, TILE), 1) + (r * TILE) % half
-                scores = jnp.where(key_pos <= row_pos + task * half, scores, neg_fill)
+
+        def absorb(scores, cols):
             old_max = m_ref[:, cols]
             new_max = jnp.maximum(old_max, jnp.max(scores, axis=0, keepdims=True))
             weights = jnp.exp2(scores - new_max)
@@ -87,7 +95,23 @@
             acc_ref[:, cols] = acc_ref[:, cols] * factor + jnp.dot(
                 values_t, weights.astype(jnp.bfloat16), preferred_element_type=jnp.float32
             )
-            if not last:
+
+        if last:
+            key_pos = lax.broadcasted_iota(jnp.int32, (span, half), 0)
+            row_pos = lax.broadcasted_iota(jnp.int32, (span, half), 1) + task * half
+
+            def head(h, _):
+                cols = pl.ds(pl.multiple_of(h * half, half), half)
+                absorb(jnp.where(key_pos <= row_pos, s_ref[:, cols], neg_fill), cols)
+                return 0
+
+            lax.fori_loop(0, 2, head, 0)
+        else:
+            keys = keys_twice(at_span + 1)
+            for cols in tiles:
+                scores = s_ref[:, cols]
+                following = scores_of(keys, task, cols)
+                absorb(scores, cols)
                 s_ref[:, cols] = following
 
     def one_task(t, _):
@@ -95,11 +119,16 @@
         l_ref[...] = jnp.zeros_like(l_ref)
         acc_ref[...] = jnp.zeros_like(acc_ref)
 
-        @pl.when((diag[t] > 0) | (lo[t] < hi[t]))
+        @pl.when(masked | (lo[t] < hi[t]))
         def _():
             keys = keys_twice(lo[t])
-            for cols in tiles:
+
+            def fill(r, _):
+                cols = pl.ds(pl.multiple_of(r * TILE, TILE), TILE)
                 s_ref[:, cols] = scores_of(keys, t, cols)
+                return 0
+
+            lax.fori_loop(0, rows // TILE, fill, 0)
 
         def body(at_span, _):
             step(t, at_span, False)
@@ -107,8 +136,7 @@
 
         lax.fori_loop(lo[t], hi[t], body, 0)
 
-        @pl.when(diag[t] > 0)
-        def _():
+        if masked:
             step(t, hi[t], True)
 
         total = l_ref[...]
@@ -125,21 +153,22 @@
     lax.fori_loop(0, tasks, one_task, 0)
 
 
-def attend(lo, hi, diag, slots, q, pieces):
-    tasks, _, rows = q.shape
+def attend(lo, hi, slots, q, pieces, masked):
+    tasks, rows = q.shape[0], 2 * q.shape[1]
     smem = pl.BlockSpec(memory_space=pltpu.SMEM)
     vmem = pl.BlockSpec(memory_space=pltpu.VMEM)
     hbm = pl.BlockSpec(memory_space=pltpu.MemorySpace.HBM)
     return pl.pallas_call(
-        attend_kernel,
+        functools.partial(attend_kernel, masked=masked),
         out_shape=(
             jax.ShapeDtypeStruct((tasks, rows // 2, PAIR), jnp.bfloat16),
             jax.ShapeDtypeStruct((tasks, 1, rows), jnp.float32),
         ),
-        in_specs=[smem] * 4 + [vmem] + [hbm] * len(pieces),
+        in_specs=[smem] * 3 + [vmem] + [hbm] * len(pieces),
         out_specs=(vmem, vmem),
         scratch_shapes=[
             pltpu.VMEM((16,) + pieces[0].shape, jnp.bfloat16),
+            pltpu.VMEM((tasks, PAIR, rows), jnp.bfloat16),
             pltpu.VMEM((pieces[0].shape[0] // 2, rows), jnp.float32),
             pltpu.VMEM((1, rows), jnp.float32),
             pltpu.VMEM((1, rows), jnp.float32),
@@ -148,9 +177,9 @@
         ],
         compiler_params=pltpu.CompilerParams(vmem_limit_bytes=48 * 2**20),
         cost_estimate=pl.CostEstimate(
-            flops=16384 * 1024 * HD * 4, bytes_accessed=9_000_000, transcendentals=0
+            flops=8192 * 1024 * HD * 4, bytes_accessed=9_000_000, transcendentals=0
         ),
-    )(lo, hi, diag, slots, q, *pieces)
+    )(lo, hi, slots, q, *pieces)
 
 
 def project_kernel(at, low_ref, high_ref, *refs):
@@ -170,7 +199,7 @@
 
 def project(at, low, high, *weights):
     rows, width = low.shape[0], weights[0].shape[1]
-    tile = 384
+    tile = width // 3
     whole = pl.BlockSpec(low.shape, lambda n: (0, 0))
     weight = pl.BlockSpec((PAIR, tile), lambda n: (0, n))
     out = pl.BlockSpec((rows // 4, tile), lambda n: (0, n))
@@ -188,15 +217,6 @@
     )(at, low, high, *weights)
 
 
-def packed_queries(q):
-    tokens = q.shape[0]
-    scaled = q.astype(jnp.float32) * query_scale
-    scaled = scaled.reshape(tokens, 2, HD).transpose(2, 1, 0).reshape(HD, 2 * tokens)
-    high = lax.reduce_precision(scaled, 8, 7)
-    low = scaled - high
-    return jnp.concatenate([high, low], axis=0).astype(jnp.bfloat16)
-
-
 def values_in_blocks(v):
     tokens = v.shape[0]
     return v.reshape(tokens // HD, HD, HD).transpose(0, 2, 1).reshape(tokens, HD)
@@ -281,31 +301,35 @@
     w2_top = x_up(w1_top)
     w2_low = x_down(w3_low)
 
-    lent_len = jnp.maximum(2 * span - (spans - 1), 0)
-    taken_len = jnp.maximum(spans - 1 - 2 * span, 0)
+    late = span >= spans // 2
+    early_keys = jnp.abs(2 * span - (spans - 1))
     ints = lambda *v: jnp.stack([jnp.asarray(e, jnp.int32) for e in v])
     order = jnp.arange(spans, dtype=jnp.int32)
     slots = (lax.axis_index("y") - order // spans_z) % spans_y * 4
     slots = (slots + (lax.axis_index("zh") - order % spans_z) % spans_z).astype(jnp.int32)
-    q_all = jnp.stack([packed_queries(a) for a in (first[:, :PAIR], second[:, :PAIR], lent)])
+    q_first, q_second = first[:, :PAIR], second[:, :PAIR]
+    part_out, part_lse = attend(
+        ints(0), ints(early_keys), slots, jnp.where(late, q_first, lent)[None], pieces, False
+    )
+    back_out = moved(part_out[0], ("y", "zh"), mirror)
+    back_lse = moved(part_lse[0], ("y", "zh"), mirror)
+    begin = jnp.where(late, early_keys, 0)
     out, lse = attend(
-        ints(0, lent_len, 0), ints(span, span, taken_len), ints(1, 1, 0), slots, q_all, pieces
-    )
-    back_out = moved(out[2], ("y", "zh"), mirror)
-    back_lse = moved(lse[2], ("y", "zh"), mirror)
-    back_lse = jnp.where(lent_len > 0, back_lse[0], neg_fill)
-    joint = jnp.maximum(lse[1, 0], back_lse)
-    own_part = jnp.exp2(lse[1, 0] - joint)
-    back_part = jnp.exp2(back_lse - joint)
-    total = own_part + back_part
+        ints(begin, begin), ints(span, span), slots, jnp.stack([q_first, q_second]), pieces, True
+    )
+    part_lse = jnp.stack([part_lse[0, 0], back_lse[0]])
+    part_lse = jnp.where(late, part_lse, neg_fill)
+    lse = lse[:, 0]
+    joint = jnp.maximum(lse, part_lse)
+    own_share, part_share = jnp.exp2(lse - joint), jnp.exp2(part_lse - joint)
+    total = own_share + part_share
 
     def by_row(a):
-        return jnp.repeat(a.reshape(2, rows).T, HD, axis=1)
-
-    merged = out[1].astype(jnp.float32) * by_row(own_part / total) + back_out.astype(
-        jnp.float32
-    ) * by_row(back_part / total)
-    attended = jnp.stack([out[0], merged.astype(jnp.bfloat16)])
+        return jnp.repeat(a.reshape(2, 2, rows).transpose(0, 2, 1), HD, axis=2)
+
+    merged = out.astype(jnp.float32) * by_row(own_share / total)
+    merged = merged + jnp.stack([part_out[0], back_out]).astype(jnp.float32) * by_row(part_share / total)
+    attended = merged.astype(jnp.bfloat16)
 
     groups = lax.axis_size("x")
     piece = rows // groups

time: 222 us -> 236 us (1.063)
  waiting for transfers between devices: 70 us -> 83.1 us
  starting transfers between devices: 68.4 us -> 80.8 us
  local copies, waits for them, and re-layouts: 29.3 us -> 21.3 us
  other arithmetic: 14.3 us -> 10.2 us
    ppermute x35, waiting for transfers between devices: 70 us -> 83.1 us  [moved(): return lax.ppermute(value, axes, pairs)]
    ppermute x35, starting transfers between devices: 68.4 us -> 80.8 us  [moved(): return lax.ppermute(value, axes, pairs)]
    transpose x5 -> x2, local copies, waits for them, and re-layouts: 6.1 us -> 0.44 us  [by_row(): return jnp.repeat(a.reshape(2, 2, rows).transpose(0, 2, 1), HD, axis=2)]
    reshape x3 -> x2, local copies, waits for them, and re-layouts: 6.31 us -> 2.9 us  [by_row(): return jnp.repeat(a.reshape(2, 2, rows).transpose(0, 2, 1), HD, axis=2)]
    pallas_call x1 -> x2, Pallas kernels: 28.8 us -> 31.8 us  [attend(): pl.pallas_call(functools.partial(attend_kernel, masked=masked), out_shape...]
    mul x3 -> x0, other arithmetic: 2.54 us -> none  [packed_queries(): scaled = q.astype(jnp.float32) * query_scale]
    unnamed x27 -> x20, local copies, waits for them, and re-layouts: 5.1 us -> 4.61 us
  transfers between devices with their start and end apart: 35 -> 35, of which waited for: 17 -> 18; matrix products, arithmetic and copies ran while one was open for 17% -> 10% of each run, Pallas kernels for 13% -> 13%
where the time goes in v2:
time: 236 us
  waiting for transfers between devices  83.1 us (35%)
  starting transfers between devices  80.8 us (34%)
  Pallas kernels  40.2 us (17%)
  local copies, waits for them, and re-layouts  21.3 us (9%)
  other arithmetic  10.2 us (4%)
    ppermute x35, waiting for transfers between devices, moved(): return lax.ppermute(value, axes, pairs)  83.1 us
    ppermute x35, starting transfers between devices, moved(): return lax.ppermute(value, axes, pairs)  80.8 us
    pallas_call x2, Pallas kernels, attend(): pl.pallas_call(functools.partial(attend_kernel, masked=masked), out_shape...  31.8 us
    pallas_call x1, Pallas kernels, project(): pl.pallas_call(project_kernel, grid=(width // tile,), out_shape=(jax.Shap...  8.38 us
  transfers between devices with their start and end apart: 35, of which 18 were waited for; matrix products, arithmetic and copies ran while one was open for 10% of the time, Pallas kernels for 13%

profile of v2, /device:TPU:1, one launch (start us, length us, event | category | flops | bytes accessed | tf_op | source)
XLA Modules:
  0.0 236.0 jit_solution(10621431050142486120)
XLA Ops:
  0.0 1.1 constant_dynamic-slice_fusion.6
  1.1 1.1 constant_dynamic-slice_fusion.4
  2.3 3.3 %collective-permute-start = (bf16[512,512]{1,0:T(8,128)(2,1)S(1)}, bf16[512,512]{1,0:T(8,128)(2,1)S(1)}, u32[]{:S(2)}, u32[]{:S(2)}) collective-permute-start(bf16[512,512]{1,0:T(8,128)(2,1)S(1)} %pad_maximum_fusion.1), channel_id=1, source_target_pairs={{0,8},{8,0},{1,9},{9,1},{2,10},{10,2},{3,11},{11,3},{4,12},{12,4},... | collective-permute-start | bytes 1572872 | tf_op jit(solution)/shard_map/ppermute | solution.py:41
  5.6 1.5 collective-permute-done
  8.2 1.1 collective-permute-start.4
  9.7 5.6 %collective-permute-start.2 = (bf16[2048,128]{1,0:T(8,128)(2,1)S(1)}, bf16[2048,128]{1,0:T(8,128)(2,1)S(1)}, u32[]{:S(2)}, u32[]{:S(2)}) collective-permute-start(bf16[2048,128]{1,0:T(8,128)(2,1)S(1)} %pad_maximum_fusion.3.refs_0_), channel_id=1, source_target_pairs={{0,48},{16,0},{32,16},{48,32},{1,49},{17,1},{33,17},{49,33},{2,50}... | collective-permute-start | bytes 1572872 | tf_op jit(solution)/shard_map/ppermute | solution.py:41
  15.3 6.1 %collective-permute-done.4.refs_2_ = bf16[2048,128]{1,0:T(8,128)(2,1)S(1)} collective-permute-done((bf16[2048,128]{1,0:T(8,128)(2,1)S(1)}, bf16[2048,128]{1,0:T(8,128)(2,1)S(1)}, u32[]{:S(2)}, u32[]{:S(2)}) %collective-permute-start.4) | collective-permute-done | bytes 524320 | tf_op jit(solution)/shard_map/ppermute | solution.py:41
  21.4 0.7 slice.64
  22.1 2.2 collective-permute-start.6
  24.3 0.7 slice.63
  25.1 4.0 %collective-permute-done.6 = bf16[1024,128]{1,0:T(8,128)(2,1)} collective-permute-done((bf16[1024,128]{1,0:T(8,128)(2,1)}, bf16[1024,128]{1,0:T(8,128)(2,1)}, u32[]{:S(2)}, u32[]{:S(2)}) %collective-permute-start.6) | collective-permute-done | bytes 262176 | tf_op jit(solution)/shard_map/ppermute | solution.py:41
  29.1 3.9 %collective-permute-done.5 = bf16[1024,128]{1,0:T(8,128)(2,1)} collective-permute-done((bf16[1024,128]{1,0:T(8,128)(2,1)}, bf16[1024,128]{1,0:T(8,128)(2,1)}, u32[]{:S(2)}, u32[]{:S(2)}) %collective-permute-start.5) | collective-permute-done | bytes 262176 | tf_op jit(solution)/shard_map/ppermute | solution.py:41
  32.9 1.1 pad_maximum_fusion.4.refs_3_
  34.0 1.3 collective-permute-done.2.refs_8_
  35.3 6.7 %collective-permute-start.8 = (bf16[1024,128]{1,0:T(8,128)(2,1)S(1)}, bf16[1024,128]{1,0:T(8,128)(2,1)S(1)}, u32[]{:S(2)}, u32[]{:S(2)}) collective-permute-start(bf16[1024,128]{1,0:T(8,128)(2,1)S(1)} %slice.52), channel_id=1, source_target_pairs={{0,48},{16,0},{32,16},{48,32},{1,49},{17,1},{33,17},{49,33},{2,50}... | collective-permute-start | bytes 786440 | tf_op jit(solution)/shard_map/ppermute | solution.py:41
  42.0 3.5 %fusion.12 = (bf16[256,2688]{1,0:T(8,128)(2,1)}, bf16[256,2688]{1,0:T(8,128)(2,1)}) fusion(bf16[512,5376]{1,0:T(8,128)(2,1)} %param.7, s32[]{:T(128)S(6)} %add.140, s32[]{:T(128)S(6)} %select_n.150), kind=kLoop, calls=%fused_computation.60 | loop fusion | bytes 5505032 | tf_op jit(solution)/shard_map/slice | solution.py:276
  45.5 2.5 %collective-permute-start.27 = (bf16[256,2688]{1,0:T(8,128)(2,1)}, bf16[256,2688]{1,0:T(8,128)(2,1)}, u32[]{:S(2)}, u32[]{:S(2)}) collective-permute-start(bf16[256,2688]{1,0:T(8,128)(2,1)} %get-tuple-element.45.refs_1_), channel_id=1, source_target_pairs={{0,6},{2,0},{4,2},{6,4},{1,7},{3,1},{5,3},{7,5},{8,14},{10,8},{12,... | collective-permute-start | bytes 4128776 | tf_op jit(solution)/shard_map/ppermute | solution.py:41
  48.5 1.1 collective-permute-start.9
  49.6 3.4 %collective-permute-done.8 = bf16[1024,128]{1,0:T(8,128)(2,1)S(1)} collective-permute-done((bf16[1024,128]{1,0:T(8,128)(2,1)S(1)}, bf16[1024,128]{1,0:T(8,128)(2,1)S(1)}, u32[]{:S(2)}, u32[]{:S(2)}) %collective-permute-start.8) | collective-permute-done | bytes 262176 | tf_op jit(solution)/shard_map/ppermute | solution.py:41
  53.0 1.2 collective-permute-start.19
  54.2 2.3 collective-permute-done.7
  56.5 3.2 %collective-permute-start.13 = (bf16[2048,128]{1,0:T(8,128)(2,1)S(1)}, bf16[2048,128]{1,0:T(8,128)(2,1)S(1)}, u32[]{:S(2)}, u32[]{:S(2)}) collective-permute-start(bf16[2048,128]{1,0:T(8,128)(2,1)S(1)} %collective-permute-done.2.refs_8_), channel_id=1, source_target_pairs={{0,192},{64,0},{128,64},{192,128},{1,193},{65,1},{129,65},{193,129... | collective-permute-start | bytes 1572872 | tf_op jit(solution)/shard_map/ppermute | solution.py:41
  59.7 10.3 %collective-permute-done.19 = bf16[512,256]{1,0:T(8,128)(2,1)S(1)} collective-permute-done((bf16[512,256]{1,0:T(8,128)(2,1)S(1)}, bf16[512,256]{1,0:T(8,128)(2,1)S(1)}, u32[]{:S(2)}, u32[]{:S(2)}) %collective-permute-start.19) | collective-permute-done | bytes 262176 | tf_op jit(solution)/shard_map/ppermute | solution.py:41
  70.7 0.8 pad_maximum_fusion.5.refs_12_
  71.6 0.8 copy-done.3
  72.4 0.9 collective-permute-start.16
  73.3 0.8 copy-done.5
  74.6 1.3 collective-permute-done.13.refs_10_
  75.9 0.8 copy-done.9
  76.7 10.6 %collective-permute-done.16.refs_14_ = bf16[2048,128]{1,0:T(8,128)(2,1)} collective-permute-done((bf16[2048,128]{1,0:T(8,128)(2,1)}, bf16[2048,128]{1,0:T(8,128)(2,1)}, u32[]{:S(2)}, u32[]{:S(2)}) %collective-permute-start.16) | collective-permute-done | bytes 524320 | tf_op jit(solution)/shard_map/ppermute | solution.py:41
  87.3 2.9 %collective-permute-start.14 = (bf16[2048,128]{1,0:T(8,128)(2,1)S(1)}, bf16[2048,128]{1,0:T(8,128)(2,1)}, u32[]{:S(2)}, u32[]{:S(2)}) collective-permute-start(bf16[2048,128]{1,0:T(8,128)(2,1)S(1)} %pad_maximum_fusion.4.refs_3_), channel_id=1, source_target_pairs={{0,48},{16,0},{32,16},{48,32},{1,49},{17,1},{33,17},{49,33},{2,50}... | collective-permute-start | bytes 1572872 | tf_op jit(solution)/shard_map/ppermute | solution.py:41
  90.3 1.0 slice.66
  91.3 1.1 slice.65
  92.4 6.0 %collective-permute-done.12.refs_9_ = bf16[2048,128]{1,0:T(8,128)(2,1)} collective-permute-done((bf16[2048,128]{1,0:T(8,128)(2,1)S(1)}, bf16[2048,128]{1,0:T(8,128)(2,1)}, u32[]{:S(2)}, u32[]{:S(2)}) %collective-permute-start.12) | collective-permute-done | bytes 524320 | tf_op jit(solution)/shard_map/ppermute | solution.py:41
  98.3 1.5 collective-permute-start.17
  99.8 1.1 select_bitcast_fusion
  100.9 1.3 collective-permute-done.26.refs_2_
  102.6 2.3 collective-permute-start.31
  105.5 22.5 %shard_map.47 = (bf16[1,512,256]{2,1,0:T(8,128)(2,1)S(1)}, f32[1,1,1024]{2,1,0:T(1,128)S(1)}) custom-call(s32[1]{0:T(128)} %constant.110.clone.1.lo, s32[1]{0:T(128)} %bitcast.14.hi, s32[16]{0:T(128)S(1)} %fusion.7.slots, bf16[1,512,256]{2,1,0:T(8,128)(2,1)S(1)} %get-tuple-element.55.q_ref, bf16[2048,128]{1,0:T(8,128)(2,1)S(1)} %pad_maximum_fusion.3.refs_0_, ...), custom_call_target="tpu_custom_call" | custom-call | flops 4294967296 | bytes 9000000 | tf_op jit(solution)/shard_map/pallas_call | solution.py:161
  127.9 4.6 %collective-permute-start.20 = (f32[1,1024]{1,0:T(1,128)S(1)}, f32[1,1024]{1,0:T(1,128)S(1)}, u32[]{:S(2)}, u32[]{:S(2)}) collective-permute-start(f32[1,1024]{1,0:T(1,128)S(1)} %bitcast.41), channel_id=1, source_target_pairs={{0,240},{16,224},{32,208},{48,192},{64,176},{80,160},{96,144},{112... | collective-permute-start | bytes 12296 | tf_op jit(solution)/shard_map/ppermute | solution.py:41
  132.5 1.2 collective-permute-start.21
  133.7 1.0 copy-done.2
  134.8 9.3 %shard_map.46 = (bf16[2,512,256]{2,1,0:T(8,128)(2,1)S(1)}, f32[2,1,1024]{2,1,0:T(1,128)S(1)}) custom-call(s32[2]{0:T(128)S(1)} %get-tuple-element.71.lo, s32[2]{0:T(128)S(1)} %get-tuple-element.72.hi, s32[16]{0:T(128)S(1)} %fusion.7.slots, bf16[2,512,256]{2,1,0:T(8,128)(2,1)S(1)} %pad_maximum_fusion.2.q_ref, ...), custom_call_target="tpu_custom_call" | custom-call | flops 4294967296 | bytes 9000000 | tf_op jit(solution)/shard_map/pallas_call | solution.py:161
  145.3 2.3 collective-permute-start.30
  148.5 1.2 broadcast_in_dim.15
  149.8 0.8 reshape.38
  150.9 2.0 broadcast_in_dim.16
  152.9 2.1 reshape.39
  155.0 1.2 add_convert_fusion
  156.2 0.8 collective-permute-start.24
  157.0 9.2 %collective-permute-done.24 = bf16[256,256]{1,0:T(8,128)(2,1)S(1)} collective-permute-done((bf16[256,256]{1,0:T(8,128)(2,1)S(1)}, bf16[256,256]{1,0:T(8,128)(2,1)S(1)}, u32[]{:S(2)}, u32[]{:S(2)}) %collective-permute-start.24) | collective-permute-done | bytes 131104 | tf_op jit(solution)/shard_map/ppermute | solution.py:41
  166.2 3.6 %collective-permute-start.23 = (bf16[256,256]{1,0:T(8,128)(2,1)S(1)}, bf16[256,256]{1,0:T(8,128)(2,1)S(1)}, u32[]{:S(2)}, u32[]{:S(2)}) collective-permute-start(bf16[256,256]{1,0:T(8,128)(2,1)S(1)} %get-tuple-element.53), channel_id=1, source_target_pairs={{0,4},{2,6},{4,0},{6,2},{1,5},{3,7},{5,1},{7,3},{8,12},{10,14},{12... | collective-permute-start | bytes 393224 | tf_op jit(solution)/shard_map/ppermute | solution.py:41
  169.8 2.4 collective-permute-done.23
  172.1 1.9 collective-permute-start.22
  174.0 4.7 %collective-permute-done.22 = bf16[256,256]{1,0:T(8,128)(2,1)S(1)} collective-permute-done((bf16[256,256]{1,0:T(8,128)(2,1)S(1)}, bf16[256,256]{1,0:T(8,128)(2,1)S(1)}, u32[]{:S(2)}, u32[]{:S(2)}) %collective-permute-start.22) | collective-permute-done | bytes 131104 | tf_op jit(solution)/shard_map/ppermute | solution.py:41
  178.8 16.8 %collective-permute-start.25 = (bf16[256,1024]{1,0:T(8,128)(2,1)S(1)}, bf16[256,1024]{1,0:T(8,128)(2,1)S(1)}, u32[]{:S(2)}, u32[]{:S(2)}) collective-permute-start(bf16[256,1024]{1,0:T(8,128)(2,1)S(1)} %pad_maximum_fusion.6), channel_id=1, source_target_pairs={{0,8},{8,0},{1,9},{9,1},{2,10},{10,2},{3,11},{11,3},{4,12},{12,4},... | collective-permute-start | bytes 1572872 | tf_op jit(solution)/shard_map/ppermute | solution.py:41
  196.3 0.9 collective-permute-done.25
  197.2 1.2 broadcast_select_fusion.2
  198.5 8.4 %shard_map.48 = (f32[64,2688]{1,0:T(8,128)}, bf16[64,2688]{1,0:T(8,128)(2,1)}, bf16[64,2688]{1,0:T(8,128)(2,1)}, bf16[64,2688]{1,0:T(8,128)(2,1)}) custom-call(s32[4]{0:T(128)} %pad_add_fusion.at, bf16[256,1024]{1,0:T(8,128)(2,1)} %get-tuple-element.48.low_ref, bf16[256,1024]{1,0:T(8,128)(2,1)} %get-tuple-element.47.high_ref, ...), custom_call_target="tpu_custom_call" | custom-call | flops 2818572288 | bytes 12000000 | tf_op jit(solution)/shard_map/pallas_call | solution.py:207
  206.9 12.1 %collective-permute-start.32 = (bf16[64,2688]{1,0:T(8,128)(2,1)}, bf16[64,2688]{1,0:T(8,128)(2,1)S(1)}, u32[]{:S(2)}, u32[]{:S(2)}) collective-permute-start(bf16[64,2688]{1,0:T(8,128)(2,1)} %get-tuple-element.42), channel_id=1, source_target_pairs={{0,1},{1,0},{2,3},{3,2},{4,5},{5,4},{6,7},{7,6},{8,9},{9,8},{10,11... | collective-permute-start | bytes 1032200 | tf_op jit(solution)/shard_map/ppermute | solution.py:41
  219.6 7.6 %collective-permute-done.32 = bf16[64,2688]{1,0:T(8,128)(2,1)S(1)} collective-permute-done((bf16[64,2688]{1,0:T(8,128)(2,1)}, bf16[64,2688]{1,0:T(8,128)(2,1)S(1)}, u32[]{:S(2)}, u32[]{:S(2)}) %collective-permute-start.32) | collective-permute-done | bytes 344096 | tf_op jit(solution)/shard_map/ppermute | solution.py:41
  227.3 1.2 add_convert_fusion.2
  228.4 6.5 %collective-permute-done.34 = bf16[64,2688]{1,0:T(8,128)(2,1)S(1)} collective-permute-done((bf16[64,2688]{1,0:T(8,128)(2,1)}, bf16[64,2688]{1,0:T(8,128)(2,1)S(1)}, u32[]{:S(2)}, u32[]{:S(2)}) %collective-permute-start.34) | collective-permute-done | bytes 344096 | tf_op jit(solution)/shard_map/ppermute | solution.py:41
  235.0 1.0 maximum_select_fusion
  (75 shorter events, 8.4 us)
Async XLA Ops:
  2.3 4.8 %collective-permute-start = (bf16[512,512]{1,0:T(8,128)(2,1)S(1)}, bf16[512,512]{1,0:T(8,128)(2,1)S(1)}, u32[]{:S(2)}, u32[]{:S(2)}) collective-permute-start(bf16[512,512]{1,0:T(8,128)(2,1)S(1)} %pad_maximum_fusion.1), channel_id=1, source_target_pairs={{0,8},{8,0},{1,9},{9,1},{2,10},{10,2},{3,11},{11,3},{4,12},{12,4},... | collective-permute-start | bytes 1572872 | tf_op jit(solution)/shard_map/ppermute | solution.py:41
  7.4 0.8 copy-start.7
  8.2 13.2 %collective-permute-start.4 = (bf16[2048,128]{1,0:T(8,128)(2,1)S(1)}, bf16[2048,128]{1,0:T(8,128)(2,1)S(1)}, u32[]{:S(2)}, u32[]{:S(2)}) collective-permute-start(bf16[2048,128]{1,0:T(8,128)(2,1)S(1)} %pad_maximum_fusion.3.refs_0_), channel_id=1, source_target_pairs={{0,192},{64,0},{128,64},{192,128},{1,193},{65,1},{129,65},{193,129... | collective-permute-start | bytes 1572872 | tf_op jit(solution)/shard_map/ppermute | solution.py:41
  9.3 15.0 %collective-permute-start.3 = (bf16[2048,128]{1,0:T(8,128)(2,1)S(1)}, bf16[2048,128]{1,0:T(8,128)(2,1)S(1)}, u32[]{:S(2)}, u32[]{:S(2)}) collective-permute-start(bf16[2048,128]{1,0:T(8,128)(2,1)S(1)} %pad_maximum_fusion.3.refs_0_), channel_id=1, source_target_pairs={{0,64},{64,128},{128,192},{192,0},{1,65},{65,129},{129,193},{193,1... | collective-permute-start | bytes 1572872 | tf_op jit(solution)/shard_map/ppermute | solution.py:41
  9.7 25.6 %collective-permute-start.2 = (bf16[2048,128]{1,0:T(8,128)(2,1)S(1)}, bf16[2048,128]{1,0:T(8,128)(2,1)S(1)}, u32[]{:S(2)}, u32[]{:S(2)}) collective-permute-start(bf16[2048,128]{1,0:T(8,128)(2,1)S(1)} %pad_maximum_fusion.3.refs_0_), channel_id=1, source_target_pairs={{0,48},{16,0},{32,16},{48,32},{1,49},{17,1},{33,17},{49,33},{2,50}... | collective-permute-start | bytes 1572872 | tf_op jit(solution)/shard_map/ppermute | solution.py:41
  15.3 20.0 %collective-permute-start.1 = (bf16[2048,128]{1,0:T(8,128)(2,1)S(1)}, bf16[2048,128]{1,0:T(8,128)(2,1)S(1)}, u32[]{:S(2)}, u32[]{:S(2)}) collective-permute-start(bf16[2048,128]{1,0:T(8,128)(2,1)S(1)} %pad_maximum_fusion.3.refs_0_), channel_id=1, source_target_pairs={{0,16},{16,32},{32,48},{48,0},{1,17},{17,33},{33,49},{49,1},{2,18}... | collective-permute-start | bytes 1572872 | tf_op jit(solution)/shard_map/ppermute | solution.py:41
  22.1 7.0 %collective-permute-start.6 = (bf16[1024,128]{1,0:T(8,128)(2,1)}, bf16[1024,128]{1,0:T(8,128)(2,1)}, u32[]{:S(2)}, u32[]{:S(2)}) collective-permute-start(bf16[1024,128]{1,0:T(8,128)(2,1)} %slice.64), channel_id=1, source_target_pairs={{0,192},{64,0},{128,64},{192,128},{1,193},{65,1},{129,65},{193,129... | collective-permute-start | bytes 786440 | tf_op jit(solution)/shard_map/ppermute | solution.py:41
  25.1 7.9 %collective-permute-start.5 = (bf16[1024,128]{1,0:T(8,128)(2,1)}, bf16[1024,128]{1,0:T(8,128)(2,1)}, u32[]{:S(2)}, u32[]{:S(2)}) collective-permute-start(bf16[1024,128]{1,0:T(8,128)(2,1)} %slice.63), channel_id=1, source_target_pairs={{0,64},{64,128},{128,192},{192,0},{1,65},{65,129},{129,193},{193,1... | collective-permute-start | bytes 786440 | tf_op jit(solution)/shard_map/ppermute | solution.py:41
  35.3 70.1 %copy-start = (bf16[2048,128]{1,0:T(8,128)(2,1)}, bf16[2048,128]{1,0:T(8,128)(2,1)S(1)}, u32[]{:S(2)}) copy-start(bf16[2048,128]{1,0:T(8,128)(2,1)S(1)} %collective-permute-done.2.refs_8_) | copy-start | bytes 1572868
  35.3 70.1 %copy-start.1 = (bf16[2048,128]{1,0:T(8,128)(2,1)}, bf16[2048,128]{1,0:T(8,128)(2,1)S(1)}, u32[]{:S(2)}) copy-start(bf16[2048,128]{1,0:T(8,128)(2,1)S(1)} %collective-permute-done.1.refs_4_) | copy-start | bytes 1572868
  35.3 17.7 %collective-permute-start.8 = (bf16[1024,128]{1,0:T(8,128)(2,1)S(1)}, bf16[1024,128]{1,0:T(8,128)(2,1)S(1)}, u32[]{:S(2)}, u32[]{:S(2)}) collective-permute-start(bf16[1024,128]{1,0:T(8,128)(2,1)S(1)} %slice.52), channel_id=1, source_target_pairs={{0,48},{16,0},{32,16},{48,32},{1,49},{17,1},{33,17},{49,33},{2,50}... | collective-permute-start | bytes 786440 | tf_op jit(solution)/shard_map/ppermute | solution.py:41
  45.5 52.9 %collective-permute-start.27 = (bf16[256,2688]{1,0:T(8,128)(2,1)}, bf16[256,2688]{1,0:T(8,128)(2,1)}, u32[]{:S(2)}, u32[]{:S(2)}) collective-permute-start(bf16[256,2688]{1,0:T(8,128)(2,1)} %get-tuple-element.45.refs_1_), channel_id=1, source_target_pairs={{0,6},{2,0},{4,2},{6,4},{1,7},{3,1},{5,3},{7,5},{8,14},{10,8},{12,... | collective-permute-start | bytes 4128776 | tf_op jit(solution)/shard_map/ppermute | solution.py:41
  48.0 8.5 %collective-permute-start.7 = (bf16[1024,128]{1,0:T(8,128)(2,1)S(1)}, bf16[1024,128]{1,0:T(8,128)(2,1)S(1)}, u32[]{:S(2)}, u32[]{:S(2)}) collective-permute-start(bf16[1024,128]{1,0:T(8,128)(2,1)S(1)} %slice.51), channel_id=1, source_target_pairs={{0,16},{16,32},{32,48},{48,0},{1,17},{17,33},{33,49},{49,1},{2,18}... | collective-permute-start | bytes 786440 | tf_op jit(solution)/shard_map/ppermute | solution.py:41
  48.1 23.5 %collective-permute-start.10 = (bf16[2048,128]{1,0:T(8,128)(2,1)S(1)}, bf16[2048,128]{1,0:T(8,128)(2,1)S(1)}, u32[]{:S(2)}, u32[]{:S(2)}) collective-permute-start(bf16[2048,128]{1,0:T(8,128)(2,1)S(1)} %collective-permute-done.1.refs_4_), channel_id=1, source_target_pairs={{0,192},{64,0},{128,64},{192,128},{1,193},{65,1},{129,65},{193,129... | collective-permute-start | bytes 1572872 | tf_op jit(solution)/shard_map/ppermute | solution.py:41
  48.5 24.8 %collective-permute-start.9 = (bf16[2048,128]{1,0:T(8,128)(2,1)S(1)}, bf16[2048,128]{1,0:T(8,128)(2,1)S(1)}, u32[]{:S(2)}, u32[]{:S(2)}) collective-permute-start(bf16[2048,128]{1,0:T(8,128)(2,1)S(1)} %collective-permute-done.1.refs_4_), channel_id=1, source_target_pairs={{0,64},{64,128},{128,192},{192,0},{1,65},{65,129},{129,193},{193,1... | collective-permute-start | bytes 1572872 | tf_op jit(solution)/shard_map/ppermute | solution.py:41
  53.0 17.0 %collective-permute-start.19 = (bf16[512,256]{1,0:T(8,128)(2,1)S(1)}, bf16[512,256]{1,0:T(8,128)(2,1)S(1)}, u32[]{:S(2)}, u32[]{:S(2)}) collective-permute-start(bf16[512,256]{1,0:T(8,128)(2,1)S(1)} %get-tuple-element.35), channel_id=1, source_target_pairs={{0,240},{16,224},{32,208},{48,192},{64,176},{80,160},{96,144},{112... | collective-permute-start | bytes 786440 | tf_op jit(solution)/shard_map/ppermute | solution.py:41
  56.5 19.4 %collective-permute-start.13 = (bf16[2048,128]{1,0:T(8,128)(2,1)S(1)}, bf16[2048,128]{1,0:T(8,128)(2,1)S(1)}, u32[]{:S(2)}, u32[]{:S(2)}) collective-permute-start(bf16[2048,128]{1,0:T(8,128)(2,1)S(1)} %collective-permute-done.2.refs_8_), channel_id=1, source_target_pairs={{0,192},{64,0},{128,64},{192,128},{1,193},{65,1},{129,65},{193,129... | collective-permute-start | bytes 1572872 | tf_op jit(solution)/shard_map/ppermute | solution.py:41
  70.0 0.7 copy-start.8
  70.7 31.5 %collective-permute-start.26 = (bf16[256,2688]{1,0:T(8,128)(2,1)}, bf16[256,2688]{1,0:T(8,128)(2,1)}, u32[]{:S(2)}, u32[]{:S(2)}) collective-permute-start(bf16[256,2688]{1,0:T(8,128)(2,1)} %get-tuple-element.46.refs_0_), channel_id=1, source_target_pairs={{0,2},{2,4},{4,6},{6,0},{1,3},{3,5},{5,7},{7,1},{8,10},{10,12},{12... | collective-permute-start | bytes 4128776 | tf_op jit(solution)/shard_map/ppermute | solution.py:41
  71.6 0.8 copy-start.3
  72.4 14.9 %collective-permute-start.16 = (bf16[2048,128]{1,0:T(8,128)(2,1)}, bf16[2048,128]{1,0:T(8,128)(2,1)}, u32[]{:S(2)}, u32[]{:S(2)}) collective-permute-start(bf16[2048,128]{1,0:T(8,128)(2,1)} %pad_maximum_fusion.5.refs_12_), channel_id=1, source_target_pairs={{0,192},{64,0},{128,64},{192,128},{1,193},{65,1},{129,65},{193,129... | collective-permute-start | bytes 1572872 | tf_op jit(solution)/shard_map/ppermute | solution.py:41
  73.3 0.8 copy-start.5
  74.1 16.1 %collective-permute-start.15 = (bf16[2048,128]{1,0:T(8,128)(2,1)}, bf16[2048,128]{1,0:T(8,128)(2,1)}, u32[]{:S(2)}, u32[]{:S(2)}) collective-permute-start(bf16[2048,128]{1,0:T(8,128)(2,1)} %pad_maximum_fusion.5.refs_12_), channel_id=1, source_target_pairs={{0,64},{64,128},{128,192},{192,0},{1,65},{65,129},{129,193},{193,1... | collective-permute-start | bytes 1572872 | tf_op jit(solution)/shard_map/ppermute | solution.py:41
  75.9 0.8 copy-start.9
  76.7 21.6 %collective-permute-start.12 = (bf16[2048,128]{1,0:T(8,128)(2,1)S(1)}, bf16[2048,128]{1,0:T(8,128)(2,1)}, u32[]{:S(2)}, u32[]{:S(2)}) collective-permute-start(bf16[2048,128]{1,0:T(8,128)(2,1)S(1)} %collective-permute-done.2.refs_8_), channel_id=1, source_target_pairs={{0,64},{64,128},{128,192},{192,0},{1,65},{65,129},{129,193},{193,1... | collective-permute-start | bytes 1572872 | tf_op jit(solution)/shard_map/ppermute | solution.py:41
  87.3 15.3 %collective-permute-start.14 = (bf16[2048,128]{1,0:T(8,128)(2,1)S(1)}, bf16[2048,128]{1,0:T(8,128)(2,1)}, u32[]{:S(2)}, u32[]{:S(2)}) collective-permute-start(bf16[2048,128]{1,0:T(8,128)(2,1)S(1)} %pad_maximum_fusion.4.refs_3_), channel_id=1, source_target_pairs={{0,48},{16,0},{32,16},{48,32},{1,49},{17,1},{33,17},{49,33},{2,50}... | collective-permute-start | bytes 1572872 | tf_op jit(solution)/shard_map/ppermute | solution.py:41
  90.2 14.8 %collective-permute-start.11 = (bf16[2048,128]{1,0:T(8,128)(2,1)S(1)}, bf16[2048,128]{1,0:T(8,128)(2,1)}, u32[]{:S(2)}, u32[]{:S(2)}) collective-permute-start(bf16[2048,128]{1,0:T(8,128)(2,1)S(1)} %pad_maximum_fusion.4.refs_3_), channel_id=1, source_target_pairs={{0,16},{16,32},{32,48},{48,0},{1,17},{17,33},{33,49},{49,1},{2,18}... | collective-permute-start | bytes 1572872 | tf_op jit(solution)/shard_map/ppermute | solution.py:41
  91.3 14.1 %copy-start.4 = (bf16[2048,128]{1,0:T(8,128)(2,1)S(1)}, bf16[2048,128]{1,0:T(8,128)(2,1)}, u32[]{:S(2)}) copy-start(bf16[2048,128]{1,0:T(8,128)(2,1)} %copy-done.3) | copy-start | bytes 1572868
  91.3 14.1 %copy-start.6 = (bf16[2048,128]{1,0:T(8,128)(2,1)S(1)}, bf16[2048,128]{1,0:T(8,128)(2,1)}, u32[]{:S(2)}) copy-start(bf16[2048,128]{1,0:T(8,128)(2,1)} %copy-done.5) | copy-start | bytes 1572868
  98.3 7.1 %collective-permute-start.18 = (bf16[1024,128]{1,0:T(8,128)(2,1)S(1)}, bf16[1024,128]{1,0:T(8,128)(2,1)S(1)}, u32[]{:S(2)}, u32[]{:S(2)}) collective-permute-start(bf16[1024,128]{1,0:T(8,128)(2,1)S(1)} %slice.66), channel_id=1, source_target_pairs={{0,192},{64,0},{128,64},{192,128},{1,193},{65,1},{129,65},{193,129... | collective-permute-start | bytes 786440 | tf_op jit(solution)/shard_map/ppermute | solution.py:41
  98.3 7.1 %collective-permute-start.17 = (bf16[1024,128]{1,0:T(8,128)(2,1)S(1)}, bf16[1024,128]{1,0:T(8,128)(2,1)S(1)}, u32[]{:S(2)}, u32[]{:S(2)}) collective-permute-start(bf16[1024,128]{1,0:T(8,128)(2,1)S(1)} %slice.65), channel_id=1, source_target_pairs={{0,64},{64,128},{128,192},{192,0},{1,65},{65,129},{129,193},{193,1... | collective-permute-start | bytes 786440 | tf_op jit(solution)/shard_map/ppermute | solution.py:41
  102.2 96.2 %collective-permute-start.28 = (bf16[256,2688]{1,0:T(8,128)(2,1)}, bf16[256,2688]{1,0:T(8,128)(2,1)}, u32[]{:S(2)}, u32[]{:S(2)}) collective-permute-start(bf16[256,2688]{1,0:T(8,128)(2,1)} %get-tuple-element.45.refs_1_), channel_id=1, source_target_pairs={{0,2},{2,4},{4,6},{6,0},{1,3},{3,5},{5,7},{7,1},{8,10},{10,12},{12... | collective-permute-start | bytes 4128776 | tf_op jit(solution)/shard_map/ppermute | solution.py:41
  102.6 95.9 %collective-permute-start.31 = (bf16[256,2688]{1,0:T(8,128)(2,1)}, bf16[256,2688]{1,0:T(8,128)(2,1)}, u32[]{:S(2)}, u32[]{:S(2)}) collective-permute-start(bf16[256,2688]{1,0:T(8,128)(2,1)} %get-tuple-element.46.refs_0_), channel_id=1, source_target_pairs={{0,6},{2,0},{4,2},{6,4},{1,7},{3,1},{5,3},{7,5},{8,14},{10,8},{12,... | collective-permute-start | bytes 4128776 | tf_op jit(solution)/shard_map/ppermute | solution.py:41
  104.9 93.6 %collective-permute-start.29 = (bf16[256,2688]{1,0:T(8,128)(2,1)}, bf16[256,2688]{1,0:T(8,128)(2,1)}, u32[]{:S(2)}, u32[]{:S(2)}) collective-permute-start(bf16[256,2688]{1,0:T(8,128)(2,1)} %collective-permute-done.26.refs_2_), channel_id=1, source_target_pairs={{0,2},{2,4},{4,6},{6,0},{1,3},{3,5},{5,7},{7,1},{8,10},{10,12},{12... | collective-permute-start | bytes 4128776 | tf_op jit(solution)/shard_map/ppermute | solution.py:41
  127.9 17.4 %collective-permute-start.20 = (f32[1,1024]{1,0:T(1,128)S(1)}, f32[1,1024]{1,0:T(1,128)S(1)}, u32[]{:S(2)}, u32[]{:S(2)}) collective-permute-start(f32[1,1024]{1,0:T(1,128)S(1)} %bitcast.41), channel_id=1, source_target_pairs={{0,240},{16,224},{32,208},{48,192},{64,176},{80,160},{96,144},{112... | collective-permute-start | bytes 12296 | tf_op jit(solution)/shard_map/ppermute | solution.py:41
  132.5 22.4 %collective-permute-start.21 = (bf16[512,256]{1,0:T(8,128)(2,1)S(1)}, bf16[512,256]{1,0:T(8,128)(2,1)}, u32[]{:S(2)}, u32[]{:S(2)}) collective-permute-start(bf16[512,256]{1,0:T(8,128)(2,1)S(1)} %bitcast.40), channel_id=1, source_target_pairs={{0,240},{16,224},{32,208},{48,192},{64,176},{80,160},{96,144},{112... | collective-permute-start | bytes 786440 | tf_op jit(solution)/shard_map/ppermute | solution.py:41
  133.7 1.0 copy-start.2
  145.3 53.1 %collective-permute-start.30 = (bf16[256,2688]{1,0:T(8,128)(2,1)}, bf16[256,2688]{1,0:T(8,128)(2,1)}, u32[]{:S(2)}, u32[]{:S(2)}) collective-permute-start(bf16[256,2688]{1,0:T(8,128)(2,1)} %collective-permute-done.27.refs_7_), channel_id=1, source_target_pairs={{0,6},{2,0},{4,2},{6,4},{1,7},{3,1},{5,3},{7,5},{8,14},{10,8},{12,... | collective-permute-start | bytes 4128776 | tf_op jit(solution)/shard_map/ppermute | solution.py:41
  156.2 9.9 %collective-permute-start.24 = (bf16[256,256]{1,0:T(8,128)(2,1)S(1)}, bf16[256,256]{1,0:T(8,128)(2,1)S(1)}, u32[]{:S(2)}, u32[]{:S(2)}) collective-permute-start(bf16[256,256]{1,0:T(8,128)(2,1)S(1)} %get-tuple-element.52), channel_id=1, source_target_pairs={{0,6},{2,0},{4,2},{6,4},{1,7},{3,1},{5,3},{7,5},{8,14},{10,8},{12,... | collective-permute-start | bytes 393224 | tf_op jit(solution)/shard_map/ppermute | solution.py:41
  166.2 5.9 %collective-permute-start.23 = (bf16[256,256]{1,0:T(8,128)(2,1)S(1)}, bf16[256,256]{1,0:T(8,128)(2,1)S(1)}, u32[]{:S(2)}, u32[]{:S(2)}) collective-permute-start(bf16[256,256]{1,0:T(8,128)(2,1)S(1)} %get-tuple-element.53), channel_id=1, source_target_pairs={{0,4},{2,6},{4,0},{6,2},{1,5},{3,7},{5,1},{7,3},{8,12},{10,14},{12... | collective-permute-start | bytes 393224 | tf_op jit(solution)/shard_map/ppermute | solution.py:41
  172.1 6.7 %collective-permute-start.22 = (bf16[256,256]{1,0:T(8,128)(2,1)S(1)}, bf16[256,256]{1,0:T(8,128)(2,1)S(1)}, u32[]{:S(2)}, u32[]{:S(2)}) collective-permute-start(bf16[256,256]{1,0:T(8,128)(2,1)S(1)} %get-tuple-element.54), channel_id=1, source_target_pairs={{0,2},{2,4},{4,6},{6,0},{1,3},{3,5},{5,7},{7,1},{8,10},{10,12},{12... | collective-permute-start | bytes 393224 | tf_op jit(solution)/shard_map/ppermute | solution.py:41
  178.8 18.4 %collective-permute-start.25 = (bf16[256,1024]{1,0:T(8,128)(2,1)S(1)}, bf16[256,1024]{1,0:T(8,128)(2,1)S(1)}, u32[]{:S(2)}, u32[]{:S(2)}) collective-permute-start(bf16[256,1024]{1,0:T(8,128)(2,1)S(1)} %pad_maximum_fusion.6), channel_id=1, source_target_pairs={{0,8},{8,0},{1,9},{9,1},{2,10},{10,2},{3,11},{11,3},{4,12},{12,4},... | collective-permute-start | bytes 1572872 | tf_op jit(solution)/shard_map/ppermute | solution.py:41
  206.9 20.4 %collective-permute-start.32 = (bf16[64,2688]{1,0:T(8,128)(2,1)}, bf16[64,2688]{1,0:T(8,128)(2,1)S(1)}, u32[]{:S(2)}, u32[]{:S(2)}) collective-permute-start(bf16[64,2688]{1,0:T(8,128)(2,1)} %get-tuple-element.42), channel_id=1, source_target_pairs={{0,1},{1,0},{2,3},{3,2},{4,5},{5,4},{6,7},{7,6},{8,9},{9,8},{10,11... | collective-permute-start | bytes 1032200 | tf_op jit(solution)/shard_map/ppermute | solution.py:41
  219.0 9.4 %collective-permute-start.33 = (bf16[64,2688]{1,0:T(8,128)(2,1)}, bf16[64,2688]{1,0:T(8,128)(2,1)S(1)}, u32[]{:S(2)}, u32[]{:S(2)}) collective-permute-start(bf16[64,2688]{1,0:T(8,128)(2,1)} %get-tuple-element.43), channel_id=1, source_target_pairs={{0,8},{8,0},{1,9},{9,1},{2,10},{10,2},{3,11},{11,3},{4,12},{12,4},... | collective-permute-start | bytes 1032200 | tf_op jit(solution)/shard_map/ppermute | solution.py:41
  219.6 15.3 %collective-permute-start.34 = (bf16[64,2688]{1,0:T(8,128)(2,1)}, bf16[64,2688]{1,0:T(8,128)(2,1)S(1)}, u32[]{:S(2)}, u32[]{:S(2)}) collective-permute-start(bf16[64,2688]{1,0:T(8,128)(2,1)} %get-tuple-element.44), channel_id=1, source_target_pairs={{0,9},{1,8},{8,1},{9,0},{2,11},{3,10},{10,3},{11,2},{4,13},{5,12},... | collective-permute-start | bytes 1032200 | tf_op jit(solution)/shard_map/ppermute | solution.py:41

commit v3 on v1

--- a/solution.py
+++ b/solution.py
@@ -40,9 +40,9 @@
 
 
 def attend_kernel(lo, hi, diag, slots, q_ref, *refs):
-    pieces, (out_ref, lse_ref, kv_ref, s_ref, m_ref, l_ref, acc_ref, sems) = refs[:-8], refs[-8:]
-    tasks, _, rows = q_ref.shape
-    half = rows // 2
+    pieces, (out_ref, lse_ref, kv_ref, qt_ref, s_ref, m_ref, l_ref, acc_ref, sems) = refs[:-9], refs[-9:]
+    tasks, half, _ = q_ref.shape
+    rows = 2 * half
     span = kv_ref.shape[1] // 2
 
     copies = [
@@ -53,6 +53,18 @@
     ]
     for copy in copies:
         copy.start()
+
+    def pack(t, _):
+        for h in range(2):
+            cols = pl.ds(h * half, half)
+            scaled = q_ref[t, :, h * HD : (h + 1) * HD].astype(jnp.float32) * query_scale
+            scaled = scaled.T
+            high = scaled.astype(jnp.bfloat16)
+            qt_ref[t, :HD, cols] = high
+            qt_ref[t, HD:, cols] = (scaled - high.astype(jnp.float32)).astype(jnp.bfloat16)
+        return 0
+
+    lax.fori_loop(0, tasks, pack, 0)
     for copy in copies:
         copy.wait()
 
@@ -63,7 +75,7 @@
         return jnp.concatenate([keys, keys], axis=1)
 
     def scores_of(keys, task, cols):
-        return jnp.dot(keys, q_ref[task, :, cols], preferred_element_type=jnp.float32)
+        return jnp.dot(keys, qt_ref[task, :, cols], preferred_element_type=jnp.float32)
 
     def step(task, at_span, last):
         slot = slots[at_span]
@@ -126,7 +138,7 @@
 
 
 def attend(lo, hi, diag, slots, q, pieces):
-    tasks, _, rows = q.shape
+    tasks, rows = q.shape[0], 2 * q.shape[1]
     smem = pl.BlockSpec(memory_space=pltpu.SMEM)
     vmem = pl.BlockSpec(memory_space=pltpu.VMEM)
     hbm = pl.BlockSpec(memory_space=pltpu.MemorySpace.HBM)
@@ -140,6 +152,7 @@
         out_specs=(vmem, vmem),
         scratch_shapes=[
             pltpu.VMEM((16,) + pieces[0].shape, jnp.bfloat16),
+            pltpu.VMEM((tasks, PAIR, rows), jnp.bfloat16),
             pltpu.VMEM((pieces[0].shape[0] // 2, rows), jnp.float32),
             pltpu.VMEM((1, rows), jnp.float32),
             pltpu.VMEM((1, rows), jnp.float32),
@@ -170,7 +183,7 @@
 
 def project(at, low, high, *weights):
     rows, width = low.shape[0], weights[0].shape[1]
-    tile = 384
+    tile = width // 3
     whole = pl.BlockSpec(low.shape, lambda n: (0, 0))
     weight = pl.BlockSpec((PAIR, tile), lambda n: (0, n))
     out = pl.BlockSpec((rows // 4, tile), lambda n: (0, n))
@@ -188,15 +201,6 @@
     )(at, low, high, *weights)
 
 
-def packed_queries(q):
-    tokens = q.shape[0]
-    scaled = q.astype(jnp.float32) * query_scale
-    scaled = scaled.reshape(tokens, 2, HD).transpose(2, 1, 0).reshape(HD, 2 * tokens)
-    high = lax.reduce_precision(scaled, 8, 7)
-    low = scaled - high
-    return jnp.concatenate([high, low], axis=0).astype(jnp.bfloat16)
-
-
 def values_in_blocks(v):
     tokens = v.shape[0]
     return v.reshape(tokens // HD, HD, HD).transpose(0, 2, 1).reshape(tokens, HD)
@@ -268,7 +272,6 @@
     z2 = jnp.concatenate(z2, axis=0)
     mirror = lambda at: (spans_y - 1 - at[0], spans_z - 1 - at[1])
     lent = moved(lending, ("y", "zh"), mirror)
-    z2, y2 = lax.optimization_barrier((z2, y2))
     z2_up, z2_down = y_up(z2), y_down(z2)
     z1_far, z3_far = z_up(y2), z_down(y2)
     pieces = [own_kv, y1, y3, y2]
@@ -287,7 +290,7 @@
     order = jnp.arange(spans, dtype=jnp.int32)
     slots = (lax.axis_index("y") - order // spans_z) % spans_y * 4
     slots = (slots + (lax.axis_index("zh") - order % spans_z) % spans_z).astype(jnp.int32)
-    q_all = jnp.stack([packed_queries(a) for a in (first[:, :PAIR], second[:, :PAIR], lent)])
+    q_all = jnp.stack([first[:, :PAIR], second[:, :PAIR], lent])
     out, lse = attend(
         ints(0, lent_len, 0), ints(span, span, taken_len), ints(1, 1, 0), slots, q_all, pieces
     )

time: 222 us -> 223 us (level)
  waiting for transfers between devices: 70 us -> 85.2 us
  local copies, waits for them, and re-layouts: 29.3 us -> 18.1 us
  other arithmetic: 14.3 us -> 7.8 us
  starting transfers between devices: 68.4 us -> 74.1 us
  Pallas kernels: 39 us -> 36.6 us
    ppermute x35, waiting for transfers between devices: 70 us -> 85.2 us  [moved(): return lax.ppermute(value, axes, pairs)]
    reshape x3 -> x0, local copies, waits for them, and re-layouts: 6.31 us -> none  [packed_queries(): scaled.reshape(tokens, 2, HD).transpose(2, 1, 0).reshape(HD, 2 * tokens)]
    transpose x3 -> x0, local copies, waits for them, and re-layouts: 5.8 us -> none  [packed_queries(): scaled.reshape(tokens, 2, HD).transpose(2, 1, 0).reshape(HD, 2 * tokens)]
    ppermute x35, starting transfers between devices: 68.4 us -> 74.1 us  [moved(): return lax.ppermute(value, axes, pairs)]
    concatenate x4 -> x0, other arithmetic: 3.61 us -> none  [the longest x1 1.88 us: layer(): z2 = jnp.concatenate(z2, axis=0)]
    mul x3 -> x0, other arithmetic: 2.54 us -> none  [packed_queries(): scaled = q.astype(jnp.float32) * query_scale]
    unnamed x27 -> x19, local copies, waits for them, and re-layouts: 5.1 us -> 4.28 us
  transfers between devices with their start and end apart: 35 -> 35, of which waited for: 17 -> 20; matrix products, arithmetic and copies ran while one was open for 17% -> 8% of each run, Pallas kernels for 13% -> 13%
where the time goes in v3:
time: 223 us; the launch traced here: 222 us
  waiting for transfers between devices  85.2 us (38%)
  starting transfers between devices  74.1 us (33%)
  Pallas kernels  36.6 us (16%)
  local copies, waits for them, and re-layouts  18.1 us (8%)
  other arithmetic  7.8 us (3%)
    ppermute x35, waiting for transfers between devices, moved(): return lax.ppermute(value, axes, pairs)  85.2 us
    ppermute x35, starting transfers between devices, moved(): return lax.ppermute(value, axes, pairs)  74.1 us
    pallas_call x1, Pallas kernels, attend(): pl.pallas_call(attend_kernel, out_shape=(jax.ShapeDtypeStruct((tasks, row...  28.2 us
    pallas_call x1, Pallas kernels, project(): pl.pallas_call(project_kernel, grid=(width // tile,), out_shape=(jax.Shap...  8.41 us
  transfers between devices with their start and end apart: 35, of which 20 were waited for; matrix products, arithmetic and copies ran while one was open for 8% of the time, Pallas kernels for 13%

profile of v3, /device:TPU:1, one launch (start us, length us, event | category | flops | bytes accessed | tf_op | source)
XLA Modules:
  0.0 222.2 jit_solution(16116101362445664532)
XLA Ops:
  0.0 1.1 constant_dynamic-slice_fusion.6
  1.1 1.1 constant_dynamic-slice_fusion.4
  2.3 3.3 %collective-permute-start = (bf16[512,512]{1,0:T(8,128)(2,1)S(1)}, bf16[512,512]{1,0:T(8,128)(2,1)S(1)}, u32[]{:S(2)}, u32[]{:S(2)}) collective-permute-start(bf16[512,512]{1,0:T(8,128)(2,1)S(1)} %pad_maximum_fusion.2), channel_id=1, source_target_pairs={{0,8},{8,0},{1,9},{9,1},{2,10},{10,2},{3,11},{11,3},{4,12},{12,4},... | collective-permute-start | bytes 1572872 | tf_op jit(solution)/shard_map/ppermute | solution.py:39
  5.6 1.5 collective-permute-done
  8.2 1.1 collective-permute-start.4
  9.7 5.6 %collective-permute-start.2 = (bf16[2048,128]{1,0:T(8,128)(2,1)S(1)}, bf16[2048,128]{1,0:T(8,128)(2,1)S(1)}, u32[]{:S(2)}, u32[]{:S(2)}) collective-permute-start(bf16[2048,128]{1,0:T(8,128)(2,1)S(1)} %pad_maximum_fusion.3.refs_0_), channel_id=1, source_target_pairs={{0,48},{16,0},{32,16},{48,32},{1,49},{17,1},{33,17},{49,33},{2,50}... | collective-permute-start | bytes 1572872 | tf_op jit(solution)/shard_map/ppermute | solution.py:39
  15.3 6.1 %collective-permute-done.4.refs_2_ = bf16[2048,128]{1,0:T(8,128)(2,1)S(1)} collective-permute-done((bf16[2048,128]{1,0:T(8,128)(2,1)S(1)}, bf16[2048,128]{1,0:T(8,128)(2,1)S(1)}, u32[]{:S(2)}, u32[]{:S(2)}) %collective-permute-start.4) | collective-permute-done | bytes 524320 | tf_op jit(solution)/shard_map/ppermute | solution.py:39
  21.4 0.7 slice.85
  22.1 2.2 %collective-permute-start.6 = (bf16[1024,128]{1,0:T(8,128)(2,1)}, bf16[1024,128]{1,0:T(8,128)(2,1)}, u32[]{:S(2)}, u32[]{:S(2)}) collective-permute-start(bf16[1024,128]{1,0:T(8,128)(2,1)} %slice.85), channel_id=1, source_target_pairs={{0,192},{64,0},{128,64},{192,128},{1,193},{65,1},{129,65},{193,129... | collective-permute-start | bytes 786440 | tf_op jit(solution)/shard_map/ppermute | solution.py:39
  24.3 0.7 slice.84
  25.1 4.0 %collective-permute-done.6 = bf16[1024,128]{1,0:T(8,128)(2,1)} collective-permute-done((bf16[1024,128]{1,0:T(8,128)(2,1)}, bf16[1024,128]{1,0:T(8,128)(2,1)}, u32[]{:S(2)}, u32[]{:S(2)}) %collective-permute-start.6) | collective-permute-done | bytes 262176 | tf_op jit(solution)/shard_map/ppermute | solution.py:39
  29.1 3.8 %collective-permute-done.5 = bf16[1024,128]{1,0:T(8,128)(2,1)} collective-permute-done((bf16[1024,128]{1,0:T(8,128)(2,1)}, bf16[1024,128]{1,0:T(8,128)(2,1)}, u32[]{:S(2)}, u32[]{:S(2)}) %collective-permute-start.5) | collective-permute-done | bytes 262176 | tf_op jit(solution)/shard_map/ppermute | solution.py:39
  32.9 1.1 pad_maximum_fusion.4.refs_3_
  34.0 1.3 collective-permute-done.2.refs_8_
  35.3 6.7 %collective-permute-start.15 = (bf16[1024,128]{1,0:T(8,128)(2,1)S(1)}, bf16[1024,128]{1,0:T(8,128)(2,1)S(1)}, u32[]{:S(2)}, u32[]{:S(2)}) collective-permute-start(bf16[1024,128]{1,0:T(8,128)(2,1)S(1)} %slice.68), channel_id=1, source_target_pairs={{0,48},{16,0},{32,16},{48,32},{1,49},{17,1},{33,17},{49,33},{2,50}... | collective-permute-start | bytes 786440 | tf_op jit(solution)/shard_map/ppermute | solution.py:39
  42.0 3.5 %fusion.15 = (bf16[256,2688]{1,0:T(8,128)(2,1)}, bf16[256,2688]{1,0:T(8,128)(2,1)}) fusion(bf16[512,5376]{1,0:T(8,128)(2,1)} %param.7, s32[]{:T(128)S(6)} %add.141, s32[]{:T(128)S(6)} %select_n.139), kind=kLoop, calls=%fused_computation.68 | loop fusion | bytes 5505032 | tf_op jit(solution)/shard_map/slice | solution.py:260
  45.5 2.5 %collective-permute-start.27 = (bf16[256,2688]{1,0:T(8,128)(2,1)}, bf16[256,2688]{1,0:T(8,128)(2,1)}, u32[]{:S(2)}, u32[]{:S(2)}) collective-permute-start(bf16[256,2688]{1,0:T(8,128)(2,1)} %get-tuple-element.37.refs_1_), channel_id=1, source_target_pairs={{0,6},{2,0},{4,2},{6,4},{1,7},{3,1},{5,3},{7,5},{8,14},{10,8},{12,... | collective-permute-start | bytes 4128776 | tf_op jit(solution)/shard_map/ppermute | solution.py:39
  48.3 1.3 collective-permute-start.8
  49.6 3.4 %collective-permute-done.15 = bf16[1024,128]{1,0:T(8,128)(2,1)S(1)} collective-permute-done((bf16[1024,128]{1,0:T(8,128)(2,1)S(1)}, bf16[1024,128]{1,0:T(8,128)(2,1)S(1)}, u32[]{:S(2)}, u32[]{:S(2)}) %collective-permute-start.15) | collective-permute-done | bytes 262176 | tf_op jit(solution)/shard_map/ppermute | solution.py:39
  53.0 1.2 collective-permute-start.7
  54.2 2.3 %collective-permute-done.14 = bf16[1024,128]{1,0:T(8,128)(2,1)S(1)} collective-permute-done((bf16[1024,128]{1,0:T(8,128)(2,1)S(1)}, bf16[1024,128]{1,0:T(8,128)(2,1)S(1)}, u32[]{:S(2)}, u32[]{:S(2)}) %collective-permute-start.14) | collective-permute-done | bytes 262176 | tf_op jit(solution)/shard_map/ppermute | solution.py:39
  56.5 3.2 %collective-permute-start.12 = (bf16[2048,128]{1,0:T(8,128)(2,1)S(1)}, bf16[2048,128]{1,0:T(8,128)(2,1)S(1)}, u32[]{:S(2)}, u32[]{:S(2)}) collective-permute-start(bf16[2048,128]{1,0:T(8,128)(2,1)S(1)} %collective-permute-done.2.refs_8_), channel_id=1, source_target_pairs={{0,192},{64,0},{128,64},{192,128},{1,193},{65,1},{129,65},{193,129... | collective-permute-start | bytes 1572872 | tf_op jit(solution)/shard_map/ppermute | solution.py:39
  59.7 10.3 %collective-permute-done.7 = bf16[512,256]{1,0:T(8,128)(2,1)S(1)} collective-permute-done((bf16[512,256]{1,0:T(8,128)(2,1)S(1)}, bf16[512,256]{1,0:T(8,128)(2,1)S(1)}, u32[]{:S(2)}, u32[]{:S(2)}) %collective-permute-start.7) | collective-permute-done | bytes 262176 | tf_op jit(solution)/shard_map/ppermute | solution.py:39
  70.0 0.7 copy-done.6
  70.7 0.7 constant_dynamic-update-slice_fusion.1
  71.4 0.7 constant_dynamic-update-slice_fusion.refs_12_
  72.2 0.8 copy-done
  73.0 0.7 collective-permute-start.17
  73.7 0.8 copy-done.2
  74.5 0.7 collective-permute-start.16
  75.2 0.7 collective-permute-done.12.refs_10_
  75.9 0.8 copy-done.8
  76.7 10.5 %collective-permute-done.17.refs_14_ = bf16[2048,128]{1,0:T(8,128)(2,1)} collective-permute-done((bf16[2048,128]{1,0:T(8,128)(2,1)}, bf16[2048,128]{1,0:T(8,128)(2,1)}, u32[]{:S(2)}, u32[]{:S(2)}) %collective-permute-start.17) | collective-permute-done | bytes 524320 | tf_op jit(solution)/shard_map/ppermute | solution.py:39
  87.3 3.4 %collective-permute-start.13 = (bf16[2048,128]{1,0:T(8,128)(2,1)S(1)}, bf16[2048,128]{1,0:T(8,128)(2,1)}, u32[]{:S(2)}, u32[]{:S(2)}) collective-permute-start(bf16[2048,128]{1,0:T(8,128)(2,1)S(1)} %pad_maximum_fusion.4.refs_3_), channel_id=1, source_target_pairs={{0,48},{16,0},{32,16},{48,32},{1,49},{17,1},{33,17},{49,33},{2,50}... | collective-permute-start | bytes 1572872 | tf_op jit(solution)/shard_map/ppermute | solution.py:39
  90.9 1.0 slice.87
  91.9 1.1 slice.86
  93.0 5.6 %collective-permute-done.11.refs_9_ = bf16[2048,128]{1,0:T(8,128)(2,1)} collective-permute-done((bf16[2048,128]{1,0:T(8,128)(2,1)S(1)}, bf16[2048,128]{1,0:T(8,128)(2,1)}, u32[]{:S(2)}, u32[]{:S(2)}) %collective-permute-start.11) | collective-permute-done | bytes 524320 | tf_op jit(solution)/shard_map/ppermute | solution.py:39
  98.6 1.5 collective-permute-start.18
  100.0 1.0 slice_bitcast_fusion
  101.0 1.0 pad_maximum_fusion.q_ref
  102.2 1.7 collective-permute-start.28
  103.9 1.0 collective-permute-start.31
  104.9 1.1 collective-permute-start.29
  106.0 1.6 collective-permute-start.30
  107.6 28.2 %shard_map.46 = (bf16[3,512,256]{2,1,0:T(8,128)(2,1)}, f32[3,1,1024]{2,1,0:T(1,128)S(1)}) custom-call(s32[3]{0:T(128)S(1)} %get-tuple-element.65.lo, s32[3]{0:T(128)S(1)} %get-tuple-element.66.hi, s32[3]{0:T(128)S(1)} %copy-done.4, s32[16]{0:T(128)S(1)} %fusion.10.slots, bf16[3,512,256]{2,1,0:T(8,128)(2,1)} %pad_maximum_fusion.q_ref, ...), custom_call_target="tpu_custom_call" | custom-call | flops 8589934592 | bytes 9000000 | tf_op jit(solution)/shard_map/pallas_call | solution.py:145
  135.8 5.1 %collective-permute-start.20 = (f32[1,1024]{1,0:T(1,128)S(1)}, f32[1,1024]{1,0:T(1,128)S(1)}, u32[]{:S(2)}, u32[]{:S(2)}) collective-permute-start(f32[1,1024]{1,0:T(1,128)S(1)} %get-tuple-element.62), channel_id=1, source_target_pairs={{0,240},{16,224},{32,208},{48,192},{64,176},{80,160},{96,144},{112... | collective-permute-start | bytes 12296 | tf_op jit(solution)/shard_map/ppermute | solution.py:39
  140.9 1.1 fusion.16
  142.6 5.0 %collective-permute-start.21 = (bf16[512,256]{1,0:T(8,128)(2,1)S(1)}, bf16[512,256]{1,0:T(8,128)(2,1)S(1)}, u32[]{:S(2)}, u32[]{:S(2)}) collective-permute-start(bf16[512,256]{1,0:T(8,128)(2,1)S(1)} %get-tuple-element.44), channel_id=1, source_target_pairs={{0,240},{16,224},{32,208},{48,192},{64,176},{80,160},{96,144},{112... | collective-permute-start | bytes 786440 | tf_op jit(solution)/shard_map/ppermute | solution.py:39
  147.9 4.1 %collective-permute-done.21 = bf16[512,256]{1,0:T(8,128)(2,1)S(1)} collective-permute-done((bf16[512,256]{1,0:T(8,128)(2,1)S(1)}, bf16[512,256]{1,0:T(8,128)(2,1)S(1)}, u32[]{:S(2)}, u32[]{:S(2)}) %collective-permute-start.21) | collective-permute-done | bytes 262176 | tf_op jit(solution)/shard_map/ppermute | solution.py:39
  153.2 1.1 fusion.1
  155.0 5.1 %collective-permute-done.24 = bf16[256,256]{1,0:T(8,128)(2,1)S(1)} collective-permute-done((bf16[256,256]{1,0:T(8,128)(2,1)S(1)}, bf16[256,256]{1,0:T(8,128)(2,1)S(1)}, u32[]{:S(2)}, u32[]{:S(2)}) %collective-permute-start.24) | collective-permute-done | bytes 131104 | tf_op jit(solution)/shard_map/ppermute | solution.py:39
  160.1 1.2 collective-permute-start.23
  161.3 5.6 %collective-permute-done.23 = bf16[256,256]{1,0:T(8,128)(2,1)S(1)} collective-permute-done((bf16[256,256]{1,0:T(8,128)(2,1)S(1)}, bf16[256,256]{1,0:T(8,128)(2,1)S(1)}, u32[]{:S(2)}, u32[]{:S(2)}) %collective-permute-start.23) | collective-permute-done | bytes 131104 | tf_op jit(solution)/shard_map/ppermute | solution.py:39
  167.0 4.9 %collective-permute-done.22 = bf16[256,256]{1,0:T(8,128)(2,1)S(1)} collective-permute-done((bf16[256,256]{1,0:T(8,128)(2,1)S(1)}, bf16[256,256]{1,0:T(8,128)(2,1)S(1)}, u32[]{:S(2)}, u32[]{:S(2)}) %collective-permute-start.22) | collective-permute-done | bytes 131104 | tf_op jit(solution)/shard_map/ppermute | solution.py:39
  172.0 16.5 %collective-permute-start.25 = (bf16[256,1024]{1,0:T(8,128)(2,1)S(1)}, bf16[256,1024]{1,0:T(8,128)(2,1)S(1)}, u32[]{:S(2)}, u32[]{:S(2)}) collective-permute-start(bf16[256,1024]{1,0:T(8,128)(2,1)S(1)} %pad_maximum_fusion.5), channel_id=1, source_target_pairs={{0,8},{8,0},{1,9},{9,1},{2,10},{10,2},{3,11},{11,3},{4,12},{12,4},... | collective-permute-start | bytes 1572872 | tf_op jit(solution)/shard_map/ppermute | solution.py:39
  189.1 0.9 collective-permute-done.25
  190.0 1.2 broadcast_select_fusion.2
  191.3 8.4 %shard_map.47 = (f32[64,2688]{1,0:T(8,128)}, bf16[64,2688]{1,0:T(8,128)(2,1)}, bf16[64,2688]{1,0:T(8,128)(2,1)}, bf16[64,2688]{1,0:T(8,128)(2,1)}) custom-call(s32[4]{0:T(128)} %pad_add_fusion.at, bf16[256,1024]{1,0:T(8,128)(2,1)} %get-tuple-element.40.low_ref, bf16[256,1024]{1,0:T(8,128)(2,1)} %get-tuple-element.39.high_ref, ...), custom_call_target="tpu_custom_call" | custom-call | flops 2818572288 | bytes 12000000 | tf_op jit(solution)/shard_map/pallas_call | solution.py:191
  199.7 5.4 %collective-permute-start.32 = (bf16[64,2688]{1,0:T(8,128)(2,1)}, bf16[64,2688]{1,0:T(8,128)(2,1)S(1)}, u32[]{:S(2)}, u32[]{:S(2)}) collective-permute-start(bf16[64,2688]{1,0:T(8,128)(2,1)} %get-tuple-element.34), channel_id=1, source_target_pairs={{0,1},{1,0},{2,3},{3,2},{4,5},{5,4},{6,7},{7,6},{8,9},{9,8},{10,11... | collective-permute-start | bytes 1032200 | tf_op jit(solution)/shard_map/ppermute | solution.py:39
  205.1 0.7 collective-permute-start.33
  205.8 7.6 %collective-permute-done.32 = bf16[64,2688]{1,0:T(8,128)(2,1)S(1)} collective-permute-done((bf16[64,2688]{1,0:T(8,128)(2,1)}, bf16[64,2688]{1,0:T(8,128)(2,1)S(1)}, u32[]{:S(2)}, u32[]{:S(2)}) %collective-permute-start.32) | collective-permute-done | bytes 344096 | tf_op jit(solution)/shard_map/ppermute | solution.py:39
  213.4 1.2 add_convert_fusion.1
  214.6 6.5 %collective-permute-done.34 = bf16[64,2688]{1,0:T(8,128)(2,1)S(1)} collective-permute-done((bf16[64,2688]{1,0:T(8,128)(2,1)}, bf16[64,2688]{1,0:T(8,128)(2,1)S(1)}, u32[]{:S(2)}, u32[]{:S(2)}) %collective-permute-start.34) | collective-permute-done | bytes 344096 | tf_op jit(solution)/shard_map/ppermute | solution.py:39
  221.1 1.0 maximum_select_fusion
  (70 shorter events, 6.1 us)
Async XLA Ops:
  2.3 4.8 %collective-permute-start = (bf16[512,512]{1,0:T(8,128)(2,1)S(1)}, bf16[512,512]{1,0:T(8,128)(2,1)S(1)}, u32[]{:S(2)}, u32[]{:S(2)}) collective-permute-start(bf16[512,512]{1,0:T(8,128)(2,1)S(1)} %pad_maximum_fusion.2), channel_id=1, source_target_pairs={{0,8},{8,0},{1,9},{9,1},{2,10},{10,2},{3,11},{11,3},{4,12},{12,4},... | collective-permute-start | bytes 1572872 | tf_op jit(solution)/shard_map/ppermute | solution.py:39
  7.4 0.8 copy-start.5
  8.2 13.2 %collective-permute-start.4 = (bf16[2048,128]{1,0:T(8,128)(2,1)S(1)}, bf16[2048,128]{1,0:T(8,128)(2,1)S(1)}, u32[]{:S(2)}, u32[]{:S(2)}) collective-permute-start(bf16[2048,128]{1,0:T(8,128)(2,1)S(1)} %pad_maximum_fusion.3.refs_0_), channel_id=1, source_target_pairs={{0,192},{64,0},{128,64},{192,128},{1,193},{65,1},{129,65},{193,129... | collective-permute-start | bytes 1572872 | tf_op jit(solution)/shard_map/ppermute | solution.py:39
  9.3 15.0 %collective-permute-start.3 = (bf16[2048,128]{1,0:T(8,128)(2,1)S(1)}, bf16[2048,128]{1,0:T(8,128)(2,1)S(1)}, u32[]{:S(2)}, u32[]{:S(2)}) collective-permute-start(bf16[2048,128]{1,0:T(8,128)(2,1)S(1)} %pad_maximum_fusion.3.refs_0_), channel_id=1, source_target_pairs={{0,64},{64,128},{128,192},{192,0},{1,65},{65,129},{129,193},{193,1... | collective-permute-start | bytes 1572872 | tf_op jit(solution)/shard_map/ppermute | solution.py:39
  9.7 25.6 %collective-permute-start.2 = (bf16[2048,128]{1,0:T(8,128)(2,1)S(1)}, bf16[2048,128]{1,0:T(8,128)(2,1)S(1)}, u32[]{:S(2)}, u32[]{:S(2)}) collective-permute-start(bf16[2048,128]{1,0:T(8,128)(2,1)S(1)} %pad_maximum_fusion.3.refs_0_), channel_id=1, source_target_pairs={{0,48},{16,0},{32,16},{48,32},{1,49},{17,1},{33,17},{49,33},{2,50}... | collective-permute-start | bytes 1572872 | tf_op jit(solution)/shard_map/ppermute | solution.py:39
  15.3 20.0 %collective-permute-start.1 = (bf16[2048,128]{1,0:T(8,128)(2,1)S(1)}, bf16[2048,128]{1,0:T(8,128)(2,1)S(1)}, u32[]{:S(2)}, u32[]{:S(2)}) collective-permute-start(bf16[2048,128]{1,0:T(8,128)(2,1)S(1)} %pad_maximum_fusion.3.refs_0_), channel_id=1, source_target_pairs={{0,16},{16,32},{32,48},{48,0},{1,17},{17,33},{33,49},{49,1},{2,18}... | collective-permute-start | bytes 1572872 | tf_op jit(solution)/shard_map/ppermute | solution.py:39
  22.1 7.0 %collective-permute-start.6 = (bf16[1024,128]{1,0:T(8,128)(2,1)}, bf16[1024,128]{1,0:T(8,128)(2,1)}, u32[]{:S(2)}, u32[]{:S(2)}) collective-permute-start(bf16[1024,128]{1,0:T(8,128)(2,1)} %slice.85), channel_id=1, source_target_pairs={{0,192},{64,0},{128,64},{192,128},{1,193},{65,1},{129,65},{193,129... | collective-permute-start | bytes 786440 | tf_op jit(solution)/shard_map/ppermute | solution.py:39
  25.0 7.9 %collective-permute-start.5 = (bf16[1024,128]{1,0:T(8,128)(2,1)}, bf16[1024,128]{1,0:T(8,128)(2,1)}, u32[]{:S(2)}, u32[]{:S(2)}) collective-permute-start(bf16[1024,128]{1,0:T(8,128)(2,1)} %slice.84), channel_id=1, source_target_pairs={{0,64},{64,128},{128,192},{192,0},{1,65},{65,129},{129,193},{193,1... | collective-permute-start | bytes 786440 | tf_op jit(solution)/shard_map/ppermute | solution.py:39
  35.3 17.7 %collective-permute-start.15 = (bf16[1024,128]{1,0:T(8,128)(2,1)S(1)}, bf16[1024,128]{1,0:T(8,128)(2,1)S(1)}, u32[]{:S(2)}, u32[]{:S(2)}) collective-permute-start(bf16[1024,128]{1,0:T(8,128)(2,1)S(1)} %slice.68), channel_id=1, source_target_pairs={{0,48},{16,0},{32,16},{48,32},{1,49},{17,1},{33,17},{49,33},{2,50}... | collective-permute-start | bytes 786440 | tf_op jit(solution)/shard_map/ppermute | solution.py:39
  45.5 53.1 %collective-permute-start.27 = (bf16[256,2688]{1,0:T(8,128)(2,1)}, bf16[256,2688]{1,0:T(8,128)(2,1)}, u32[]{:S(2)}, u32[]{:S(2)}) collective-permute-start(bf16[256,2688]{1,0:T(8,128)(2,1)} %get-tuple-element.37.refs_1_), channel_id=1, source_target_pairs={{0,6},{2,0},{4,2},{6,4},{1,7},{3,1},{5,3},{7,5},{8,14},{10,8},{12,... | collective-permute-start | bytes 4128776 | tf_op jit(solution)/shard_map/ppermute | solution.py:39
  48.0 8.5 %collective-permute-start.14 = (bf16[1024,128]{1,0:T(8,128)(2,1)S(1)}, bf16[1024,128]{1,0:T(8,128)(2,1)S(1)}, u32[]{:S(2)}, u32[]{:S(2)}) collective-permute-start(bf16[1024,128]{1,0:T(8,128)(2,1)S(1)} %slice.67), channel_id=1, source_target_pairs={{0,16},{16,32},{32,48},{48,0},{1,17},{17,33},{33,49},{49,1},{2,18}... | collective-permute-start | bytes 786440 | tf_op jit(solution)/shard_map/ppermute | solution.py:39
  48.0 24.1 %collective-permute-start.9 = (bf16[2048,128]{1,0:T(8,128)(2,1)S(1)}, bf16[2048,128]{1,0:T(8,128)(2,1)S(1)}, u32[]{:S(2)}, u32[]{:S(2)}) collective-permute-start(bf16[2048,128]{1,0:T(8,128)(2,1)S(1)} %collective-permute-done.1.refs_4_), channel_id=1, source_target_pairs={{0,192},{64,0},{128,64},{192,128},{1,193},{65,1},{129,65},{193,129... | collective-permute-start | bytes 1572872 | tf_op jit(solution)/shard_map/ppermute | solution.py:39
  48.3 25.4 %collective-permute-start.8 = (bf16[2048,128]{1,0:T(8,128)(2,1)S(1)}, bf16[2048,128]{1,0:T(8,128)(2,1)S(1)}, u32[]{:S(2)}, u32[]{:S(2)}) collective-permute-start(bf16[2048,128]{1,0:T(8,128)(2,1)S(1)} %collective-permute-done.1.refs_4_), channel_id=1, source_target_pairs={{0,64},{64,128},{128,192},{192,0},{1,65},{65,129},{129,193},{193,1... | collective-permute-start | bytes 1572872 | tf_op jit(solution)/shard_map/ppermute | solution.py:39
  53.0 17.0 %collective-permute-start.7 = (bf16[512,256]{1,0:T(8,128)(2,1)S(1)}, bf16[512,256]{1,0:T(8,128)(2,1)S(1)}, u32[]{:S(2)}, u32[]{:S(2)}) collective-permute-start(bf16[512,256]{1,0:T(8,128)(2,1)S(1)} %get-tuple-element.22), channel_id=1, source_target_pairs={{0,240},{16,224},{32,208},{48,192},{64,176},{80,160},{96,144},{112... | collective-permute-start | bytes 786440 | tf_op jit(solution)/shard_map/ppermute | solution.py:39
  56.5 19.4 %collective-permute-start.12 = (bf16[2048,128]{1,0:T(8,128)(2,1)S(1)}, bf16[2048,128]{1,0:T(8,128)(2,1)S(1)}, u32[]{:S(2)}, u32[]{:S(2)}) collective-permute-start(bf16[2048,128]{1,0:T(8,128)(2,1)S(1)} %collective-permute-done.2.refs_8_), channel_id=1, source_target_pairs={{0,192},{64,0},{128,64},{192,128},{1,193},{65,1},{129,65},{193,129... | collective-permute-start | bytes 1572872 | tf_op jit(solution)/shard_map/ppermute | solution.py:39
  70.0 0.7 copy-start.6
  70.7 31.5 %collective-permute-start.26 = (bf16[256,2688]{1,0:T(8,128)(2,1)}, bf16[256,2688]{1,0:T(8,128)(2,1)}, u32[]{:S(2)}, u32[]{:S(2)}) collective-permute-start(bf16[256,2688]{1,0:T(8,128)(2,1)} %get-tuple-element.38.refs_0_), channel_id=1, source_target_pairs={{0,2},{2,4},{4,6},{6,0},{1,3},{3,5},{5,7},{7,1},{8,10},{10,12},{12... | collective-permute-start | bytes 4128776 | tf_op jit(solution)/shard_map/ppermute | solution.py:39
  72.2 0.8 copy-start
  73.0 14.3 %collective-permute-start.17 = (bf16[2048,128]{1,0:T(8,128)(2,1)}, bf16[2048,128]{1,0:T(8,128)(2,1)}, u32[]{:S(2)}, u32[]{:S(2)}) collective-permute-start(bf16[2048,128]{1,0:T(8,128)(2,1)} %constant_dynamic-update-slice_fusion.refs_12_), channel_id=1, source_target_pairs={{0,192},{64,0},{128,64},{192,128},{1,193},{65,1},{129,65},{193,129... | collective-permute-start | bytes 1572872 | tf_op jit(solution)/shard_map/ppermute | solution.py:39
  73.7 0.8 copy-start.2
  74.5 16.2 %collective-permute-start.16 = (bf16[2048,128]{1,0:T(8,128)(2,1)}, bf16[2048,128]{1,0:T(8,128)(2,1)}, u32[]{:S(2)}, u32[]{:S(2)}) collective-permute-start(bf16[2048,128]{1,0:T(8,128)(2,1)} %constant_dynamic-update-slice_fusion.refs_12_), channel_id=1, source_target_pairs={{0,64},{64,128},{128,192},{192,0},{1,65},{65,129},{129,193},{193,1... | collective-permute-start | bytes 1572872 | tf_op jit(solution)/shard_map/ppermute | solution.py:39
  75.9 0.8 copy-start.8
  76.7 21.8 %collective-permute-start.11 = (bf16[2048,128]{1,0:T(8,128)(2,1)S(1)}, bf16[2048,128]{1,0:T(8,128)(2,1)}, u32[]{:S(2)}, u32[]{:S(2)}) collective-permute-start(bf16[2048,128]{1,0:T(8,128)(2,1)S(1)} %collective-permute-done.2.refs_8_), channel_id=1, source_target_pairs={{0,64},{64,128},{128,192},{192,0},{1,65},{65,129},{129,193},{193,1... | collective-permute-start | bytes 1572872 | tf_op jit(solution)/shard_map/ppermute | solution.py:39
  87.3 16.6 %collective-permute-start.13 = (bf16[2048,128]{1,0:T(8,128)(2,1)S(1)}, bf16[2048,128]{1,0:T(8,128)(2,1)}, u32[]{:S(2)}, u32[]{:S(2)}) collective-permute-start(bf16[2048,128]{1,0:T(8,128)(2,1)S(1)} %pad_maximum_fusion.4.refs_3_), channel_id=1, source_target_pairs={{0,48},{16,0},{32,16},{48,32},{1,49},{17,1},{33,17},{49,33},{2,50}... | collective-permute-start | bytes 1572872 | tf_op jit(solution)/shard_map/ppermute | solution.py:39
  90.7 14.2 %collective-permute-start.10 = (bf16[2048,128]{1,0:T(8,128)(2,1)S(1)}, bf16[2048,128]{1,0:T(8,128)(2,1)}, u32[]{:S(2)}, u32[]{:S(2)}) collective-permute-start(bf16[2048,128]{1,0:T(8,128)(2,1)S(1)} %pad_maximum_fusion.4.refs_3_), channel_id=1, source_target_pairs={{0,16},{16,32},{32,48},{48,0},{1,17},{17,33},{33,49},{49,1},{2,18}... | collective-permute-start | bytes 1572872 | tf_op jit(solution)/shard_map/ppermute | solution.py:39
  90.8 10.2 %copy-start.7 = (bf16[512,256]{1,0:T(8,128)(2,1)S(1)}, bf16[512,256]{1,0:T(8,128)(2,1)}, u32[]{:S(2)}) copy-start(bf16[512,256]{1,0:T(8,128)(2,1)} %copy-done.6) | copy-start | bytes 786436
  91.9 15.7 %copy-start.1 = (bf16[2048,128]{1,0:T(8,128)(2,1)S(1)}, bf16[2048,128]{1,0:T(8,128)(2,1)}, u32[]{:S(2)}) copy-start(bf16[2048,128]{1,0:T(8,128)(2,1)} %copy-done) | copy-start | bytes 1572868
  91.9 15.7 %copy-start.3 = (bf16[2048,128]{1,0:T(8,128)(2,1)S(1)}, bf16[2048,128]{1,0:T(8,128)(2,1)}, u32[]{:S(2)}) copy-start(bf16[2048,128]{1,0:T(8,128)(2,1)} %copy-done.2) | copy-start | bytes 1572868
  91.9 15.7 %copy-start.4 = (s32[3]{0:T(128)S(1)}, s32[3]{0:T(128)}, u32[]{:S(2)}) copy-start(s32[3]{0:T(128)} %constant.107.clone.1.diag) | copy-start | bytes 40
  98.6 7.4 %collective-permute-start.19 = (bf16[1024,128]{1,0:T(8,128)(2,1)S(1)}, bf16[1024,128]{1,0:T(8,128)(2,1)S(1)}, u32[]{:S(2)}, u32[]{:S(2)}) collective-permute-start(bf16[1024,128]{1,0:T(8,128)(2,1)S(1)} %slice.87), channel_id=1, source_target_pairs={{0,192},{64,0},{128,64},{192,128},{1,193},{65,1},{129,65},{193,129... | collective-permute-start | bytes 786440 | tf_op jit(solution)/shard_map/ppermute | solution.py:39
  98.6 9.0 %collective-permute-start.18 = (bf16[1024,128]{1,0:T(8,128)(2,1)S(1)}, bf16[1024,128]{1,0:T(8,128)(2,1)S(1)}, u32[]{:S(2)}, u32[]{:S(2)}) collective-permute-start(bf16[1024,128]{1,0:T(8,128)(2,1)S(1)} %slice.86), channel_id=1, source_target_pairs={{0,64},{64,128},{128,192},{192,0},{1,65},{65,129},{129,193},{193,1... | collective-permute-start | bytes 786440 | tf_op jit(solution)/shard_map/ppermute | solution.py:39
  102.2 89.1 %collective-permute-start.28 = (bf16[256,2688]{1,0:T(8,128)(2,1)}, bf16[256,2688]{1,0:T(8,128)(2,1)}, u32[]{:S(2)}, u32[]{:S(2)}) collective-permute-start(bf16[256,2688]{1,0:T(8,128)(2,1)} %get-tuple-element.37.refs_1_), channel_id=1, source_target_pairs={{0,2},{2,4},{4,6},{6,0},{1,3},{3,5},{5,7},{7,1},{8,10},{10,12},{12... | collective-permute-start | bytes 4128776 | tf_op jit(solution)/shard_map/ppermute | solution.py:39
  103.9 87.4 %collective-permute-start.31 = (bf16[256,2688]{1,0:T(8,128)(2,1)}, bf16[256,2688]{1,0:T(8,128)(2,1)}, u32[]{:S(2)}, u32[]{:S(2)}) collective-permute-start(bf16[256,2688]{1,0:T(8,128)(2,1)} %get-tuple-element.38.refs_0_), channel_id=1, source_target_pairs={{0,6},{2,0},{4,2},{6,4},{1,7},{3,1},{5,3},{7,5},{8,14},{10,8},{12,... | collective-permute-start | bytes 4128776 | tf_op jit(solution)/shard_map/ppermute | solution.py:39
  104.9 86.4 %collective-permute-start.29 = (bf16[256,2688]{1,0:T(8,128)(2,1)}, bf16[256,2688]{1,0:T(8,128)(2,1)}, u32[]{:S(2)}, u32[]{:S(2)}) collective-permute-start(bf16[256,2688]{1,0:T(8,128)(2,1)} %collective-permute-done.26.refs_2_), channel_id=1, source_target_pairs={{0,2},{2,4},{4,6},{6,0},{1,3},{3,5},{5,7},{7,1},{8,10},{10,12},{12... | collective-permute-start | bytes 4128776 | tf_op jit(solution)/shard_map/ppermute | solution.py:39
  106.0 85.3 %collective-permute-start.30 = (bf16[256,2688]{1,0:T(8,128)(2,1)}, bf16[256,2688]{1,0:T(8,128)(2,1)}, u32[]{:S(2)}, u32[]{:S(2)}) collective-permute-start(bf16[256,2688]{1,0:T(8,128)(2,1)} %collective-permute-done.27.refs_7_), channel_id=1, source_target_pairs={{0,6},{2,0},{4,2},{6,4},{1,7},{3,1},{5,3},{7,5},{8,14},{10,8},{12,... | collective-permute-start | bytes 4128776 | tf_op jit(solution)/shard_map/ppermute | solution.py:39
  135.8 6.8 %collective-permute-start.20 = (f32[1,1024]{1,0:T(1,128)S(1)}, f32[1,1024]{1,0:T(1,128)S(1)}, u32[]{:S(2)}, u32[]{:S(2)}) collective-permute-start(f32[1,1024]{1,0:T(1,128)S(1)} %get-tuple-element.62), channel_id=1, source_target_pairs={{0,240},{16,224},{32,208},{48,192},{64,176},{80,160},{96,144},{112... | collective-permute-start | bytes 12296 | tf_op jit(solution)/shard_map/ppermute | solution.py:39
  142.6 9.4 %collective-permute-start.21 = (bf16[512,256]{1,0:T(8,128)(2,1)S(1)}, bf16[512,256]{1,0:T(8,128)(2,1)S(1)}, u32[]{:S(2)}, u32[]{:S(2)}) collective-permute-start(bf16[512,256]{1,0:T(8,128)(2,1)S(1)} %get-tuple-element.44), channel_id=1, source_target_pairs={{0,240},{16,224},{32,208},{48,192},{64,176},{80,160},{96,144},{112... | collective-permute-start | bytes 786440 | tf_op jit(solution)/shard_map/ppermute | solution.py:39
  154.4 5.7 %collective-permute-start.24 = (bf16[256,256]{1,0:T(8,128)(2,1)S(1)}, bf16[256,256]{1,0:T(8,128)(2,1)S(1)}, u32[]{:S(2)}, u32[]{:S(2)}) collective-permute-start(bf16[256,256]{1,0:T(8,128)(2,1)S(1)} %get-tuple-element.46), channel_id=1, source_target_pairs={{0,6},{2,0},{4,2},{6,4},{1,7},{3,1},{5,3},{7,5},{8,14},{10,8},{12,... | collective-permute-start | bytes 393224 | tf_op jit(solution)/shard_map/ppermute | solution.py:39
  160.1 6.7 %collective-permute-start.23 = (bf16[256,256]{1,0:T(8,128)(2,1)S(1)}, bf16[256,256]{1,0:T(8,128)(2,1)S(1)}, u32[]{:S(2)}, u32[]{:S(2)}) collective-permute-start(bf16[256,256]{1,0:T(8,128)(2,1)S(1)} %get-tuple-element.47), channel_id=1, source_target_pairs={{0,4},{2,6},{4,0},{6,2},{1,5},{3,7},{5,1},{7,3},{8,12},{10,14},{12... | collective-permute-start | bytes 393224 | tf_op jit(solution)/shard_map/ppermute | solution.py:39
  166.9 5.0 %collective-permute-start.22 = (bf16[256,256]{1,0:T(8,128)(2,1)S(1)}, bf16[256,256]{1,0:T(8,128)(2,1)S(1)}, u32[]{:S(2)}, u32[]{:S(2)}) collective-permute-start(bf16[256,256]{1,0:T(8,128)(2,1)S(1)} %get-tuple-element.48), channel_id=1, source_target_pairs={{0,2},{2,4},{4,6},{6,0},{1,3},{3,5},{5,7},{7,1},{8,10},{10,12},{12... | collective-permute-start | bytes 393224 | tf_op jit(solution)/shard_map/ppermute | solution.py:39
  172.0 18.1 %collective-permute-start.25 = (bf16[256,1024]{1,0:T(8,128)(2,1)S(1)}, bf16[256,1024]{1,0:T(8,128)(2,1)S(1)}, u32[]{:S(2)}, u32[]{:S(2)}) collective-permute-start(bf16[256,1024]{1,0:T(8,128)(2,1)S(1)} %pad_maximum_fusion.5), channel_id=1, source_target_pairs={{0,8},{8,0},{1,9},{9,1},{2,10},{10,2},{3,11},{11,3},{4,12},{12,4},... | collective-permute-start | bytes 1572872 | tf_op jit(solution)/shard_map/ppermute | solution.py:39
  199.7 13.7 %collective-permute-start.32 = (bf16[64,2688]{1,0:T(8,128)(2,1)}, bf16[64,2688]{1,0:T(8,128)(2,1)S(1)}, u32[]{:S(2)}, u32[]{:S(2)}) collective-permute-start(bf16[64,2688]{1,0:T(8,128)(2,1)} %get-tuple-element.34), channel_id=1, source_target_pairs={{0,1},{1,0},{2,3},{3,2},{4,5},{5,4},{6,7},{7,6},{8,9},{9,8},{10,11... | collective-permute-start | bytes 1032200 | tf_op jit(solution)/shard_map/ppermute | solution.py:39
  205.1 9.4 %collective-permute-start.33 = (bf16[64,2688]{1,0:T(8,128)(2,1)}, bf16[64,2688]{1,0:T(8,128)(2,1)S(1)}, u32[]{:S(2)}, u32[]{:S(2)}) collective-permute-start(bf16[64,2688]{1,0:T(8,128)(2,1)} %get-tuple-element.35), channel_id=1, source_target_pairs={{0,8},{8,0},{1,9},{9,1},{2,10},{10,2},{3,11},{11,3},{4,12},{12,4},... | collective-permute-start | bytes 1032200 | tf_op jit(solution)/shard_map/ppermute | solution.py:39
  205.8 15.3 %collective-permute-start.34 = (bf16[64,2688]{1,0:T(8,128)(2,1)}, bf16[64,2688]{1,0:T(8,128)(2,1)S(1)}, u32[]{:S(2)}, u32[]{:S(2)}) collective-permute-start(bf16[64,2688]{1,0:T(8,128)(2,1)} %get-tuple-element.36), channel_id=1, source_target_pairs={{0,9},{1,8},{8,1},{9,0},{2,11},{3,10},{10,3},{11,2},{4,13},{5,12},... | collective-permute-start | bytes 1032200 | tf_op jit(solution)/shard_map/ppermute | solution.py:39
